TPU v7x, 8 devices: a whole 2x2x1 slice. The times are simulated.
8 devices in a mesh: dp: 2 (over z, y), sp: 4 (over x, core).
Axes of the slice: x: 2, y: 2, z: 1, core: 2. Of those that a mesh axis runs over, the one named last changes fastest.
Arguments:
- u_in: bfloat16 [4, 1024, 4096], P('dp', 'sp'), parts along dimension 0
- w_in: bfloat16 [4096, 12288], replicated
- b_in: float32 [12288], replicated
- conv_taps: float32 [3, 12288], replicated
- w_out: bfloat16 [4096, 4096], replicated
- skip_one: float32 [4096], replicated
- skip_two: float32 [4096], replicated
- filt_one: float32 [1024, 4096], P('sp')
- filt_two: float32 [1024, 4096], P('sp')
Outputs:
- output: bfloat16 [4, 1024, 4096], P('dp', 'sp'), parts along dimension 0
There are 2 independent parts. A program takes and returns all parts, laid end to end along the dimension named above; an argument that names none is the same for every part.
All inputs are finite; a program needn't handle non-finite values.
Results may differ from a plain program's by a relative error of at most 0.014832.
Values sent between devices are 32-bit elements.
A program may use at most 1 GiB of HBM per device.

v0:
```python
import math
import jax
import jax.numpy as jnp
from jax import lax
from jax.sharding import PartitionSpec as P


def phase_table(row_idx, col_idx, fft_len, phase_sign):
    phase_angle = (phase_sign * 2.0 * math.pi / fft_len) * (row_idx[:, None] * col_idx[None, :]).astype(jnp.float32)
    return lax.complex(jnp.cos(phase_angle), jnp.sin(phase_angle))


def to_spectrum(signal, n_dev, dev_rank):
    groups, seq_len, channels = signal.shape
    piece_len = seq_len // n_dev
    fft_len = 2 * n_dev * seq_len
    by_block = lax.all_to_all(signal.reshape(groups, n_dev, piece_len, channels), 'sp', 1, 1, tiled=True)
    coarse = jnp.fft.fft(by_block, n=2 * n_dev, axis=1)
    pos_local = dev_rank * piece_len + jnp.arange(piece_len)
    coarse = coarse * phase_table(jnp.arange(2 * n_dev), pos_local, fft_len, -1.0)[None, :, :, None]
    pair_parts = lax.all_to_all(jnp.stack([coarse.real, coarse.imag]), 'sp', 2, 3, tiled=True)
    return jnp.fft.fft(lax.complex(pair_parts[0], pair_parts[1]), axis=2)


def from_spectrum(spectrum_in, n_dev, dev_rank):
    groups, seq_len, channels = spectrum_in.shape[0], spectrum_in.shape[2], spectrum_in.shape[3]
    fft_len = 2 * n_dev * seq_len
    fine_part = jnp.fft.ifft(spectrum_in, axis=2)
    own_freq = 2 * dev_rank + jnp.arange(2)
    fine_part = fine_part * phase_table(own_freq, jnp.arange(seq_len), fft_len, 1.0)[None, :, :, None]
    pair_parts = lax.all_to_all(jnp.stack([fine_part.real, fine_part.imag]), 'sp', 3, 2, tiled=True)
    coarse = jnp.fft.ifft(lax.complex(pair_parts[0], pair_parts[1]), axis=1)[:, :n_dev].real
    restored = lax.all_to_all(coarse, 'sp', 1, 1, tiled=True)
    return restored.reshape(groups, seq_len, channels)


def solution(mesh):
    n_dev = mesh.shape['sp']
    halo_perm = list(zip(range(n_dev - 1), range(1, n_dev)))

    def local_step(u_in, w_in, b_in, conv_taps, w_out, skip_one, skip_two, filt_one, filt_two):
        dev_rank = lax.axis_index('sp')
        model_width = u_in.shape[2]
        projected = (jnp.einsum('bsd,de->bse', u_in, w_in, preferred_element_type=jnp.float32) + b_in).astype(jnp.bfloat16).astype(jnp.float32)
        tail_rows = lax.ppermute(projected[:, -2:], 'sp', halo_perm)
        extended = jnp.concatenate([tail_rows, projected], axis=1)
        mixed = (conv_taps[0] * extended[:, 2:] + conv_taps[1] * extended[:, 1:-1] + conv_taps[2] * extended[:, :-2]).astype(jnp.bfloat16).astype(jnp.float32)
        gate_one = mixed[..., :model_width]
        gate_two = mixed[..., model_width:2 * model_width]
        values = mixed[..., 2 * model_width:]
        spec_one = to_spectrum(filt_one[None], n_dev, dev_rank)
        spec_two = to_spectrum(filt_two[None], n_dev, dev_rank)
        conv_one = from_spectrum(to_spectrum(values, n_dev, dev_rank) * spec_one, n_dev, dev_rank)
        z_one = gate_one * (conv_one + skip_one * values)
        conv_two = from_spectrum(to_spectrum(z_one, n_dev, dev_rank) * spec_two, n_dev, dev_rank)
        gated = gate_two * (conv_two + skip_two * z_one)
        out_sum = u_in.astype(jnp.float32) + jnp.einsum('bsd,de->bse', gated.astype(jnp.bfloat16), w_out, preferred_element_type=jnp.float32)
        return out_sum.astype(jnp.bfloat16)

    seq_spec = P('dp', 'sp', None)
    filt_spec = P('sp', None)
    return jax.shard_map(local_step, mesh=mesh, in_specs=(seq_spec, P(), P(), P(), P(), P(), P(), filt_spec, filt_spec), out_specs=seq_spec, check_vma=False)
```

profile of v0, /device:TPU:7, one launch (start us, length us, event | category | flops | bytes accessed | tf_op | source)
XLA Modules:
  0.0 3555.9 jit_solution(11777385125470627990)
XLA Ops:
  5.6 60.9 %fusion.20 = f32[2,256,12288]{2,1,0:T(8,128)} fusion(bf16[2,256,4096]{2,1,0:T(8,128)(2,1)} %param.13, bf16[4096,12288]{1,0:T(8,128)(2,1)} %param.14, f32[12288]{0:T(1024)} %param.15), kind=kOutput, calls=%fused_computation.26 | convolution fusion | flops 51558481920 | bytes 130072576 | tf_op jit(solution)/shard_map/bsd,de->bse/dot_general | solution.py:44
  75.1 34.2 fusion.71
  185.1 27.9 fusion.103
  291.4 38.4 %fusion.64 = (f32[1,2,8,64,4096]{4,2,3,1,0:T(8,128)}, f32[1,2,8,64,4096]{4,2,3,1,0:T(8,128)}) fusion(f32[8,64]{0,1:T(8,128)S(1)} %get-tuple-element.58, f32[8,64]{0,1:T(8,128)S(1)} %get-tuple-element.57, f32[2,64,4096,8]{2,3,1,0:T(8,128)} %fusion.16, f32[2,64,4096,8]{2,3,1,0:T(8,128)} %fusion.125, f32[2,64,4096,4]{2,3,1,0:T(4,128)} %bitcast.516), kind=kOutput, calls=%fused_computation.92 | convolution fusion | flops 436207936 | bytes 75501568 | tf_op jit(solution)/shard_map/jit(fft) | solution.py:18
  342.1 33.1 copy.102
  375.2 49.8 %all-to-all-done.3 = f32[2,1,8,64,4096]{4,3,1,0,2:T(8,128)} async-done(((f32[2,1,8,64,4096]{4,3,1,0,2:T(8,128)}), f32[2,1,8,64,4096]{4,3,1,0,2:T(8,128)}, u32[]{:S(2)}, u32[]{:S(2)}) %all-to-all-start.3) | async-done | bytes 16777248 | tf_op jit(solution)/shard_map/all_to_all | solution.py:21
  520.3 277.2 %all-to-all-done.1 = f32[2,2,8,64,4096]{4,3,1,0,2:T(8,128)} async-done(((f32[2,2,8,64,4096]{4,3,1,0,2:T(8,128)}), f32[2,2,8,64,4096]{4,3,1,0,2:T(8,128)}, u32[]{:S(2)}, u32[]{:S(2)}) %all-to-all-start.1) | async-done | bytes 33554464 | tf_op jit(solution)/shard_map/all_to_all | solution.py:21
  914.6 24.4 fusion.81
  962.9 30.0 fusion.69
  993.0 30.7 bitcast_subtract_fusion.3
  1023.7 42.0 %fusion.56 = (f32[1,2,2,256,4096]{3,4,2,1,0:T(8,128)}, f32[1,2,2,256,4096]{3,4,2,1,0:T(8,128)}) fusion(f32[2,256]{1,0:T(2,128)S(1)} %copy-done.12, f32[2,256]{1,0:T(2,128)S(1)} %copy-done.10, f32[2,2,4096,256]{3,2,1,0:T(8,128)} %bitcast_subtract_fusion.3, f32[2,2,4096,256]{3,2,1,0:T(8,128)} %fusion.69, f32[2,2,4096,256]{3,2,1,0:T(8,128)} %fusion.78, ...), kind=kOutput, calls=%fused_computation.79 | convolution fusion | flops 12943622144 | bytes 117706752 | tf_op jit(solution)/shard_map/jit(fft)/dot.31 | solution.py:28
  1088.1 49.5 %copy.119 = f32[2,2,2,256,4096]{4,2,1,0,3:T(2,128)} copy(f32[2,2,2,256,4096]{3,4,2,1,0:T(8,128)} %pad_maximum_fusion.1) | data formatting | bytes 67108864 | tf_op jit(solution)/shard_map/stack | solution.py:31
  1137.7 368.3 %all_to_all.114 = f32[2,2,2,256,4096]{4,2,1,0,3:T(2,128)S(1)} all-to-all(f32[2,2,2,256,4096]{4,2,1,0,3:T(2,128)} %copy.119), channel_id=1, replica_groups=mesh['dp'=2,'sp'=4] {'sp'}, dimensions={3} | all-to-all | bytes 67108864 | tf_op jit(solution)/shard_map/all_to_all | solution.py:31
  1506.0 33.4 copy.120
  1591.2 28.6 copy.122
  1685.3 29.4 fusion.47
  1722.9 95.9 %all_to_all.115 = f32[2,4,64,4096]{3,2,0,1:T(8,128)S(1)} all-to-all(f32[2,4,64,4096]{3,2,0,1:T(8,128)S(1)} %copy.123), channel_id=1, replica_groups=mesh['dp'=2,'sp'=4] {'sp'}, dimensions={1} | all-to-all | bytes 16777216 | tf_op jit(solution)/shard_map/all_to_all | solution.py:33
  1865.4 67.4 %all-to-all-done.6 = f32[2,4,64,4096]{3,2,0,1:T(8,128)} async-done(((f32[2,4,64,4096]{3,2,0,1:T(8,128)}), f32[2,4,64,4096]{3,2,0,1:T(8,128)}, u32[]{:S(2)}, u32[]{:S(2)}) %all-to-all-start.6) | async-done | bytes 8388640 | tf_op jit(solution)/shard_map/all_to_all | solution.py:17
  1973.1 38.2 %fusion.42 = (f32[1,2,8,64,4096]{4,2,3,1,0:T(8,128)}, f32[1,2,8,64,4096]{4,2,3,1,0:T(8,128)}) fusion(f32[8,64]{0,1:T(8,128)S(1)} %copy-done.7, f32[8,64]{0,1:T(8,128)S(1)} %copy-done.5, f32[2,64,4096,8]{2,3,1,0:T(8,128)} %fusion.12, f32[2,64,4096,8]{2,3,1,0:T(8,128)} %fusion.125, f32[2,64,4096,4]{2,3,1,0:T(4,128)} %bitcast.514), kind=kOutput, calls=%fused_computation.58 | convolution fusion | flops 436207936 | bytes 75501568 | tf_op jit(solution)/shard_map/jit(fft) | solution.py:18
  2023.6 33.1 copy.127
  2056.7 66.2 %all-to-all-done.9 = f32[2,1,8,64,4096]{4,3,1,0,2:T(8,128)} async-done(((f32[2,1,8,64,4096]{4,3,1,0,2:T(8,128)}), f32[2,1,8,64,4096]{4,3,1,0,2:T(8,128)}, u32[]{:S(2)}, u32[]{:S(2)}) %all-to-all-start.9) | async-done | bytes 16777248 | tf_op jit(solution)/shard_map/all_to_all | solution.py:21
  2217.8 277.6 %all-to-all-done.7 = f32[2,2,8,64,4096]{4,3,1,0,2:T(8,128)} async-done(((f32[2,2,8,64,4096]{4,3,1,0,2:T(8,128)}), f32[2,2,8,64,4096]{4,3,1,0,2:T(8,128)}, u32[]{:S(2)}, u32[]{:S(2)}) %all-to-all-start.7) | async-done | bytes 33554464 | tf_op jit(solution)/shard_map/all_to_all | solution.py:21
  2660.5 30.1 fusion.67
  2690.6 30.7 bitcast_subtract_fusion.1
  2721.3 42.2 %fusion.34 = (f32[1,2,2,256,4096]{3,4,2,1,0:T(8,128)}, f32[1,2,2,256,4096]{3,4,2,1,0:T(8,128)}) fusion(f32[2,256]{1,0:T(2,128)S(1)} %copy-done.13, f32[2,256]{1,0:T(2,128)S(1)} %copy-done.11, f32[2,2,4096,256]{3,2,1,0:T(8,128)} %bitcast_subtract_fusion.1, f32[2,2,4096,256]{3,2,1,0:T(8,128)} %fusion.67, f32[2,2,4096,256]{3,2,1,0:T(8,128)} %fusion.84, ...), kind=kOutput, calls=%fused_computation.45 | convolution fusion | flops 12943622144 | bytes 117706752 | tf_op jit(solution)/shard_map/jit(fft)/dot.31 | solution.py:28
  2785.9 49.5 %copy.144 = f32[2,2,2,256,4096]{4,2,1,0,3:T(2,128)} copy(f32[2,2,2,256,4096]{3,4,2,1,0:T(8,128)} %pad_maximum_fusion.3) | data formatting | bytes 67108864 | tf_op jit(solution)/shard_map/stack | solution.py:31
  2835.5 368.3 %all_to_all.116 = f32[2,2,2,256,4096]{4,2,1,0,3:T(2,128)S(1)} all-to-all(f32[2,2,2,256,4096]{4,2,1,0,3:T(2,128)} %copy.144), channel_id=1, replica_groups=mesh['dp'=2,'sp'=4] {'sp'}, dimensions={3} | all-to-all | bytes 67108864 | tf_op jit(solution)/shard_map/all_to_all | solution.py:31
  3203.8 33.4 copy.145
  3289.0 28.6 copy.147
  3382.9 29.4 fusion.25
  3420.6 97.1 %all_to_all.117 = f32[2,4,64,4096]{3,2,0,1:T(8,128)} all-to-all(f32[2,4,64,4096]{3,2,0,1:T(8,128)S(1)} %copy.148), channel_id=1, replica_groups=mesh['dp'=2,'sp'=4] {'sp'}, dimensions={1} | all-to-all | bytes 16777216 | tf_op jit(solution)/shard_map/all_to_all | solution.py:33
  3529.0 26.5 add_convert_fusion.1
  (150 shorter events, 1083.2 us)
Async XLA Ops:
  0.0 69.2 %all-to-all-start.2 = ((f32[1,4,64,4096]{3,2,0,1:T(8,128)}), f32[1,4,64,4096]{3,2,0,1:T(8,128)}, u32[]{:S(2)}, u32[]{:S(2)}) async-start(f32[1,4,64,4096]{3,2,0,1:T(8,128)} %bitcast.531), calls=%async_computation.2 | async-start | bytes 8388608 | tf_op jit(solution)/shard_map/all_to_all | solution.py:17
  5.6 63.4 %copy-start.14 = (f32[3,12288]{1,0:T(4,128)S(1)}, f32[3,12288]{1,0:T(4,128)}, u32[]{:S(2)}) copy-start(f32[3,12288]{1,0:T(4,128)} %param.16) | copy-start | bytes 442372
  67.7 7.4 collective-permute-start
  69.2 52.2 %all-to-all-start.8 = ((f32[1,4,64,4096]{3,2,0,1:T(8,128)}), f32[1,4,64,4096]{3,2,0,1:T(8,128)}, u32[]{:S(2)}, u32[]{:S(2)}) async-start(f32[1,4,64,4096]{3,2,0,1:T(8,128)} %bitcast.532), calls=%async_computation.8 | async-start | bytes 8388608 | tf_op jit(solution)/shard_map/all_to_all | solution.py:17
  121.3 115.5 %all-to-all-start = ((f32[2,4,64,4096]{3,2,0,1:T(8,128)}), f32[2,4,64,4096]{3,2,0,1:T(8,128)}, u32[]{:S(2)}, u32[]{:S(2)}) async-start(f32[2,4,64,4096]{3,2,0,1:T(8,128)} %copy.100), calls=%async_computation | async-start | bytes 16777216 | tf_op jit(solution)/shard_map/all_to_all | solution.py:17
  128.9 162.6 %copy-start.4 = (f32[8,64]{0,1:T(8,128)}, f32[8,64]{0,1:T(8,128)S(1)}, u32[]{:S(2)}) copy-start(f32[8,64]{0,1:T(8,128)S(1)} %get-tuple-element.57) | copy-start | bytes 6148
  128.9 162.6 %copy-start.6 = (f32[8,64]{0,1:T(8,128)}, f32[8,64]{0,1:T(8,128)S(1)}, u32[]{:S(2)}) copy-start(f32[8,64]{0,1:T(8,128)S(1)} %get-tuple-element.58) | copy-start | bytes 6148
  159.8 25.3 copy-start.2
  236.8 188.2 %all-to-all-start.3 = ((f32[2,1,8,64,4096]{4,3,1,0,2:T(8,128)}), f32[2,1,8,64,4096]{4,3,1,0,2:T(8,128)}, u32[]{:S(2)}, u32[]{:S(2)}) async-start(f32[2,1,8,64,4096]{4,3,1,0,2:T(8,128)} %copy.110), calls=%async_computation.3 | async-start | bytes 33554432 | tf_op jit(solution)/shard_map/all_to_all | solution.py:21
  425.0 372.5 %all-to-all-start.1 = ((f32[2,2,8,64,4096]{4,3,1,0,2:T(8,128)}), f32[2,2,8,64,4096]{4,3,1,0,2:T(8,128)}, u32[]{:S(2)}, u32[]{:S(2)}) async-start(f32[2,2,8,64,4096]{4,3,1,0,2:T(8,128)} %copy.102), calls=%async_computation.1 | async-start | bytes 67108864 | tf_op jit(solution)/shard_map/all_to_all | solution.py:21
  485.2 13.0 copy-start
  485.2 24.0 slice-start.1
  498.1 11.0 slice-start.2
  993.0 30.7 copy-start.8
  993.0 30.7 copy-start.10
  993.0 30.7 copy-start.12
  1714.6 3.4 slice-start.7
  1722.9 96.9 %copy-start.15 = (f32[4096]{0:T(1024)S(1)}, f32[4096]{0:T(1024)}, u32[]{:S(2)}) copy-start(f32[4096]{0:T(1024)} %param.18) | copy-start | bytes 49156
  1834.1 98.6 %all-to-all-start.6 = ((f32[2,4,64,4096]{3,2,0,1:T(8,128)}), f32[2,4,64,4096]{3,2,0,1:T(8,128)}, u32[]{:S(2)}, u32[]{:S(2)}) async-start(f32[2,4,64,4096]{3,2,0,1:T(8,128)} %copy.125), calls=%async_computation.6 | async-start | bytes 16777216 | tf_op jit(solution)/shard_map/all_to_all | solution.py:17
  1932.7 190.1 %all-to-all-start.9 = ((f32[2,1,8,64,4096]{4,3,1,0,2:T(8,128)}), f32[2,1,8,64,4096]{4,3,1,0,2:T(8,128)}, u32[]{:S(2)}, u32[]{:S(2)}) async-start(f32[2,1,8,64,4096]{4,3,1,0,2:T(8,128)} %copy.135), calls=%async_computation.9 | async-start | bytes 33554432 | tf_op jit(solution)/shard_map/all_to_all | solution.py:21
  1953.9 19.2 copy-start.5
  1953.9 19.2 copy-start.7
  2122.8 372.5 %all-to-all-start.7 = ((f32[2,2,8,64,4096]{4,3,1,0,2:T(8,128)}), f32[2,2,8,64,4096]{4,3,1,0,2:T(8,128)}, u32[]{:S(2)}, u32[]{:S(2)}) async-start(f32[2,2,8,64,4096]{4,3,1,0,2:T(8,128)} %copy.127), calls=%async_computation.7 | async-start | bytes 67108864 | tf_op jit(solution)/shard_map/all_to_all | solution.py:21
  2182.5 13.0 copy-start.1
  2182.5 23.9 slice-start.3
  2195.5 11.0 slice-start.4
  2690.6 30.7 copy-start.9
  2690.6 30.7 copy-start.11
  2690.6 30.7 copy-start.13
  3420.5 101.2 %slice-start.5 = ((s8[8388608]{0:T(1024)(128)(4,1)}), s8[4194304]{0:T(1024)(128)(4,1)S(1)}, s32[]{:S(2)}) async-start(s8[8388608]{0:T(1024)(128)(4,1)} %bitcast.511), calls=%async_computation.17 | async-start | bytes 8388608
  3420.6 101.2 %copy-start.16 = (f32[4096]{0:T(1024)S(1)}, f32[4096]{0:T(1024)}, u32[]{:S(2)}) copy-start(f32[4096]{0:T(1024)} %param.19) | copy-start | bytes 49156
  3517.7 4.6 slice-start.6
  (3 other events, 10.0 us)
where the time goes:
time: 3570 us; the launch traced here: 3560 us
  blocking collectives  930 us (26%)
  matrix products  861 us (24%)
  local copies, waits for them, and re-layouts  819 us (23%)
  waiting for transfers between devices  743 us (21%)
  other arithmetic  135 us (4%)
  starting transfers between devices  67.5 us (2%)
    all_to_all x2, blocking collectives, from_spectrum(): lax.all_to_all(jnp.stack([fine_part.real, fine_part.imag]), 'sp', 3, 2, t...  737 us
    all_to_all x4, waiting for transfers between devices, to_spectrum(): lax.all_to_all(jnp.stack([coarse.real, coarse.imag]), 'sp', 2, 3, tiled=T...  671 us
    another operation x12, matrix products, to_spectrum(): return jnp.fft.fft(lax.complex(pair_parts[0], pair_parts[1]), axis=2)  214 us
    another operation x6, matrix products, from_spectrum(): fine_part = jnp.fft.ifft(spectrum_in, axis=2)  206 us
    another operation x10, matrix products, to_spectrum(): coarse = jnp.fft.fft(by_block, n=2 * n_dev, axis=1)  205 us
    all_to_all x2, blocking collectives, from_spectrum(): restored = lax.all_to_all(coarse, 'sp', 1, 1, tiled=True)  193 us
    another operation x6, matrix products, from_spectrum(): jnp.fft.ifft(lax.complex(pair_parts[0], pair_parts[1]), axis=1)[:, :n_dev]  149 us
    slice x12, local copies, waits for them, and re-layouts, to_spectrum(): return jnp.fft.fft(lax.complex(pair_parts[0], pair_parts[1]), axis=2)  114 us
  transfers between devices with their start and end apart: 9, of which 6 were waited for; matrix products, arithmetic and copies ran while one was open for 18% of the time, Pallas kernels for 0%

commit v1 on v0

v1 whole, which is shorter than its diff:
```python
import functools

import jax
import jax.numpy as jnp
import numpy as np
from jax import lax
from jax.experimental import pallas as pl
from jax.experimental.pallas import tpu as pltpu
from jax.sharding import PartitionSpec as P

F32, BF16 = jnp.float32, jnp.bfloat16
BLK = 128
TN = 512
TC = 256
MESH = pl.DeviceIdType.MESH


def split_table(table):
    parts, rest = [], table.astype(np.float64)
    for _ in range(3):
        part = rest.astype(np.float32).astype(jnp.bfloat16)
        parts.append(part)
        rest = rest - part.astype(np.float64)
    return parts


def transform_tables():
    freq = np.concatenate([np.arange(0, BLK, 2), np.arange(1, BLK, 2)]) + 0.5
    angle = 2.0 * np.pi * freq[:, None] * np.arange(BLK)[None, :] / (2 * BLK)
    fwd = np.concatenate([np.cos(angle), -np.sin(angle)], 0)
    inv = np.concatenate([np.cos(angle).T, -np.sin(angle).T], 1) / BLK
    f1, f2, f3 = split_table(fwd)
    e1, e2, e3 = split_table(inv)
    fwd3 = np.concatenate([f1, f2, f3], 1)
    fwd6 = np.concatenate([f1, f1, f2, f2, f1, f3], 1)
    inv6 = np.concatenate([e1, e1, e2, e2, e1, e3], 1)
    return fwd3, fwd6, inv6


def dot(a, b):
    return jnp.dot(a, b, preferred_element_type=F32)


def split3(x):
    hi = x.astype(BF16)
    rest = x - hi.astype(F32)
    mid = rest.astype(BF16)
    low = (rest - mid.astype(F32)).astype(BF16)
    return hi, mid, low


def stack6(hi, mid, low):
    return jnp.concatenate([hi, mid, hi, mid, low, hi], axis=0)


def split_blocks(src, parts, first):
    for j in range(src.shape[0] // BLK):
        for i, a in enumerate(split3(src[j * BLK:(j + 1) * BLK])):
            parts[first + j, i] = a


def block_spectrum(fwd6_ref, parts, j):
    return dot(fwd6_ref[...], stack6(parts[j, 0], parts[j, 1], parts[j, 2]))


def shifted_add(cur, old, lo, sign):
    re, im = slice(lo, lo + BLK // 2), slice(BLK + lo, BLK + lo + BLK // 2)
    return re, im, cur[re] - sign * old[im], cur[im] + sign * old[re]


SIDES = ((0, 1.0), (BLK // 2, -1.0))


def short_conv(pbuf, t, first, rows):
    return (t[0:1] * pbuf[8 + first:8 + first + rows] + t[1:2] * pbuf[7 + first:7 + first + rows] + t[2:3] * pbuf[6 + first:6 + first + rows]).astype(BF16)


def block_values(fwd3_ref, blk):
    return dot(fwd3_ref[...], jnp.concatenate([blk, blk, blk], axis=0))


def main_body(fwd3_ref, fwd6_ref, inv6_ref, bias_ref, taps_ref, sk1_ref, sk2_ref, u_bf, u32, w_in, f1, f2,
              keep, part, qx, qv, vhat, far, u_sw, u_x, u_fw, tail, pf,
              land, ts, tr, os, orr, ws, wr, ss, sr, fs, fr, l_sem, x_send, x_recv, y_send, y_recv, p_send, p_recv):
    sp, dp = lax.axis_index("sp"), lax.axis_index("dp")
    c = lax.rem(sp, 2)
    on_b = sp >= 2
    on_a = jnp.logical_not(on_b)
    other = sp + 1 - 2 * c
    n_seq, n_pos, width = u_bf.shape
    half_w = width // 2
    nt, n_tile = half_w // TN, half_w // TC
    n_own, hp = 2 * n_pos, n_pos // 2
    nbo = n_own // BLK
    n_piece = 2 * n_seq

    def remote(src, dst, send, recv, peer):
        return pltpu.make_async_remote_copy(src, dst, send, recv, device_id=peer, device_id_type=MESH)

    def at(start, size):
        return pl.ds(pl.multiple_of(start, size), size)

    def piece(ref, s, h):
        return ref.at[s, h * hp:(h + 1) * hp]

    def tail_copy(k):
        return remote(u32.at[:, n_pos - 8:], tail, ts.at[k], tr.at[0], (dp, 2 + k))

    def over(s, h):
        return remote(piece(u32, s, h), piece(u_x, s, h), os.at[s, h], orr.at[s, h], (dp, lax.rem(sp + 2, 4)))

    def onward(s, h):
        return remote(piece(u_x, s, h), piece(u_fw, s, h), ws.at[s, h], wr.at[s, h], (dp, other))

    def swap_u(s):
        return remote(u32.at[s], u_sw.at[s], ss.at[s], sr.at[s], (dp, other))

    def swap_f(f):
        return remote((f1, f2)[f].at[:, at((1 - c) * half_w, half_w)], pf.at[f], fs.at[f], fr.at[f], (dp, other))

    def filt(src, u, k):
        return remote(src.at[:, at(k * half_w + u * TC, TC)], land.at[dp, u, c], x_send.at[u, k], x_recv.at[u, c], (dp, 2 + k))

    def landed(u, side):
        return remote(land.at[dp, u, side], land.at[dp, u, side], x_send.at[u, side], x_recv.at[u, side], (dp, sp))

    def across(u, side, f):
        return remote(land.at[f, u, side], land.at[f, u, side], y_send.at[u, side], y_recv.at[u, side], (1 - dp, sp))

    def fill(f, u, side, src, start):
        return pltpu.make_async_copy(src.at[:, at(start, TC)], land.at[f, u, side], l_sem.at[f, u, side])

    barrier = pltpu.get_barrier_semaphore()
    for peer in ((dp, other), (dp, lax.rem(sp + 2, 4)), (dp, lax.rem(other + 2, 4)), (1 - dp, sp)):
        pl.semaphore_signal(barrier, inc=1, device_id=peer, device_id_type=MESH)
    pl.semaphore_wait(barrier, 4)

    @pl.when(sp == 1)
    def _():
        for k in range(2):
            tail_copy(k).start()

    @pl.when(on_a)
    def _():
        for i in range(n_piece):
            over(*divmod(i, 2)).start()
        for which, src in ((0, f1), (1, f2)):
            @pl.when(dp == which)
            def _():
                for u in range(n_tile):
                    for k in range(2):
                        filt(src, u, k).start()

    for i in range(n_seq):
        swap_u(i).start()
    for f in range(2):
        swap_f(f).start()

    def front(wbuf, wsem, lhs, lhs_p, stage, st_sem, lhs_sem, tailbuf, q_st, q_sem, vh_st, vh_sem, pbuf, pstash):
        def column(g, j):
            return (g + j // nt) * width + c * half_w + lax.rem(j, nt) * TN

        def weights(g, j, slot):
            rows = width // 4
            return [pltpu.make_async_copy(w_in.at[i * rows:(i + 1) * rows, at(column(g, j), TN)],
                                          wbuf.at[slot, i * rows:(i + 1) * rows], wsem.at[slot, i]) for i in range(4)]

        def stream(g, body, following, n=nt):
            def step(j, carry):
                slot = lax.rem(j, 2)

                @pl.when(j + 1 < n)
                def _():
                    for copy in weights(g, j + 1, 1 - slot):
                        copy.start()

                @pl.when(j + 1 == n)
                def _():
                    following(1 - slot)

                for copy in weights(g, j, slot):
                    copy.wait()
                body(j, slot, bias_ref[:, at(column(g, j), TN)], taps_ref[:, at(column(g, j), TN)])
                return carry

            lax.fori_loop(0, n, step, 0)

        def begin(g):
            def start(slot):
                for copy in weights(g, 0, slot):
                    copy.start()
            return start

        def project(rows_ref, slot, bias):
            return (dot(rows_ref, wbuf[slot]) + bias).astype(BF16).astype(F32)

        def load_rows(n, src, dst_row):
            def copy(i):
                return pltpu.make_async_copy(src(i), stage.at[i % 2], st_sem.at[i % 2])

            copy(0).start()
            for i in range(n):
                if i + 1 < n:
                    copy(i + 1).start()
                copy(i).wait()
                ref, row = dst_row(i)
                ref[pl.ds(pl.multiple_of(row, 16), hp), :] = stage[i % 2].astype(BF16)

        tail_rows = n_seq * 8
        begin(0)(0)
        own_rows = [pltpu.make_async_copy(u_bf.at[s], lhs.at[pl.ds(pl.multiple_of(tail_rows + s * n_own + c * n_pos, 16), n_pos)], lhs_sem.at[s])
                    for s in range(n_seq)]
        for copy in own_rows:
            copy.start()
        for s in range(n_seq):
            swap_u(s).wait_recv()
        load_rows(n_piece, lambda i: piece(u_sw, *divmod(i, 2)), lambda i: (lhs, tail_rows + (i // 2) * n_own + (1 - c) * n_pos + (i % 2) * hp))
        for copy in own_rows:
            copy.wait()

        @pl.when(on_b)
        def _():
            tail_copy(0).wait_recv()
            copy = pltpu.make_async_copy(tail, tailbuf, lhs_sem.at[0])
            copy.start()
            copy.wait()

        @pl.when(on_a)
        def _():
            tailbuf[...] = jnp.zeros_like(tailbuf)

        lhs[:tail_rows, :] = tailbuf[...].reshape(tail_rows, width).astype(BF16)
        chunk = n_pos

        def own_phase(g, n, dst, spectrum, following):
            def flush(j, slot):
                cols = at(lax.rem(j, nt) * TN, TN)
                blocks = pl.ds(nbo * (1 + j // nt), nbo)
                copies = [pltpu.make_async_copy(q_st.at[slot], dst.at[:, blocks, :, cols], q_sem.at[slot])]
                if spectrum:
                    copies.append(pltpu.make_async_copy(vh_st.at[slot], vhat.at[:, nbo:, :, cols], vh_sem.at[slot]))
                return copies

            def body(j, slot, bias, taps):
                @pl.when(j >= 2)
                def _():
                    for copy in flush(j - 2, slot):
                        copy.wait()

                for i in range(n_seq * n_own // chunk):
                    s, r = divmod(i * chunk, n_own)
                    p = project(lhs[(tail_rows + i * chunk if i else 0):tail_rows + (i + 1) * chunk, :], slot, bias)
                    if i == 0:
                        for k in range(n_seq):
                            pbuf[k, 0:8] = jnp.where(on_b, p[8 * k:8 * k + 8], 0.0)
                        p = p[tail_rows:]
                    pbuf[s, 8 + r:8 + r + chunk] = p
                    q = short_conv(pbuf.at[s], taps, r, chunk)
                    for b in range(chunk // BLK):
                        blk = q[b * BLK:(b + 1) * BLK]
                        q_st[slot, s, r // BLK + b] = blk
                        if spectrum:
                            vh_st[slot, s, r // BLK + b] = block_values(fwd3_ref, blk)
                for copy in flush(j, slot):
                    copy.start()

            stream(g, body, following, n)
            for j in (n - 2, n - 1):
                for copy in flush(j, j % 2):
                    copy.wait()

        own_phase(0, 2 * nt, qx, False, begin(2))
        own_phase(2, nt, qv, True, begin(0))

        def far_phase(fin, fin_sem, fout, fout_sem, parts):
            hk = n_pos // BLK

            def fetch(j, slot):
                mine = at(c * half_w + j * TC, TC)
                srcs = (f1.at[:, mine], f2.at[:, mine], pf.at[0, :, at(j * TC, TC)], pf.at[1, :, at(j * TC, TC)])
                return [pltpu.make_async_copy(src, fin.at[slot, i], fin_sem.at[slot, i]) for i, src in enumerate(srcs)]

            def flush(j, slot):
                return pltpu.make_async_copy(fout.at[slot], far.at[:, :, :, at(j * TC, TC)], fout_sem.at[slot])

            for copy in fetch(0, 0):
                copy.start()

            def step(j, carry):
                slot = lax.rem(j, 2)

                @pl.when(j + 1 < n_tile)
                def _():
                    for copy in fetch(j + 1, 1 - slot):
                        copy.start()

                for copy in fetch(j, slot):
                    copy.wait()

                @pl.when(j >= 2)
                def _():
                    flush(j - 2, slot).wait()

                for f in range(2):
                    split_blocks(fin.at[slot, f], parts.at[f], c * hk)
                    split_blocks(fin.at[slot, 2 + f], parts.at[f], (1 - c) * hk)
                g_ref = fout.at[slot]
                for f in range(2):
                    for b in range(2 * hk):
                        g_ref[f, b] = block_spectrum(fwd6_ref, parts.at[f], b)
                    for b in range(2 * hk - 1, 0, -1):
                        for lo, sign in SIDES:
                            re, im, new_re, new_im = shifted_add(g_ref.at[f, b], g_ref.at[f, b - 1], lo, sign)
                            g_ref[f, b, re], g_ref[f, b, im] = new_re, new_im
                flush(j, slot).start()
                return carry

            lax.fori_loop(0, n_tile, step, 0)
            for j in (n_tile - 2, n_tile - 1):
                flush(j, j % 2).wait()

        for f in range(2):
            swap_f(f).wait_recv()
        pl.run_scoped(
            far_phase, pltpu.VMEM((2, 4, n_pos, TC), F32), pltpu.SemaphoreType.DMA((2, 4)),
            pltpu.VMEM((2, 2, nbo, 2 * BLK, TC), F32), pltpu.SemaphoreType.DMA((2,)), pltpu.VMEM((2, nbo, 3, BLK, TC), BF16))

        def prev_rows(s, h):
            @pl.when(on_b)
            def _():
                over(s, h).wait_recv()
                onward(s, h).start()
                load_rows(1, lambda _: piece(u_x, s, h), lambda _: (lhs_p, c * hp))
                onward(s, h).wait_recv()
                load_rows(1, lambda _: piece(u_fw, s, h), lambda _: (lhs_p, (1 - c) * hp))

            @pl.when(on_a)
            def _():
                lhs_p[...] = jnp.zeros_like(lhs_p)

        def prev_first(g, base, following):
            def body(j, slot, bias, taps):
                pstash[:, at(base + j * TN, TN)] = project(lhs_p[...], slot, bias).astype(BF16)

            stream(g, body, following)

        def prev_second(s, g, base, dst, spectrum, following):
            def flush(j, slot):
                cols = at(j * TN, TN)
                copies = [pltpu.make_async_copy(q_st.at[slot, 0], dst.at[s, :nbo, :, cols], q_sem.at[slot])]
                if spectrum:
                    copies.append(pltpu.make_async_copy(vh_st.at[slot, 0], vhat.at[s, :nbo, :, cols], vh_sem.at[slot]))
                return copies

            def body(j, slot, bias, taps):
                @pl.when(j >= 2)
                def _():
                    for copy in flush(j - 2, slot):
                        copy.wait()

                p = project(lhs_p[...], slot, bias)
                old = pstash[:, at(base + j * TN, TN)].astype(F32)
                pbuf[0, 0:8] = jnp.zeros((8, TN), F32)
                for core in range(2):
                    for h, rows in enumerate((old, p)):
                        first = 8 + (2 * core + h) * hp
                        pbuf[0, first:first + hp] = jnp.where(on_b, rows[core * hp:(core + 1) * hp], 0.0)
                for b in range(nbo):
                    blk = short_conv(pbuf.at[0], taps, b * BLK, BLK)
                    q_st[slot, 0, b] = blk
                    if spectrum:
                        vh_st[slot, 0, b] = block_values(fwd3_ref, blk)
                for copy in flush(j, slot):
                    copy.start()

            stream(g, body, following)
            for j in (nt - 2, nt - 1):
                for copy in flush(j, j % 2):
                    copy.wait()

        def prev_seq(s, carry):
            prev_rows(s, 0)
            prev_first(0, 0, begin(2))
            prev_first(2, half_w, begin(0))
            prev_rows(s, 1)
            prev_second(s, 0, 0, qx, False, begin(2))

            def again(slot):
                @pl.when(s + 1 < n_seq)
                def _():
                    begin(0)(slot)

            prev_second(s, 2, half_w, qv, True, again)
            return carry

        lax.fori_loop(0, n_seq, prev_seq, 0)

    pl.run_scoped(
        front,
        pltpu.VMEM((2, width, TN), BF16), pltpu.SemaphoreType.DMA((2, 4)),
        pltpu.VMEM((n_seq * n_own + 8 * n_seq, width), BF16), pltpu.VMEM((2 * hp, width), BF16),
        pltpu.VMEM((2, hp, width), F32), pltpu.SemaphoreType.DMA((2,)), pltpu.SemaphoreType.DMA((n_seq,)), pltpu.VMEM((n_seq, 8, width), F32),
        pltpu.VMEM((2, n_seq, nbo, BLK, TN), BF16), pltpu.SemaphoreType.DMA((2,)),
        pltpu.VMEM((2, n_seq, nbo, 2 * BLK, TN), F32), pltpu.SemaphoreType.DMA((2,)),
        pltpu.VMEM((n_seq, n_own + 8, TN), F32), pltpu.VMEM((2 * hp, 2 * half_w), BF16))

    @pl.when(on_a)
    def _():
        for u in range(n_tile):
            for f, own in enumerate((f1, f2)):
                fill(f, u, c, own, c * half_w + u * TC).start()
                fill(f, u, 1 - c, pf.at[f], u * TC).start()

    def forward(u):
        @pl.when(on_b)
        def _():
            for side in range(2):
                landed(u, side).wait_recv()
                across(u, side, dp).start()

    def conv(x1b, vb, x2b, vhb, farb, in_sem, kst, k_sem, sendbuf, *scratch):
        def fetch(t, slot):
            cols = at(t * TC, TC)
            srcs = (qx.at[:, :2 * nbo], qv, qx.at[:, 2 * nbo:], far)
            pairs = [(r.at[:, :, :, cols], b.at[slot]) for r, b in zip(srcs, (x1b, vb, x2b, farb))]
            pairs += [(vhat.at[s, :, :, cols], vhb.at[slot, s]) for s in range(n_seq)]
            return [pltpu.make_async_copy(src, dst, in_sem.at[slot, i]) for i, (src, dst) in enumerate(pairs)]

        def flush(t, slot):
            return pltpu.make_async_copy(kst.at[slot], keep.at[:, :, at(t * TC, TC)], k_sem.at[slot])

        def swap_y(u):
            return remote(sendbuf.at[lax.rem(u, 2)], part.at[:, :, at(u * TC, TC)], p_send.at[u], p_recv.at[u], (dp, other))

        for copy in fetch(0, 0):
            copy.start()
        forward(0)
        forward(1)

        def step(t, carry):
            slot = lax.rem(t, 2)

            @pl.when(t + 1 < n_tile)
            def _():
                for copy in fetch(t + 1, 1 - slot):
                    copy.start()

            @pl.when(on_a)
            def _():
                for f in range(2):
                    for side in range(2):
                        fill(f, t, side, f1, 0).wait()

            @pl.when(on_b)
            def _():
                for side in range(2):
                    across(t, side, 1 - dp).wait_recv()

            for copy in fetch(t, slot):
                copy.wait()

            @pl.when(t >= 2)
            def _():
                flush(t - 2, slot).wait()
                swap_y(t - 2).wait_send()

            cols = at(c * half_w + t * TC, TC)
            conv_tile(c, fwd6_ref, inv6_ref, x1b.at[slot], vb.at[slot], x2b.at[slot], vhb.at[slot], farb.at[slot],
                      sk1_ref[:, cols], sk2_ref[:, cols], land, t, kst.at[slot], sendbuf.at[slot], *scratch)
            flush(t, slot).start()

            @pl.when(t + 2 < n_tile)
            def _():
                forward(t + 2)

            swap_y(t).start()
            return carry

        lax.fori_loop(0, n_tile, step, 0)
        for u in (n_tile - 2, n_tile - 1):
            flush(u, u % 2).wait()
            swap_y(u).wait_send()
        for u in range(n_tile):
            swap_y(u).wait_recv()

    nb = 2 * nbo
    pl.run_scoped(
        conv,
        pltpu.VMEM((2, n_seq, nb, BLK, TC), BF16), pltpu.VMEM((2, n_seq, nb, BLK, TC), BF16), pltpu.VMEM((2, n_seq, nbo, BLK, TC), BF16),
        pltpu.VMEM((2, n_seq, nb, 2 * BLK, TC), F32), pltpu.VMEM((2, 2, nbo, 2 * BLK, TC), F32), pltpu.SemaphoreType.DMA((2, 4 + n_seq)),
        pltpu.VMEM((2, n_seq, n_pos, TC), BF16), pltpu.SemaphoreType.DMA((2,)), pltpu.VMEM((2, n_seq, n_pos, TC), F32),
        pltpu.VMEM((2, nbo, 3, BLK, TC), BF16),
        *[pltpu.VMEM((nbo + 1, 2 * BLK, TC), F32)] * 2,
        *[pltpu.VMEM((nb, 3, 2 * BLK, TC), BF16)] * n_seq,
        *[pltpu.VMEM((nb, 3, BLK, TC), BF16)] * n_seq,
        *[pltpu.VMEM((nb, BLK, TC), F32)] * n_seq,
        *[pltpu.VMEM((nb, 2 * BLK, TC), F32)] * n_seq,
        pltpu.VMEM((n_seq, nbo, BLK, TC), BF16))

    for s in range(n_seq):
        swap_u(s).wait_send()
    for f in range(2):
        swap_f(f).wait_send()

    @pl.when(sp == 1)
    def _():
        for k in range(2):
            tail_copy(k).wait_send()

    @pl.when(on_a)
    def _():
        for i in range(n_piece):
            over(*divmod(i, 2)).wait_send()
        for u in range(n_tile):
            for k in range(2):
                filt(f1, u, k).wait_send()

    @pl.when(on_b)
    def _():
        for i in range(n_piece):
            onward(*divmod(i, 2)).wait_send()
        for u in range(n_tile):
            for side in range(2):
                across(u, side, dp).wait_send()


def conv_tile(c, fwd6_ref, inv6_ref, x1_ref, v_ref, x2_ref, vhat, far_ref, sk1, sk2, land, t, keep_ref, send_ref,
              hparts, g1, g2, sp0, sp1, zp0, zp1, zv0, zv1, zh0, zh1, ybuf):
    n_seq, nb = vhat.shape[0], vhat.shape[1]
    nbo = nb // 2
    hk = nbo // 2
    g, sparts, zparts, zval, zhat = (g1, g2), (sp0, sp1), (zp0, zp1), (zv0, zv1), (zh0, zh1)

    for f in range(2):
        for side in range(2):
            split_blocks(land.at[f, t, side], hparts.at[f], side * hk)

    def near_spectrum(f, j):
        g[f][j] = block_spectrum(fwd6_ref, hparts.at[f], j)

    def window(f):
        for j in range(nbo, 0, -1):
            cur = far_ref.at[f, 0] if j == nbo else g[f].at[j]
            for lo, sign in SIDES:
                re, im, new_re, new_im = shifted_add(cur, g[f].at[j - 1], lo, sign)
                g[f][j, re], g[f][j, im] = new_re, new_im

    def pointwise(xhat, f, dst, r, first):
        re, im = pl.ds(pl.multiple_of(r * 16, 16), 16), pl.ds(pl.multiple_of(BLK + r * 16, 16), 16)
        for k in range(first, nb):
            acc_re = acc_im = None
            for j in range(k + 1):
                i = k - j
                gr, gi = (g[f][i, re], g[f][i, im]) if i <= nbo else (far_ref[f, i - nbo, re], far_ref[f, i - nbo, im])
                xr, xi = xhat[j, re], xhat[j, im]
                t_re, t_im = xr * gr - xi * gi, xr * gi + xi * gr
                acc_re = t_re if acc_re is None else acc_re + t_re
                acc_im = t_im if acc_im is None else acc_im + t_im
            for part, (a, b) in enumerate(zip(split3(acc_re), split3(acc_im))):
                dst[k, part, re], dst[k, part, im] = a, b

    def inverse(s, k):
        return dot(inv6_ref[...], stack6(sparts[s][k, 0], sparts[s][k, 1], sparts[s][k, 2]))

    def gate_one(s, k):
        z = x1_ref[s, k].astype(F32) * (inverse(s, k) + sk1 * v_ref[s, k].astype(F32))
        zval[s][k] = z
        for part, a in enumerate(split3(z)):
            zparts[s][k, part] = a

    def spectrum(s, k):
        zhat[s][k] = block_spectrum(fwd6_ref, zparts[s], k)

    def gate_two(s, k):
        y = x2_ref[s, k].astype(F32) * (inverse(s, nbo + k) + sk2 * zval[s][nbo + k])
        ybuf[s, k] = y.astype(BF16)

    def loop(body, trips=nb // 2):
        def run(i, carry):
            body(i)
            return carry
        lax.fori_loop(0, trips, run, 0)

    for j in range(nbo):
        near_spectrum(0, j)
    window(0)

    @loop
    def _(i):
        pointwise(vhat.at[0], 0, sparts[0], 2 * i, 0)
        near_spectrum(1, i)
        pointwise(vhat.at[0], 0, sparts[0], 2 * i + 1, 0)

    window(1)

    @loop
    def _(i):
        for r in range(2):
            pointwise(vhat.at[1], 0, sparts[1], 2 * i + r, 0)
            gate_one(0, 2 * i + r)

    @functools.partial(loop, trips=nb // 4)
    def _(i):
        for r in range(4):
            gate_one(1, 4 * i + r)
            spectrum(0, 4 * i + r)

    @loop
    def _(i):
        for r in range(2):
            pointwise(zhat[0], 1, sparts[0], 2 * i + r, nbo)
            spectrum(1, 2 * i + r)

    @functools.partial(loop, trips=nbo // 2)
    def _(i):
        for r in range(4):
            pointwise(zhat[1], 1, sparts[1], 4 * i + r, nbo)
            if r % 2:
                gate_two(0, 2 * i + r // 2)

    for k in range(nbo):
        gate_two(1, k)

    for s in range(n_seq):
        for b in range(hk):
            keep_ref[s, b * BLK:(b + 1) * BLK] = ybuf[s, c * hk + b]
            send_ref[s, b * BLK:(b + 1) * BLK] = ybuf[s, (1 - c) * hk + b].astype(F32)


def out_body(sc_ref, keep_ref, part_ref, wk_ref, wp_ref, u_ref, o_ref, lhs_k, lhs_p):
    @pl.when(pl.program_id(0) == 0)
    def _():
        rows = keep_ref.shape[0] * keep_ref.shape[1]
        lhs_k[...] = keep_ref[...].reshape(rows, -1)
        lhs_p[...] = part_ref[...].reshape(rows, -1).astype(BF16)

    acc = dot(lhs_k[...], wk_ref[...]) + dot(lhs_p[...], wp_ref[...])
    o_ref[...] = (u_ref[...].astype(F32) + acc.reshape(o_ref.shape)).astype(BF16)


def params(mib=60):
    return pltpu.CompilerParams(vmem_limit_bytes=mib << 20, dimension_semantics=("arbitrary",))


def solution(mesh):
    fwd3, fwd6, inv6 = transform_tables()

    def local_step(u_in, w_in, b_in, conv_taps, w_out, skip_one, skip_two, filt_one, filt_two):
        c = lax.axis_index("sp") % 2
        n_seq, n_pos, width = u_in.shape
        half_w = width // 2
        n_own = 2 * n_pos
        nb = 2 * n_own // BLK
        nbo = nb // 2
        n_tile, wt = half_w // TC, width // TN
        small, large = pl.BlockSpec(memory_space=pltpu.VMEM), pl.BlockSpec(memory_space=pl.ANY)
        dma = pltpu.SemaphoreType.DMA

        def shape(dims, dtype=F32):
            return jax.ShapeDtypeStruct(dims, dtype)

        keep, part, *_ = pl.pallas_call(
            main_body,
            in_specs=[small] * 7 + [large] * 5,
            out_specs=[large] * 11,
            out_shape=[
                shape((n_seq, n_pos, half_w), BF16), shape((n_seq, n_pos, half_w)),
                shape((n_seq, nb + nbo, BLK, half_w), BF16), shape((n_seq, nb, BLK, half_w), BF16),
                shape((n_seq, nb, 2 * BLK, half_w)), shape((2, nbo, 2 * BLK, half_w)),
                shape((n_seq, n_pos, width)), shape((n_seq, n_pos, width)), shape((n_seq, n_pos, width)),
                shape((n_seq, 8, width)), shape((2, n_pos, half_w)),
            ],
            scratch_shapes=[
                pltpu.VMEM((2, n_tile, 2, n_pos, TC), F32),
                dma((2,)), dma((1,)), *[dma((n_seq, 2))] * 4, *[dma((n_seq,))] * 2, *[dma((2,))] * 2,
                dma((2, n_tile, 2)), *[dma((n_tile, 2))] * 4, *[dma((n_tile,))] * 2,
            ],
            compiler_params=pltpu.CompilerParams(vmem_limit_bytes=62 << 20, collective_id=0, has_side_effects=True),
            name="hyena_main",
        )(fwd3, fwd6, inv6, b_in.reshape(1, -1), conv_taps, skip_one.reshape(1, -1), skip_two.reshape(1, -1),
          u_in, u_in.astype(F32), w_in, filt_one, filt_two)

        def fixed(dims):
            return pl.BlockSpec(dims, lambda *a: (0,) * len(dims))

        return pl.pallas_call(
            out_body,
            grid_spec=pltpu.PrefetchScalarGridSpec(
                num_scalar_prefetch=1,
                grid=(wt,),
                in_specs=[
                    fixed((n_seq, n_pos, half_w)),
                    fixed((n_seq, n_pos, half_w)),
                    pl.BlockSpec((half_w, TN), lambda j, sc: (sc[0], j)),
                    pl.BlockSpec((half_w, TN), lambda j, sc: (1 - sc[0], j)),
                    pl.BlockSpec((n_seq, n_pos, TN), lambda j, sc: (0, 0, j)),
                ],
                out_specs=pl.BlockSpec((n_seq, n_pos, TN), lambda j, sc: (0, 0, j)),
                scratch_shapes=[pltpu.VMEM((n_seq * n_pos, half_w), BF16)] * 2,
            ),
            out_shape=jax.ShapeDtypeStruct((n_seq, n_pos, width), BF16),
            compiler_params=params(),
            name="out_proj",
        )(c.astype(jnp.int32).reshape(1), keep, part, w_out, w_out, u_in)

    seq_spec = P("dp", "sp", None)
    filt_spec = P("sp", None)
    return jax.shard_map(local_step, mesh=mesh, in_specs=(seq_spec, P(), P(), P(), P(), P(), P(), filt_spec, filt_spec), out_specs=seq_spec, check_vma=False)
```

time: 3570 us -> 358 us (0.10)
  blocking collectives: 930 us -> 0 us
  matrix products: 861 us -> 0 us
  local copies, waits for them, and re-layouts: 819 us -> 0 us
  waiting for transfers between devices: 743 us -> 0 us
  Pallas kernels: 0 us -> 348 us
  other arithmetic: 135 us -> 6.49 us
  starting transfers between devices: 67.5 us -> 0 us
    all_to_all x4 -> x0, blocking collectives: 930 us -> none  [the longest x2 737 us: from_spectrum(): lax.all_to_all(jnp.stack([fine_part.real, fine_part.imag]), 'sp', 3, 2, t...]
    another operation x34 -> x0, matrix products: 774 us -> none  [the longest x12 214 us: to_spectrum(): return jnp.fft.fft(lax.complex(pair_parts[0], pair_parts[1]), axis=2)]
    all_to_all x8 -> x0, waiting for transfers between devices: 743 us -> none  [the longest x4 671 us: to_spectrum(): lax.all_to_all(jnp.stack([coarse.real, coarse.imag]), 'sp', 2, 3, tiled=T...]
    pallas_call x0 -> x2, Pallas kernels: none -> 348 us  [the longest x1 323 us: local_step(): pl.pallas_call(main_body, in_specs=[small] * 7 + [large] * 5, out_specs=[...]
    slice x28 -> x0, local copies, waits for them, and re-layouts: 255 us -> none  [the longest x12 114 us: to_spectrum(): return jnp.fft.fft(lax.complex(pair_parts[0], pair_parts[1]), axis=2)]
    another operation x6 -> x0, local copies, waits for them, and re-layouts: 200 us -> none  [the longest x4 100 us: to_spectrum(): jnp.stack([coarse.real, coarse.imag])]
    squeeze x12 -> x0, local copies, waits for them, and re-layouts: 188 us -> none  [the longest x8 106 us: to_spectrum(): return jnp.fft.fft(lax.complex(pair_parts[0], pair_parts[1]), axis=2)]
    all_to_all x12 -> x0, local copies, waits for them, and re-layouts: 165 us -> none  [the longest x2 66.8 us: from_spectrum(): lax.all_to_all(jnp.stack([fine_part.real, fine_part.imag]), 'sp', 3, 2, t...]
  transfers between devices with their start and end apart: 9 -> 0, of which waited for: 6 -> 0; matrix products, arithmetic and copies ran while one was open for 18% -> 0% of each run, Pallas kernels for 0% -> 0%
where the time goes in v1:
time: 358 us; the launch traced here: 355 us
  Pallas kernels  348 us (97%)
  other arithmetic  6.49 us (2%)
    pallas_call x1, Pallas kernels, local_step(): pl.pallas_call(main_body, in_specs=[small] * 7 + [large] * 5, out_specs=[...  323 us
    pallas_call x1, Pallas kernels, local_step(): pl.pallas_call(out_body, grid_spec=pltpu.PrefetchScalarGridSpec(num_scala...  25.4 us

profile of v1, /device:TPU:7, one launch (start us, length us, event | category | flops | bytes accessed | tf_op | source)
XLA Modules:
  0.0 355.0 jit_solution(3125536401190959466)
XLA Ops:
  0.0 6.5 %convert_element_type.3.u32 = f32[2,256,4096]{2,1,0:T(8,128)} convert(bf16[2,256,4096]{2,1,0:T(8,128)(2,1)} %u_ref.1) | non-fusion elementwise | flops 2097152 | bytes 12582912 | tf_op jit(solution)/shard_map/convert_element_type | solution.py:681
  6.5 323.1 %hyena_main.1 = (bf16[2,256,2048]{2,1,0:T(8,128)(2,1)}, f32[2,256,2048]{2,1,0:T(8,128)}, bf16[2,12,128,2048]{3,2,1,0:T(8,128)(2,1)}, bf16[2,8,128,2048]{3,2,1,0:...) custom-call(bf16[256,384]{1,0:T(8,128)(2,1)} %constant.23.clone.fwd3, ...), custom_call_target="tpu_custom_call" | custom-call | tf_op jit(solution)/shard_map/hyena_main/pallas_call | solution.py:662
  329.6 25.4 %out_proj.1 = bf16[2,256,4096]{2,1,0:T(8,128)(2,1)} custom-call(s32[1]{0:T(128)} %bitcast.sc_ref, bf16[2,256,2048]{2,1,0:T(8,128)(2,1)} %get-tuple-element.7.keep_ref, f32[2,256,2048]{2,1,0:T(8,128)} %get-tuple-element.8.part_ref, bf16[4096,4096]{1,0:T(8,128)(2,1)} %wp_ref.1, bf16[4096,4096]{1,0:T(8,128)(2,1)} %wp_ref.1, bf16[2,256,4096]{2,1,0:T(8,128)(2,1)} %u_ref.1), custom_call_target="tpu_custom_call" | custom-call | tf_op jit(solution)/shard_map/out_proj/pallas_call | solution.py:686

commit v2 on v1

--- a/solution.py
+++ b/solution.py
@@ -155,6 +155,13 @@
         swap_u(i).start()
     for f in range(2):
         swap_f(f).start()
+
+    def forward(u):
+        @pl.when(on_b)
+        def _():
+            for side in range(2):
+                landed(u, side).wait_recv()
+                across(u, side, dp).start()
 
     def front(wbuf, wsem, lhs, lhs_p, stage, st_sem, lhs_sem, tailbuf, q_st, q_sem, vh_st, vh_sem, pbuf, pstash):
         def column(g, j):
@@ -385,6 +392,10 @@
             prev_rows(s, 1)
             prev_second(s, 0, 0, qx, False, begin(2))
 
+            @pl.when(s + 1 == n_seq)
+            def _():
+                forward(0)
+
             def again(slot):
                 @pl.when(s + 1 < n_seq)
                 def _():
@@ -411,38 +422,48 @@
                 fill(f, u, c, own, c * half_w + u * TC).start()
                 fill(f, u, 1 - c, pf.at[f], u * TC).start()
 
-    def forward(u):
-        @pl.when(on_b)
-        def _():
-            for side in range(2):
-                landed(u, side).wait_recv()
-                across(u, side, dp).start()
-
-    def conv(x1b, vb, x2b, vhb, farb, in_sem, kst, k_sem, sendbuf, *scratch):
-        def fetch(t, slot):
-            cols = at(t * TC, TC)
+    def conv(x1b, vb, x2b, vhb, farb, in_sem, vh_sem, kst, k_sem, sendbuf, *scratch):
+        def fetch(t):
+            cols, slot = at(t * TC, TC), lax.rem(t, 3)
             srcs = (qx.at[:, :2 * nbo], qv, qx.at[:, 2 * nbo:], far)
-            pairs = [(r.at[:, :, :, cols], b.at[slot]) for r, b in zip(srcs, (x1b, vb, x2b, farb))]
-            pairs += [(vhat.at[s, :, :, cols], vhb.at[slot, s]) for s in range(n_seq)]
-            return [pltpu.make_async_copy(src, dst, in_sem.at[slot, i]) for i, (src, dst) in enumerate(pairs)]
-
-        def flush(t, slot):
+            copies = [pltpu.make_async_copy(r.at[:, :, :, cols], b.at[slot], in_sem.at[slot, i])
+                      for i, (r, b) in enumerate(zip(srcs, (x1b, vb, x2b, farb)))]
+            two = lax.rem(t, 2)
+            return copies + [pltpu.make_async_copy(vhat.at[s, :, :, cols], vhb.at[two, s], vh_sem.at[two, s]) for s in range(n_seq)]
+
+        def flush(t):
+            slot = lax.rem(t, 2)
             return pltpu.make_async_copy(kst.at[slot], keep.at[:, :, at(t * TC, TC)], k_sem.at[slot])
 
         def swap_y(u):
             return remote(sendbuf.at[lax.rem(u, 2)], part.at[:, :, at(u * TC, TC)], p_send.at[u], p_recv.at[u], (dp, other))
 
-        for copy in fetch(0, 0):
+        tile = ConvTile(fwd6_ref, inv6_ref, *scratch)
+
+        def inputs(t, back):
+            slot, cols = lax.rem(t + 3 - back, 3), at(c * half_w + lax.rem(t + n_tile - back, n_tile) * TC, TC)
+            return x1b.at[slot], vb.at[slot], x2b.at[slot], farb.at[slot], sk1_ref[:, cols], sk2_ref[:, cols]
+
+        def emit(t):
+            slot = lax.rem(t, 2)
+
+            @pl.when(t >= 2)
+            def _():
+                flush(t - 2).wait()
+                swap_y(t - 2).wait_send()
+
+            tile.result(c, kst.at[slot], sendbuf.at[slot])
+            flush(t).start()
+            swap_y(t).start()
+
+        for copy in fetch(0):
             copy.start()
-        forward(0)
         forward(1)
 
         def step(t, carry):
-            slot = lax.rem(t, 2)
-
             @pl.when(t + 1 < n_tile)
             def _():
-                for copy in fetch(t + 1, 1 - slot):
+                for copy in fetch(t + 1):
                     copy.start()
 
             @pl.when(on_a)
@@ -456,29 +477,25 @@
                 for side in range(2):
                     across(t, side, 1 - dp).wait_recv()
 
-            for copy in fetch(t, slot):
+            for copy in fetch(t):
                 copy.wait()
 
-            @pl.when(t >= 2)
-            def _():
-                flush(t - 2, slot).wait()
-                swap_y(t - 2).wait_send()
-
-            cols = at(c * half_w + t * TC, TC)
-            conv_tile(c, fwd6_ref, inv6_ref, x1b.at[slot], vb.at[slot], x2b.at[slot], vhb.at[slot], farb.at[slot],
-                      sk1_ref[:, cols], sk2_ref[:, cols], land, t, kst.at[slot], sendbuf.at[slot], *scratch)
-            flush(t, slot).start()
+            tile.step(land, t, vhb.at[lax.rem(t, 2)], inputs(t, 0), inputs(t, 1))
 
             @pl.when(t + 2 < n_tile)
             def _():
                 forward(t + 2)
 
-            swap_y(t).start()
+            @pl.when(t >= 1)
+            def _():
+                emit(t - 1)
             return carry
 
         lax.fori_loop(0, n_tile, step, 0)
+        tile.drain(inputs(n_tile, 1))
+        emit(n_tile - 1)
         for u in (n_tile - 2, n_tile - 1):
-            flush(u, u % 2).wait()
+            flush(u).wait()
             swap_y(u).wait_send()
         for u in range(n_tile):
             swap_y(u).wait_recv()
@@ -486,15 +503,17 @@
     nb = 2 * nbo
     pl.run_scoped(
         conv,
-        pltpu.VMEM((2, n_seq, nb, BLK, TC), BF16), pltpu.VMEM((2, n_seq, nb, BLK, TC), BF16), pltpu.VMEM((2, n_seq, nbo, BLK, TC), BF16),
-        pltpu.VMEM((2, n_seq, nb, 2 * BLK, TC), F32), pltpu.VMEM((2, 2, nbo, 2 * BLK, TC), F32), pltpu.SemaphoreType.DMA((2, 4 + n_seq)),
+        pltpu.VMEM((3, n_seq, nb, BLK, TC), BF16), pltpu.VMEM((3, n_seq, nb, BLK, TC), BF16), pltpu.VMEM((3, n_seq, nbo, BLK, TC), BF16),
+        pltpu.VMEM((2, n_seq, nb, 2 * BLK, TC), F32), pltpu.VMEM((3, 2, nbo, 2 * BLK, TC), F32),
+        pltpu.SemaphoreType.DMA((3, 4)), pltpu.SemaphoreType.DMA((2, n_seq)),
         pltpu.VMEM((2, n_seq, n_pos, TC), BF16), pltpu.SemaphoreType.DMA((2,)), pltpu.VMEM((2, n_seq, n_pos, TC), F32),
         pltpu.VMEM((2, nbo, 3, BLK, TC), BF16),
-        *[pltpu.VMEM((nbo + 1, 2 * BLK, TC), F32)] * 2,
+        pltpu.VMEM((nbo + 1, 2 * BLK, TC), F32), pltpu.VMEM((nbo + 1, 2 * BLK, TC), F32), pltpu.VMEM((nbo, 2 * BLK, TC), F32),
         *[pltpu.VMEM((nb, 3, 2 * BLK, TC), BF16)] * n_seq,
-        *[pltpu.VMEM((nb, 3, BLK, TC), BF16)] * n_seq,
+        pltpu.VMEM((nb, 3, BLK, TC), BF16),
         *[pltpu.VMEM((nb, BLK, TC), F32)] * n_seq,
-        *[pltpu.VMEM((nb, 2 * BLK, TC), F32)] * n_seq,
+        pltpu.VMEM((nb, 2 * BLK, TC), F32),
+        *[pltpu.VMEM((nbo, 3, 2 * BLK, TC), BF16)] * n_seq,
         pltpu.VMEM((n_seq, nbo, BLK, TC), BF16))
 
     for s in range(n_seq):
@@ -524,107 +543,136 @@
                 across(u, side, dp).wait_send()
 
 
-def conv_tile(c, fwd6_ref, inv6_ref, x1_ref, v_ref, x2_ref, vhat, far_ref, sk1, sk2, land, t, keep_ref, send_ref,
-              hparts, g1, g2, sp0, sp1, zp0, zp1, zv0, zv1, zh0, zh1, ybuf):
-    n_seq, nb = vhat.shape[0], vhat.shape[1]
-    nbo = nb // 2
-    hk = nbo // 2
-    g, sparts, zparts, zval, zhat = (g1, g2), (sp0, sp1), (zp0, zp1), (zv0, zv1), (zh0, zh1)
-
-    for f in range(2):
+def loop(trips):
+    def run(body):
+        def step(i, carry):
+            body(i)
+            return carry
+        lax.fori_loop(0, trips, step, 0)
+    return run
+
+
+class ConvTile:
+    def __init__(self, fwd6, inv6, hparts, g1, g2, raw2, sp0, sp1, zparts, zv0, zv1, zhat, sq0, sq1, ybuf):
+        self.fwd6, self.inv6, self.hparts, self.g, self.raw2 = fwd6, inv6, hparts, (g1, g2), raw2
+        self.first, self.second, self.zparts, self.zval, self.zhat, self.ybuf = (sp0, sp1), (sq0, sq1), zparts, (zv0, zv1), zhat, ybuf
+        self.nb, self.nbo = sp0.shape[0], sq0.shape[0]
+
+    def near(self, land, t, f):
         for side in range(2):
-            split_blocks(land.at[f, t, side], hparts.at[f], side * hk)
-
-    def near_spectrum(f, j):
-        g[f][j] = block_spectrum(fwd6_ref, hparts.at[f], j)
-
-    def window(f):
+            split_blocks(land.at[f, t, side], self.hparts.at[f], side * self.nbo // 2)
+
+    def window(self, f, raw, far):
+        g, nbo = self.g[f], self.nbo
         for j in range(nbo, 0, -1):
-            cur = far_ref.at[f, 0] if j == nbo else g[f].at[j]
+            cur = far.at[f, 0] if j == nbo else raw.at[j]
             for lo, sign in SIDES:
-                re, im, new_re, new_im = shifted_add(cur, g[f].at[j - 1], lo, sign)
-                g[f][j, re], g[f][j, im] = new_re, new_im
-
-    def pointwise(xhat, f, dst, r, first):
+                re, im, new_re, new_im = shifted_add(cur, raw.at[j - 1], lo, sign)
+                g[j, re], g[j, im] = new_re, new_im
+        if raw is not g:
+            g[0] = raw[0]
+
+    def pointwise(self, xhat, f, far, dst, r, first):
+        g, nbo = self.g[f], self.nbo
         re, im = pl.ds(pl.multiple_of(r * 16, 16), 16), pl.ds(pl.multiple_of(BLK + r * 16, 16), 16)
-        for k in range(first, nb):
+        for k in range(first, self.nb):
             acc_re = acc_im = None
             for j in range(k + 1):
                 i = k - j
-                gr, gi = (g[f][i, re], g[f][i, im]) if i <= nbo else (far_ref[f, i - nbo, re], far_ref[f, i - nbo, im])
+                gr, gi = (g[i, re], g[i, im]) if i <= nbo else (far[f, i - nbo, re], far[f, i - nbo, im])
                 xr, xi = xhat[j, re], xhat[j, im]
                 t_re, t_im = xr * gr - xi * gi, xr * gi + xi * gr
                 acc_re = t_re if acc_re is None else acc_re + t_re
                 acc_im = t_im if acc_im is None else acc_im + t_im
             for part, (a, b) in enumerate(zip(split3(acc_re), split3(acc_im))):
-                dst[k, part, re], dst[k, part, im] = a, b
-
-    def inverse(s, k):
-        return dot(inv6_ref[...], stack6(sparts[s][k, 0], sparts[s][k, 1], sparts[s][k, 2]))
-
-    def gate_one(s, k):
-        z = x1_ref[s, k].astype(F32) * (inverse(s, k) + sk1 * v_ref[s, k].astype(F32))
-        zval[s][k] = z
+                dst[k - first, part, re], dst[k - first, part, im] = a, b
+
+    def inverse(self, parts, k):
+        return dot(self.inv6[...], stack6(parts[k, 0], parts[k, 1], parts[k, 2]))
+
+    def gate_one(self, s, k, data):
+        x1, v, _, _, skip, _ = data
+        z = x1[s, k].astype(F32) * (self.inverse(self.first[s], k) + skip * v[s, k].astype(F32))
+        self.zval[s][k] = z
         for part, a in enumerate(split3(z)):
-            zparts[s][k, part] = a
-
-    def spectrum(s, k):
-        zhat[s][k] = block_spectrum(fwd6_ref, zparts[s], k)
-
-    def gate_two(s, k):
-        y = x2_ref[s, k].astype(F32) * (inverse(s, nbo + k) + sk2 * zval[s][nbo + k])
-        ybuf[s, k] = y.astype(BF16)
-
-    def loop(body, trips=nb // 2):
-        def run(i, carry):
-            body(i)
-            return carry
-        lax.fori_loop(0, trips, run, 0)
-
-    for j in range(nbo):
-        near_spectrum(0, j)
-    window(0)
-
-    @loop
-    def _(i):
-        pointwise(vhat.at[0], 0, sparts[0], 2 * i, 0)
-        near_spectrum(1, i)
-        pointwise(vhat.at[0], 0, sparts[0], 2 * i + 1, 0)
-
-    window(1)
-
-    @loop
-    def _(i):
-        for r in range(2):
-            pointwise(vhat.at[1], 0, sparts[1], 2 * i + r, 0)
-            gate_one(0, 2 * i + r)
-
-    @functools.partial(loop, trips=nb // 4)
-    def _(i):
-        for r in range(4):
-            gate_one(1, 4 * i + r)
-            spectrum(0, 4 * i + r)
-
-    @loop
-    def _(i):
-        for r in range(2):
-            pointwise(zhat[0], 1, sparts[0], 2 * i + r, nbo)
-            spectrum(1, 2 * i + r)
-
-    @functools.partial(loop, trips=nbo // 2)
-    def _(i):
-        for r in range(4):
-            pointwise(zhat[1], 1, sparts[1], 4 * i + r, nbo)
-            if r % 2:
-                gate_two(0, 2 * i + r // 2)
-
-    for k in range(nbo):
-        gate_two(1, k)
-
-    for s in range(n_seq):
-        for b in range(hk):
-            keep_ref[s, b * BLK:(b + 1) * BLK] = ybuf[s, c * hk + b]
-            send_ref[s, b * BLK:(b + 1) * BLK] = ybuf[s, (1 - c) * hk + b].astype(F32)
+            self.zparts[k, part] = a
+
+    def spectrum(self, k):
+        self.zhat[k] = block_spectrum(self.fwd6, self.zparts, k)
+
+    def gate_two(self, s, k, data):
+        y = data[2][s, k].astype(F32) * (self.inverse(self.second[s], k) + data[5] * self.zval[s][self.nbo + k])
+        self.ybuf[s, k] = y.astype(BF16)
+
+    def middle(self, s, data, i, point=None):
+        for q in range(4):
+            if point is not None:
+                point(4 * i + q)
+            for k in range(2):
+                if q < 2:
+                    self.gate_one(s, 4 * i + 2 * q + k, data)
+                else:
+                    self.spectrum(4 * i + 2 * (q - 2) + k)
+
+    def step(self, land, t, vhat, data, old):
+        nb, nbo = self.nb, self.nbo
+        far = data[3]
+        self.near(land, t, 0)
+        for j in range(nbo):
+            self.g[0][j] = block_spectrum(self.fwd6, self.hparts.at[0], j)
+        self.near(land, t, 1)
+        self.window(0, self.g[0], far)
+
+        @loop(nb // 4)
+        def _(i):
+            self.middle(1, old, i, lambda r: self.pointwise(vhat.at[0], 0, far, self.first[0], r, 0))
+
+        @loop(nbo // 2)
+        def _(i):
+            for q in range(4):
+                self.pointwise(self.zhat, 1, old[3], self.second[1], 4 * i + q, nbo)
+                if q < 2:
+                    self.gate_two(0, 2 * i + q, old)
+                else:
+                    j = 2 * i + q - 2
+                    self.raw2[j] = block_spectrum(self.fwd6, self.hparts.at[1], j)
+
+        self.window(1, self.raw2, far)
+
+        @loop(nb // 4)
+        def _(i):
+            self.middle(0, data, i, lambda r: self.pointwise(vhat.at[1], 0, far, self.first[1], r, 0))
+
+        @loop(nbo // 2)
+        def _(i):
+            for q in range(4):
+                self.pointwise(self.zhat, 1, far, self.second[0], 4 * i + q, nbo)
+                if q % 2 == 0:
+                    self.gate_two(1, 2 * i + q // 2, old)
+
+    def drain(self, data):
+        nb, nbo = self.nb, self.nbo
+
+        @loop(nb // 4)
+        def _(i):
+            self.middle(1, data, i)
+
+        @loop(nbo // 2)
+        def _(i):
+            for q in range(4):
+                self.pointwise(self.zhat, 1, data[3], self.second[1], 4 * i + q, nbo)
+                if q % 2 == 0:
+                    self.gate_two(0, 2 * i + q // 2, data)
+
+        for k in range(nbo):
+            self.gate_two(1, k, data)
+
+    def result(self, c, keep, send):
+        hk = self.nbo // 2
+        for s in range(self.ybuf.shape[0]):
+            for b in range(hk):
+                keep[s, b * BLK:(b + 1) * BLK] = self.ybuf[s, c * hk + b]
+                send[s, b * BLK:(b + 1) * BLK] = self.ybuf[s, (1 - c) * hk + b].astype(F32)
 
 
 def out_body(sc_ref, keep_ref, part_ref, wk_ref, wp_ref, u_ref, o_ref, lhs_k, lhs_p):

time: 358 us -> 350 us (0.978)
  Pallas kernels: 348 us -> 341 us
    pallas_call x1, Pallas kernels: 323 us -> 316 us  [local_step(): pl.pallas_call(main_body, in_specs=[small] * 7 + [large] * 5, out_specs=[...]
where the time goes in v2:
time: 350 us; the launch traced here: 348 us
  Pallas kernels  341 us (97%)
  other arithmetic  6.49 us (2%)
    pallas_call x1, Pallas kernels, local_step(): pl.pallas_call(main_body, in_specs=[small] * 7 + [large] * 5, out_specs=[...  316 us
    pallas_call x1, Pallas kernels, local_step(): pl.pallas_call(out_body, grid_spec=pltpu.PrefetchScalarGridSpec(num_scala...  25.4 us

profile of v2, /device:TPU:7, one launch (start us, length us, event | category | flops | bytes accessed | tf_op | source)
XLA Modules:
  0.0 347.8 jit_solution(17802017590688194794)
XLA Ops:
  0.0 6.5 %convert_element_type.3.u32 = f32[2,256,4096]{2,1,0:T(8,128)} convert(bf16[2,256,4096]{2,1,0:T(8,128)(2,1)} %u_ref.1) | non-fusion elementwise | flops 2097152 | bytes 12582912 | tf_op jit(solution)/shard_map/convert_element_type | solution.py:729
  6.5 315.9 %hyena_main.1 = (bf16[2,256,2048]{2,1,0:T(8,128)(2,1)}, f32[2,256,2048]{2,1,0:T(8,128)}, bf16[2,12,128,2048]{3,2,1,0:T(8,128)(2,1)}, bf16[2,8,128,2048]{3,2,1,0:...) custom-call(bf16[256,384]{1,0:T(8,128)(2,1)} %constant.23.clone.fwd3, ...), custom_call_target="tpu_custom_call" | custom-call | tf_op jit(solution)/shard_map/hyena_main/pallas_call | solution.py:710
  322.4 25.4 %out_proj.1 = bf16[2,256,4096]{2,1,0:T(8,128)(2,1)} custom-call(s32[1]{0:T(128)} %bitcast.sc_ref, bf16[2,256,2048]{2,1,0:T(8,128)(2,1)} %get-tuple-element.7.keep_ref, f32[2,256,2048]{2,1,0:T(8,128)} %get-tuple-element.8.part_ref, bf16[4096,4096]{1,0:T(8,128)(2,1)} %wp_ref.1, bf16[4096,4096]{1,0:T(8,128)(2,1)} %wp_ref.1, bf16[2,256,4096]{2,1,0:T(8,128)(2,1)} %u_ref.1), custom_call_target="tpu_custom_call" | custom-call | tf_op jit(solution)/shard_map/out_proj/pallas_call | solution.py:734

commit v3 on v2

--- a/solution.py
+++ b/solution.py
@@ -130,6 +130,21 @@
     def fill(f, u, side, src, start):
         return pltpu.make_async_copy(src.at[:, at(start, TC)], land.at[f, u, side], l_sem.at[f, u, side])
 
+    def column(g, j):
+        return (g + j // nt) * width + c * half_w + lax.rem(j, nt) * TN
+
+    def load_rows(stage, st_sem, n, src, dst_row):
+        def copy(i):
+            return pltpu.make_async_copy(src(i), stage.at[i % 2], st_sem.at[i % 2])
+
+        copy(0).start()
+        for i in range(n):
+            if i + 1 < n:
+                copy(i + 1).start()
+            copy(i).wait()
+            ref, row = dst_row(i)
+            ref[pl.ds(pl.multiple_of(row, 16), hp), :] = stage[i % 2].astype(BF16)
+
     barrier = pltpu.get_barrier_semaphore()
     for peer in ((dp, other), (dp, lax.rem(sp + 2, 4)), (dp, lax.rem(other + 2, 4)), (1 - dp, sp)):
         pl.semaphore_signal(barrier, inc=1, device_id=peer, device_id_type=MESH)
@@ -163,10 +178,7 @@
                 landed(u, side).wait_recv()
                 across(u, side, dp).start()
 
-    def front(wbuf, wsem, lhs, lhs_p, stage, st_sem, lhs_sem, tailbuf, q_st, q_sem, vh_st, vh_sem, pbuf, pstash):
-        def column(g, j):
-            return (g + j // nt) * width + c * half_w + lax.rem(j, nt) * TN
-
+    def front(wbuf, wsem, lhs, stage, st_sem, lhs_sem, tailbuf, q_st, q_sem, vh_st, vh_sem, pbuf):
         def weights(g, j, slot):
             rows = width // 4
             return [pltpu.make_async_copy(w_in.at[i * rows:(i + 1) * rows, at(column(g, j), TN)],
@@ -181,9 +193,10 @@
                     for copy in weights(g, j + 1, 1 - slot):
                         copy.start()
 
-                @pl.when(j + 1 == n)
-                def _():
-                    following(1 - slot)
+                if following is not None:
+                    @pl.when(j + 1 == n)
+                    def _():
+                        following(1 - slot)
 
                 for copy in weights(g, j, slot):
                     copy.wait()
@@ -200,18 +213,6 @@
 
         def project(rows_ref, slot, bias):
             return (dot(rows_ref, wbuf[slot]) + bias).astype(BF16).astype(F32)
-
-        def load_rows(n, src, dst_row):
-            def copy(i):
-                return pltpu.make_async_copy(src(i), stage.at[i % 2], st_sem.at[i % 2])
-
-            copy(0).start()
-            for i in range(n):
-                if i + 1 < n:
-                    copy(i + 1).start()
-                copy(i).wait()
-                ref, row = dst_row(i)
-                ref[pl.ds(pl.multiple_of(row, 16), hp), :] = stage[i % 2].astype(BF16)
 
         tail_rows = n_seq * 8
         begin(0)(0)
@@ -221,7 +222,7 @@
             copy.start()
         for s in range(n_seq):
             swap_u(s).wait_recv()
-        load_rows(n_piece, lambda i: piece(u_sw, *divmod(i, 2)), lambda i: (lhs, tail_rows + (i // 2) * n_own + (1 - c) * n_pos + (i % 2) * hp))
+        load_rows(stage, st_sem, n_piece, lambda i: piece(u_sw, *divmod(i, 2)), lambda i: (lhs, tail_rows + (i // 2) * n_own + (1 - c) * n_pos + (i % 2) * hp))
         for copy in own_rows:
             copy.wait()
 
@@ -277,7 +278,7 @@
                     copy.wait()
 
         own_phase(0, 2 * nt, qx, False, begin(2))
-        own_phase(2, nt, qv, True, begin(0))
+        own_phase(2, nt, qv, True, None)
 
         def far_phase(fin, fin_sem, fout, fout_sem, parts):
             hk = n_pos // BLK
@@ -332,88 +333,117 @@
             far_phase, pltpu.VMEM((2, 4, n_pos, TC), F32), pltpu.SemaphoreType.DMA((2, 4)),
             pltpu.VMEM((2, 2, nbo, 2 * BLK, TC), F32), pltpu.SemaphoreType.DMA((2,)), pltpu.VMEM((2, nbo, 3, BLK, TC), BF16))
 
-        def prev_rows(s, h):
-            @pl.when(on_b)
-            def _():
-                over(s, h).wait_recv()
-                onward(s, h).start()
-                load_rows(1, lambda _: piece(u_x, s, h), lambda _: (lhs_p, c * hp))
-                onward(s, h).wait_recv()
-                load_rows(1, lambda _: piece(u_fw, s, h), lambda _: (lhs_p, (1 - c) * hp))
-
-            @pl.when(on_a)
-            def _():
-                lhs_p[...] = jnp.zeros_like(lhs_p)
-
-        def prev_first(g, base, following):
-            def body(j, slot, bias, taps):
-                pstash[:, at(base + j * TN, TN)] = project(lhs_p[...], slot, bias).astype(BF16)
-
-            stream(g, body, following)
-
-        def prev_second(s, g, base, dst, spectrum, following):
-            def flush(j, slot):
-                cols = at(j * TN, TN)
-                copies = [pltpu.make_async_copy(q_st.at[slot, 0], dst.at[s, :nbo, :, cols], q_sem.at[slot])]
-                if spectrum:
-                    copies.append(pltpu.make_async_copy(vh_st.at[slot, 0], vhat.at[s, :nbo, :, cols], vh_sem.at[slot]))
-                return copies
-
-            def body(j, slot, bias, taps):
-                @pl.when(j >= 2)
-                def _():
-                    for copy in flush(j - 2, slot):
-                        copy.wait()
-
-                p = project(lhs_p[...], slot, bias)
-                old = pstash[:, at(base + j * TN, TN)].astype(F32)
-                pbuf[0, 0:8] = jnp.zeros((8, TN), F32)
-                for core in range(2):
-                    for h, rows in enumerate((old, p)):
-                        first = 8 + (2 * core + h) * hp
-                        pbuf[0, first:first + hp] = jnp.where(on_b, rows[core * hp:(core + 1) * hp], 0.0)
-                for b in range(nbo):
-                    blk = short_conv(pbuf.at[0], taps, b * BLK, BLK)
-                    q_st[slot, 0, b] = blk
-                    if spectrum:
-                        vh_st[slot, 0, b] = block_values(fwd3_ref, blk)
-                for copy in flush(j, slot):
-                    copy.start()
-
-            stream(g, body, following)
-            for j in (nt - 2, nt - 1):
-                for copy in flush(j, j % 2):
-                    copy.wait()
-
-        def prev_seq(s, carry):
-            prev_rows(s, 0)
-            prev_first(0, 0, begin(2))
-            prev_first(2, half_w, begin(0))
-            prev_rows(s, 1)
-            prev_second(s, 0, 0, qx, False, begin(2))
-
-            @pl.when(s + 1 == n_seq)
-            def _():
-                forward(0)
-
-            def again(slot):
-                @pl.when(s + 1 < n_seq)
-                def _():
-                    begin(0)(slot)
-
-            prev_second(s, 2, half_w, qv, True, again)
-            return carry
-
-        lax.fori_loop(0, n_seq, prev_seq, 0)
-
     pl.run_scoped(
         front,
         pltpu.VMEM((2, width, TN), BF16), pltpu.SemaphoreType.DMA((2, 4)),
-        pltpu.VMEM((n_seq * n_own + 8 * n_seq, width), BF16), pltpu.VMEM((2 * hp, width), BF16),
+        pltpu.VMEM((n_seq * n_own + 8 * n_seq, width), BF16),
         pltpu.VMEM((2, hp, width), F32), pltpu.SemaphoreType.DMA((2,)), pltpu.SemaphoreType.DMA((n_seq,)), pltpu.VMEM((n_seq, 8, width), F32),
         pltpu.VMEM((2, n_seq, nbo, BLK, TN), BF16), pltpu.SemaphoreType.DMA((2,)),
         pltpu.VMEM((2, n_seq, nbo, 2 * BLK, TN), F32), pltpu.SemaphoreType.DMA((2,)),
-        pltpu.VMEM((n_seq, n_own + 8, TN), F32), pltpu.VMEM((2 * hp, 2 * half_w), BF16))
+        pltpu.VMEM((n_seq, n_own + 8, TN), F32))
+
+    def prev(wres, w_sem, lhs_p, stage, st_sem, q_st, q_sem, vh_st, vh_sem, pbuf, pstash):
+        groups = ((0, 0, qx, False), (nt, 2, qv, True))
+
+        def weights(base, g, j):
+            rows = width // 4
+            return [pltpu.make_async_copy(w_in.at[i * rows:(i + 1) * rows, at(column(g, j), TN)],
+                                          wres.at[base + j, i * rows:(i + 1) * rows], w_sem.at[base + j, i]) for i in range(4)]
+
+        for base, g, _, _ in groups:
+            for j in range(nt):
+                for copy in weights(base, g, j):
+                    copy.start()
+
+        def rows(s, h):
+            @pl.when(on_b)
+            def _():
+                over(s, h).wait_recv()
+                onward(s, h).start()
+                load_rows(stage, st_sem, 1, lambda _: piece(u_x, s, h), lambda _: (lhs_p, c * hp))
+                onward(s, h).wait_recv()
+                load_rows(stage, st_sem, 1, lambda _: piece(u_fw, s, h), lambda _: (lhs_p, (1 - c) * hp))
+
+            @pl.when(on_a)
+            def _():
+                lhs_p[...] = jnp.zeros_like(lhs_p)
+
+        def project(base, g, j):
+            return (dot(lhs_p[...], wres[base + j]) + bias_ref[:, at(column(g, j), TN)]).astype(BF16)
+
+        def first(s, base, g):
+            def body(j, carry):
+                @pl.when(s == 0)
+                def _():
+                    for copy in weights(base, g, j):
+                        copy.wait()
+
+                pstash[:, at((base + j) * TN, TN)] = project(base, g, j)
+                return carry
+
+            lax.fori_loop(0, nt, body, 0)
+
+        def second(s, base, g, dst, spectrum):
+            def flush(j):
+                slot, cols = lax.rem(j, 2), at(j * TN, TN)
+                copies = [pltpu.make_async_copy(q_st.at[slot], dst.at[s, :nbo, :, cols], q_sem.at[slot])]
+                if spectrum:
+                    copies.append(pltpu.make_async_copy(vh_st.at[slot], vhat.at[s, :nbo, :, cols], vh_sem.at[slot]))
+                return copies
+
+            def body(j, carry):
+                slot = lax.rem(j, 2)
+
+                @pl.when(j >= 2)
+                def _():
+                    for copy in flush(j - 2):
+                        copy.wait()
+
+                taps = taps_ref[:, at(column(g, j), TN)]
+                old = pstash[:, at((base + j) * TN, TN)].astype(F32)
+                pbuf[0:8] = jnp.zeros((8, TN), F32)
+                p = project(base, g, j).astype(F32)
+                for core in range(2):
+                    for h, part_rows in enumerate((old, p)):
+                        start = 8 + (2 * core + h) * hp
+                        pbuf[start:start + hp] = jnp.where(on_b, part_rows[core * hp:(core + 1) * hp], 0.0)
+                for b in range(nbo):
+                    blk = short_conv(pbuf, taps, b * BLK, BLK)
+                    q_st[slot, b] = blk
+                    if spectrum:
+                        vh_st[slot, b] = block_values(fwd3_ref, blk)
+                for copy in flush(j):
+                    copy.start()
+                return carry
+
+            lax.fori_loop(0, nt, body, 0)
+            for j in (nt - 2, nt - 1):
+                for copy in flush(j):
+                    copy.wait()
+
+        def one_seq(s, carry):
+            rows(s, 0)
+            for base, g, _, _ in groups:
+                first(s, base, g)
+            rows(s, 1)
+            second(s, *groups[0])
+
+            @pl.when(s + 1 == n_seq)
+            def _():
+                forward(0)
+
+            second(s, *groups[1])
+            return carry
+
+        lax.fori_loop(0, n_seq, one_seq, 0)
+
+    pl.run_scoped(
+        prev,
+        pltpu.VMEM((2 * nt, width, TN), BF16), pltpu.SemaphoreType.DMA((2 * nt, 4)),
+        pltpu.VMEM((2 * hp, width), BF16), pltpu.VMEM((2, hp, width), F32), pltpu.SemaphoreType.DMA((2,)),
+        pltpu.VMEM((2, nbo, BLK, TN), BF16), pltpu.SemaphoreType.DMA((2,)),
+        pltpu.VMEM((2, nbo, 2 * BLK, TN), F32), pltpu.SemaphoreType.DMA((2,)),
+        pltpu.VMEM((n_own + 8, TN), F32), pltpu.VMEM((2 * hp, 2 * half_w), BF16))
 
     @pl.when(on_a)
     def _():
@@ -675,32 +705,73 @@
                 send[s, b * BLK:(b + 1) * BLK] = self.ybuf[s, (1 - c) * hk + b].astype(F32)
 
 
-def out_body(sc_ref, keep_ref, part_ref, wk_ref, wp_ref, u_ref, o_ref, lhs_k, lhs_p):
-    @pl.when(pl.program_id(0) == 0)
-    def _():
-        rows = keep_ref.shape[0] * keep_ref.shape[1]
-        lhs_k[...] = keep_ref[...].reshape(rows, -1)
-        lhs_p[...] = part_ref[...].reshape(rows, -1).astype(BF16)
-
-    acc = dot(lhs_k[...], wk_ref[...]) + dot(lhs_p[...], wp_ref[...])
-    o_ref[...] = (u_ref[...].astype(F32) + acc.reshape(o_ref.shape)).astype(BF16)
-
-
-def params(mib=60):
-    return pltpu.CompilerParams(vmem_limit_bytes=mib << 20, dimension_semantics=("arbitrary",))
+def out_body(keep, part, w_out, u_in, out, wbuf, w_sem, lhs, keep_v, stage, in_sem, u_v, o_st, o_sem):
+    c = lax.rem(lax.axis_index("sp"), 2)
+    n_seq, n_pos, half_w = keep.shape
+    width = 2 * half_w
+    n_col, rows = width // TN, width // 4
+
+    def weights(j, slot):
+        return [pltpu.make_async_copy(w_out.at[i * rows:(i + 1) * rows, pl.ds(pl.multiple_of(j * TN, TN), TN)],
+                                      wbuf.at[slot, i * rows:(i + 1) * rows], w_sem.at[slot, i]) for i in range(4)]
+
+    def flush(j):
+        slot = lax.rem(j, 2)
+        return pltpu.make_async_copy(o_st.at[slot], out.at[:, :, pl.ds(pl.multiple_of(j * TN, TN), TN)], o_sem.at[slot])
+
+    loads = [pltpu.make_async_copy(part.at[s], stage.at[s], in_sem.at[s]) for s in range(n_seq)]
+    loads += [pltpu.make_async_copy(keep.at[s], keep_v.at[s], in_sem.at[n_seq + s]) for s in range(n_seq)]
+    for copy in loads:
+        copy.start()
+    for copy in weights(0, 0):
+        copy.start()
+    resid = pltpu.make_async_copy(u_in, u_v, in_sem.at[2 * n_seq])
+    resid.start()
+    mine, theirs = (pl.ds(pl.multiple_of(k * half_w, half_w), half_w) for k in (c, 1 - c))
+    for s in range(n_seq):
+        loads[s].wait()
+        lhs[s, :, theirs] = stage[s].astype(BF16)
+    for s in range(n_seq):
+        loads[n_seq + s].wait()
+        lhs[s, :, mine] = keep_v[s]
+    resid.wait()
+
+    def step(j, carry):
+        slot = lax.rem(j, 2)
+
+        @pl.when(j + 1 < n_col)
+        def _():
+            for copy in weights(j + 1, 1 - slot):
+                copy.start()
+
+        for copy in weights(j, slot):
+            copy.wait()
+
+        @pl.when(j >= 2)
+        def _():
+            flush(j - 2).wait()
+
+        cols = pl.ds(pl.multiple_of(j * TN, TN), TN)
+        for s in range(n_seq):
+            o_st[slot, s] = (u_v[s, :, cols].astype(F32) + dot(lhs[s], wbuf[slot])).astype(BF16)
+        flush(j).start()
+        return carry
+
+    lax.fori_loop(0, n_col, step, 0)
+    for j in (n_col - 2, n_col - 1):
+        flush(j).wait()
 
 
 def solution(mesh):
     fwd3, fwd6, inv6 = transform_tables()
 
     def local_step(u_in, w_in, b_in, conv_taps, w_out, skip_one, skip_two, filt_one, filt_two):
-        c = lax.axis_index("sp") % 2
         n_seq, n_pos, width = u_in.shape
         half_w = width // 2
         n_own = 2 * n_pos
         nb = 2 * n_own // BLK
         nbo = nb // 2
-        n_tile, wt = half_w // TC, width // TN
+        n_tile = half_w // TC
         small, large = pl.BlockSpec(memory_space=pltpu.VMEM), pl.BlockSpec(memory_space=pl.ANY)
         dma = pltpu.SemaphoreType.DMA
 
@@ -728,28 +799,19 @@
         )(fwd3, fwd6, inv6, b_in.reshape(1, -1), conv_taps, skip_one.reshape(1, -1), skip_two.reshape(1, -1),
           u_in, u_in.astype(F32), w_in, filt_one, filt_two)
 
-        def fixed(dims):
-            return pl.BlockSpec(dims, lambda *a: (0,) * len(dims))
-
         return pl.pallas_call(
             out_body,
-            grid_spec=pltpu.PrefetchScalarGridSpec(
-                num_scalar_prefetch=1,
-                grid=(wt,),
-                in_specs=[
-                    fixed((n_seq, n_pos, half_w)),
-                    fixed((n_seq, n_pos, half_w)),
-                    pl.BlockSpec((half_w, TN), lambda j, sc: (sc[0], j)),
-                    pl.BlockSpec((half_w, TN), lambda j, sc: (1 - sc[0], j)),
-                    pl.BlockSpec((n_seq, n_pos, TN), lambda j, sc: (0, 0, j)),
-                ],
-                out_specs=pl.BlockSpec((n_seq, n_pos, TN), lambda j, sc: (0, 0, j)),
-                scratch_shapes=[pltpu.VMEM((n_seq * n_pos, half_w), BF16)] * 2,
-            ),
-            out_shape=jax.ShapeDtypeStruct((n_seq, n_pos, width), BF16),
-            compiler_params=params(),
+            in_specs=[large] * 4,
+            out_specs=large,
+            out_shape=shape((n_seq, n_pos, width), BF16),
+            scratch_shapes=[
+                pltpu.VMEM((2, width, TN), BF16), dma((2, 4)),
+                pltpu.VMEM((n_seq, n_pos, width), BF16), pltpu.VMEM((n_seq, n_pos, half_w), BF16), pltpu.VMEM((n_seq, n_pos, half_w), F32),
+                dma((2 * n_seq + 1,)), pltpu.VMEM((n_seq, n_pos, width), BF16), pltpu.VMEM((2, n_seq, n_pos, TN), BF16), dma((2,)),
+            ],
+            compiler_params=pltpu.CompilerParams(vmem_limit_bytes=60 << 20),
             name="out_proj",
-        )(c.astype(jnp.int32).reshape(1), keep, part, w_out, w_out, u_in)
+        )(keep, part, w_out, u_in)
 
     seq_spec = P("dp", "sp", None)
     filt_spec = P("sp", None)

time: 350 us -> 347 us (level)
  no operation moved by 1% of the time
where the time goes in v3:
time: 347 us; the launch traced here: 345 us
  Pallas kernels  338 us (97%)
  other arithmetic  6.49 us (2%)
    pallas_call x1, Pallas kernels, local_step(): pl.pallas_call(main_body, in_specs=[small] * 7 + [large] * 5, out_specs=[...  313 us
    pallas_call x1, Pallas kernels, local_step(): pl.pallas_call(out_body, in_specs=[large] * 4, out_specs=large, out_shape...  25.1 us

profile of v3, /device:TPU:7, one launch (start us, length us, event | category | flops | bytes accessed | tf_op | source)
XLA Modules:
  0.0 344.9 jit_solution(7415430429234508259)
XLA Ops:
  0.0 6.5 %convert_element_type.3.u32 = f32[2,256,4096]{2,1,0:T(8,128)} convert(bf16[2,256,4096]{2,1,0:T(8,128)(2,1)} %u_in.1) | non-fusion elementwise | flops 2097152 | bytes 12582912 | tf_op jit(solution)/shard_map/convert_element_type | solution.py:800
  6.5 313.1 %hyena_main.1 = (bf16[2,256,2048]{2,1,0:T(8,128)(2,1)}, f32[2,256,2048]{2,1,0:T(8,128)}, bf16[2,12,128,2048]{3,2,1,0:T(8,128)(2,1)}, bf16[2,8,128,2048]{3,2,1,0:...) custom-call(bf16[256,384]{1,0:T(8,128)(2,1)} %constant.6.clone.fwd3_, ...), custom_call_target="tpu_custom_call" | custom-call | tf_op jit(solution)/shard_map/hyena_main/pallas_call | solution.py:781
  319.6 25.1 %out_proj.1 = bf16[2,256,4096]{2,1,0:T(8,128)(2,1)} custom-call(bf16[2,256,2048]{2,1,0:T(8,128)(2,1)} %get-tuple-element.7.keep, f32[2,256,2048]{2,1,0:T(8,128)} %get-tuple-element.8.part, bf16[4096,4096]{1,0:T(8,128)(2,1)} %w_out.1, bf16[2,256,4096]{2,1,0:T(8,128)(2,1)} %u_in.1), custom_call_target="tpu_custom_call" | custom-call | tf_op jit(solution)/shard_map/out_proj/pallas_call | solution.py:802

commit v4 on v3

--- a/solution.py
+++ b/solution.py
@@ -12,6 +12,7 @@
 BLK = 128
 TN = 512
 TC = 256
+Q = 4
 MESH = pl.DeviceIdType.MESH
 
 
@@ -89,10 +90,11 @@
     other = sp + 1 - 2 * c
     n_seq, n_pos, width = u_bf.shape
     half_w = width // 2
-    nt, n_tile = half_w // TN, half_w // TC
+    nt, n_tile, per = half_w // TN, half_w // TC, TN // TC
     n_own, hp = 2 * n_pos, n_pos // 2
     nbo = n_own // BLK
-    n_piece = 2 * n_seq
+    cuts = (0, n_pos // 2, 3 * n_pos // 4, n_pos)
+    n_cut = len(cuts) - 1
 
     def remote(src, dst, send, recv, peer):
         return pltpu.make_async_remote_copy(src, dst, send, recv, device_id=peer, device_id_type=MESH)
@@ -101,7 +103,7 @@
         return pl.ds(pl.multiple_of(start, size), size)
 
     def piece(ref, s, h):
-        return ref.at[s, h * hp:(h + 1) * hp]
+        return ref.at[s, cuts[h]:cuts[h + 1]]
 
     def tail_copy(k):
         return remote(u32.at[:, n_pos - 8:], tail, ts.at[k], tr.at[0], (dp, 2 + k))
@@ -118,14 +120,19 @@
     def swap_f(f):
         return remote((f1, f2)[f].at[:, at((1 - c) * half_w, half_w)], pf.at[f], fs.at[f], fr.at[f], (dp, other))
 
-    def filt(src, u, k):
-        return remote(src.at[:, at(k * half_w + u * TC, TC)], land.at[dp, u, c], x_send.at[u, k], x_recv.at[u, c], (dp, 2 + k))
-
-    def landed(u, side):
-        return remote(land.at[dp, u, side], land.at[dp, u, side], x_send.at[u, side], x_recv.at[u, side], (dp, sp))
-
-    def across(u, side, f):
-        return remote(land.at[f, u, side], land.at[f, u, side], y_send.at[u, side], y_recv.at[u, side], (1 - dp, sp))
+    qr = n_pos // Q
+
+    def filt(src, u, k, q):
+        return remote(src.at[q * qr:(q + 1) * qr, at(k * half_w + u * TC, TC)], land.at[dp, u, c, q * qr:(q + 1) * qr],
+                      x_send.at[u, q, k], x_recv.at[u, q, c], (dp, 2 + k))
+
+    def landed(u, side, q):
+        ref = land.at[dp, u, side, q * qr:(q + 1) * qr]
+        return remote(ref, ref, x_send.at[u, q, side], x_recv.at[u, q, side], (dp, sp))
+
+    def across(u, side, f, q):
+        ref = land.at[f, u, side, q * qr:(q + 1) * qr]
+        return remote(ref, ref, y_send.at[u, q, side], y_recv.at[u, q, side], (1 - dp, sp))
 
     def fill(f, u, side, src, start):
         return pltpu.make_async_copy(src.at[:, at(start, TC)], land.at[f, u, side], l_sem.at[f, u, side])
@@ -133,17 +140,17 @@
     def column(g, j):
         return (g + j // nt) * width + c * half_w + lax.rem(j, nt) * TN
 
-    def load_rows(stage, st_sem, n, src, dst_row):
+    def load_rows(stage, st_sem, items):
         def copy(i):
-            return pltpu.make_async_copy(src(i), stage.at[i % 2], st_sem.at[i % 2])
+            src, rows, _, _ = items[i]
+            return pltpu.make_async_copy(src, stage.at[i % 2, :rows], st_sem.at[i % 2])
 
         copy(0).start()
-        for i in range(n):
-            if i + 1 < n:
+        for i, (_, rows, dst, row) in enumerate(items):
+            if i + 1 < len(items):
                 copy(i + 1).start()
             copy(i).wait()
-            ref, row = dst_row(i)
-            ref[pl.ds(pl.multiple_of(row, 16), hp), :] = stage[i % 2].astype(BF16)
+            dst[pl.ds(pl.multiple_of(row, 16), rows), :] = stage[i % 2, :rows].astype(BF16)
 
     barrier = pltpu.get_barrier_semaphore()
     for peer in ((dp, other), (dp, lax.rem(sp + 2, 4)), (dp, lax.rem(other + 2, 4)), (1 - dp, sp)):
@@ -157,26 +164,28 @@
 
     @pl.when(on_a)
     def _():
-        for i in range(n_piece):
-            over(*divmod(i, 2)).start()
+        for i in range(n_seq * n_cut):
+            over(*divmod(i, n_cut)).start()
         for which, src in ((0, f1), (1, f2)):
             @pl.when(dp == which)
             def _():
                 for u in range(n_tile):
-                    for k in range(2):
-                        filt(src, u, k).start()
+                    for q in range(Q):
+                        for k in range(2):
+                            filt(src, u, k, q).start()
 
     for i in range(n_seq):
         swap_u(i).start()
     for f in range(2):
         swap_f(f).start()
 
-    def forward(u):
+    def forward(u, quarters):
         @pl.when(on_b)
         def _():
-            for side in range(2):
-                landed(u, side).wait_recv()
-                across(u, side, dp).start()
+            for q in quarters:
+                for side in range(2):
+                    landed(u, side, q).wait_recv()
+                    across(u, side, dp, q).start()
 
     def front(wbuf, wsem, lhs, stage, st_sem, lhs_sem, tailbuf, q_st, q_sem, vh_st, vh_sem, pbuf):
         def weights(g, j, slot):
@@ -222,7 +231,8 @@
             copy.start()
         for s in range(n_seq):
             swap_u(s).wait_recv()
-        load_rows(stage, st_sem, n_piece, lambda i: piece(u_sw, *divmod(i, 2)), lambda i: (lhs, tail_rows + (i // 2) * n_own + (1 - c) * n_pos + (i % 2) * hp))
+        load_rows(stage, st_sem, [(u_sw.at[s, h * hp:(h + 1) * hp], hp, lhs, tail_rows + s * n_own + (1 - c) * n_pos + h * hp)
+                                  for s in range(n_seq) for h in range(2)])
         for copy in own_rows:
             copy.wait()
 
@@ -242,11 +252,13 @@
 
         def own_phase(g, n, dst, spectrum, following):
             def flush(j, slot):
-                cols = at(lax.rem(j, nt) * TN, TN)
                 blocks = pl.ds(nbo * (1 + j // nt), nbo)
-                copies = [pltpu.make_async_copy(q_st.at[slot], dst.at[:, blocks, :, cols], q_sem.at[slot])]
-                if spectrum:
-                    copies.append(pltpu.make_async_copy(vh_st.at[slot], vhat.at[:, nbo:, :, cols], vh_sem.at[slot]))
+                copies = []
+                for h in range(per):
+                    u = lax.rem(j, nt) * per + h
+                    copies.append(pltpu.make_async_copy(q_st.at[slot, h], dst.at[u, :, blocks], q_sem.at[slot, h]))
+                    if spectrum:
+                        copies.append(pltpu.make_async_copy(vh_st.at[slot, h], vhat.at[u, :, nbo:], vh_sem.at[slot, h]))
                 return copies
 
             def body(j, slot, bias, taps):
@@ -266,9 +278,12 @@
                     q = short_conv(pbuf.at[s], taps, r, chunk)
                     for b in range(chunk // BLK):
                         blk = q[b * BLK:(b + 1) * BLK]
-                        q_st[slot, s, r // BLK + b] = blk
+                        for h in range(per):
+                            q_st[slot, h, s, r // BLK + b] = blk[:, h * TC:(h + 1) * TC]
                         if spectrum:
-                            vh_st[slot, s, r // BLK + b] = block_values(fwd3_ref, blk)
+                            spec = block_values(fwd3_ref, blk)
+                            for h in range(per):
+                                vh_st[slot, h, s, r // BLK + b] = spec[:, h * TC:(h + 1) * TC]
                 for copy in flush(j, slot):
                     copy.start()
 
@@ -289,7 +304,7 @@
                 return [pltpu.make_async_copy(src, fin.at[slot, i], fin_sem.at[slot, i]) for i, src in enumerate(srcs)]
 
             def flush(j, slot):
-                return pltpu.make_async_copy(fout.at[slot], far.at[:, :, :, at(j * TC, TC)], fout_sem.at[slot])
+                return pltpu.make_async_copy(fout.at[slot], far.at[j], fout_sem.at[slot])
 
             for copy in fetch(0, 0):
                 copy.start()
@@ -338,57 +353,72 @@
         pltpu.VMEM((2, width, TN), BF16), pltpu.SemaphoreType.DMA((2, 4)),
         pltpu.VMEM((n_seq * n_own + 8 * n_seq, width), BF16),
         pltpu.VMEM((2, hp, width), F32), pltpu.SemaphoreType.DMA((2,)), pltpu.SemaphoreType.DMA((n_seq,)), pltpu.VMEM((n_seq, 8, width), F32),
-        pltpu.VMEM((2, n_seq, nbo, BLK, TN), BF16), pltpu.SemaphoreType.DMA((2,)),
-        pltpu.VMEM((2, n_seq, nbo, 2 * BLK, TN), F32), pltpu.SemaphoreType.DMA((2,)),
+        pltpu.VMEM((2, per, n_seq, nbo, BLK, TC), BF16), pltpu.SemaphoreType.DMA((2, per)),
+        pltpu.VMEM((2, per, n_seq, nbo, 2 * BLK, TC), F32), pltpu.SemaphoreType.DMA((2, per)),
         pltpu.VMEM((n_seq, n_own + 8, TN), F32))
 
     def prev(wres, w_sem, lhs_p, stage, st_sem, q_st, q_sem, vh_st, vh_sem, pbuf, pstash):
-        groups = ((0, 0, qx, False), (nt, 2, qv, True))
-
-        def weights(base, g, j):
+        def weights(j):
             rows = width // 4
-            return [pltpu.make_async_copy(w_in.at[i * rows:(i + 1) * rows, at(column(g, j), TN)],
-                                          wres.at[base + j, i * rows:(i + 1) * rows], w_sem.at[base + j, i]) for i in range(4)]
-
-        for base, g, _, _ in groups:
-            for j in range(nt):
-                for copy in weights(base, g, j):
-                    copy.start()
+            return [pltpu.make_async_copy(w_in.at[i * rows:(i + 1) * rows, at(which(j), TN)],
+                                          wres.at[j, i * rows:(i + 1) * rows], w_sem.at[j, i]) for i in range(4)]
+
+        def which(j):
+            return 2 * (j // nt) * width + c * half_w + lax.rem(j, nt) * TN
+
+        def begin(j, carry):
+            for copy in weights(j):
+                copy.start()
+            return carry
+
+        lax.fori_loop(0, 2 * nt, begin, 0)
 
         def rows(s, h):
+            n = cuts[h + 1] - cuts[h]
+
             @pl.when(on_b)
             def _():
                 over(s, h).wait_recv()
                 onward(s, h).start()
-                load_rows(stage, st_sem, 1, lambda _: piece(u_x, s, h), lambda _: (lhs_p, c * hp))
+                load_rows(stage, st_sem, [(piece(u_x, s, h), n, lhs_p, c * n)])
                 onward(s, h).wait_recv()
-                load_rows(stage, st_sem, 1, lambda _: piece(u_fw, s, h), lambda _: (lhs_p, (1 - c) * hp))
+                load_rows(stage, st_sem, [(piece(u_fw, s, h), n, lhs_p, (1 - c) * n)])
 
             @pl.when(on_a)
             def _():
                 lhs_p[...] = jnp.zeros_like(lhs_p)
 
-        def project(base, g, j):
-            return (dot(lhs_p[...], wres[base + j]) + bias_ref[:, at(column(g, j), TN)]).astype(BF16)
-
-        def first(s, base, g):
+        def project(h, j):
+            n = 2 * (cuts[h + 1] - cuts[h])
+            return (dot(lhs_p[:n, :], wres[j]) + bias_ref[:, at(which(j), TN)]).astype(BF16)
+
+        def first(s, h):
+            n = cuts[h + 1] - cuts[h]
+
             def body(j, carry):
-                @pl.when(s == 0)
-                def _():
-                    for copy in weights(base, g, j):
-                        copy.wait()
-
-                pstash[:, at((base + j) * TN, TN)] = project(base, g, j)
+                if h == 0:
+                    @pl.when(s == 0)
+                    def _():
+                        for copy in weights(j):
+                            copy.wait()
+
+                p = project(h, j)
+                for core in range(2):
+                    pstash[core, cuts[h]:cuts[h + 1], at(j * TN, TN)] = p[core * n:(core + 1) * n]
                 return carry
 
-            lax.fori_loop(0, nt, body, 0)
-
-        def second(s, base, g, dst, spectrum):
+            lax.fori_loop(0, 2 * nt, body, 0)
+
+        def last(s, base, dst, spectrum):
+            h = n_cut - 1
+            n = cuts[h + 1] - cuts[h]
+
             def flush(j):
-                slot, cols = lax.rem(j, 2), at(j * TN, TN)
-                copies = [pltpu.make_async_copy(q_st.at[slot], dst.at[s, :nbo, :, cols], q_sem.at[slot])]
-                if spectrum:
-                    copies.append(pltpu.make_async_copy(vh_st.at[slot], vhat.at[s, :nbo, :, cols], vh_sem.at[slot]))
+                slot, copies = lax.rem(j, 2), []
+                for half in range(per):
+                    copies.append(pltpu.make_async_copy(q_st.at[slot, half], dst.at[j * per + half, s, :nbo], q_sem.at[slot, half]))
+                    if spectrum:
+                        copies.append(pltpu.make_async_copy(vh_st.at[slot, half], vhat.at[j * per + half, s, :nbo], vh_sem.at[slot, half]))
                 return copies
 
             def body(j, carry):
@@ -399,19 +429,23 @@
                     for copy in flush(j - 2):
                         copy.wait()
 
-                taps = taps_ref[:, at(column(g, j), TN)]
-                old = pstash[:, at((base + j) * TN, TN)].astype(F32)
+                taps = taps_ref[:, at(which(base + j), TN)]
                 pbuf[0:8] = jnp.zeros((8, TN), F32)
-                p = project(base, g, j).astype(F32)
                 for core in range(2):
-                    for h, part_rows in enumerate((old, p)):
-                        start = 8 + (2 * core + h) * hp
-                        pbuf[start:start + hp] = jnp.where(on_b, part_rows[core * hp:(core + 1) * hp], 0.0)
+                    old = pstash[core, :cuts[h], at((base + j) * TN, TN)].astype(F32)
+                    pbuf[8 + core * n_pos:8 + core * n_pos + cuts[h]] = jnp.where(on_b, old, 0.0)
+                p = project(h, base + j).astype(F32)
+                for core in range(2):
+                    start = 8 + core * n_pos + cuts[h]
+                    pbuf[start:start + n] = jnp.where(on_b, p[core * n:(core + 1) * n], 0.0)
                 for b in range(nbo):
                     blk = short_conv(pbuf, taps, b * BLK, BLK)
-                    q_st[slot, b] = blk
+                    for half in range(per):
+                        q_st[slot, half, b] = blk[:, half * TC:(half + 1) * TC]
                     if spectrum:
-                        vh_st[slot, b] = block_values(fwd3_ref, blk)
+                        spec = block_values(fwd3_ref, blk)
+                        for half in range(per):
+                            vh_st[slot, half, b] = spec[:, half * TC:(half + 1) * TC]
                 for copy in flush(j):
                     copy.start()
                 return carry
@@ -422,17 +456,17 @@
                     copy.wait()
 
         def one_seq(s, carry):
-            rows(s, 0)
-            for base, g, _, _ in groups:
-                first(s, base, g)
-            rows(s, 1)
-            second(s, *groups[0])
+            for h in range(n_cut - 1):
+                rows(s, h)
+                first(s, h)
+            rows(s, n_cut - 1)
+            last(s, 0, qx, False)
 
             @pl.when(s + 1 == n_seq)
             def _():
-                forward(0)
-
-            second(s, *groups[1])
+                forward(0, range(Q))
+
+            last(s, nt, qv, True)
             return carry
 
         lax.fori_loop(0, n_seq, one_seq, 0)
@@ -441,9 +475,9 @@
         prev,
         pltpu.VMEM((2 * nt, width, TN), BF16), pltpu.SemaphoreType.DMA((2 * nt, 4)),
         pltpu.VMEM((2 * hp, width), BF16), pltpu.VMEM((2, hp, width), F32), pltpu.SemaphoreType.DMA((2,)),
-        pltpu.VMEM((2, nbo, BLK, TN), BF16), pltpu.SemaphoreType.DMA((2,)),
-        pltpu.VMEM((2, nbo, 2 * BLK, TN), F32), pltpu.SemaphoreType.DMA((2,)),
-        pltpu.VMEM((n_own + 8, TN), F32), pltpu.VMEM((2 * hp, 2 * half_w), BF16))
+        pltpu.VMEM((2, per, nbo, BLK, TC), BF16), pltpu.SemaphoreType.DMA((2, per)),
+        pltpu.VMEM((2, per, nbo, 2 * BLK, TC), F32), pltpu.SemaphoreType.DMA((2, per)),
+        pltpu.VMEM((n_own + 8, TN), F32), pltpu.VMEM((2, cuts[-2], 2 * half_w), BF16))
 
     @pl.when(on_a)
     def _():
@@ -454,19 +488,18 @@
 
     def conv(x1b, vb, x2b, vhb, farb, in_sem, vh_sem, kst, k_sem, sendbuf, *scratch):
         def fetch(t):
-            cols, slot = at(t * TC, TC), lax.rem(t, 3)
-            srcs = (qx.at[:, :2 * nbo], qv, qx.at[:, 2 * nbo:], far)
-            copies = [pltpu.make_async_copy(r.at[:, :, :, cols], b.at[slot], in_sem.at[slot, i])
+            slot, two = lax.rem(t, 3), lax.rem(t, 2)
+            srcs = (qx.at[t, :, :2 * nbo], qv.at[t], qx.at[t, :, 2 * nbo:], far.at[t])
+            copies = [pltpu.make_async_copy(r, b.at[slot], in_sem.at[slot, i])
                       for i, (r, b) in enumerate(zip(srcs, (x1b, vb, x2b, farb)))]
-            two = lax.rem(t, 2)
-            return copies + [pltpu.make_async_copy(vhat.at[s, :, :, cols], vhb.at[two, s], vh_sem.at[two, s]) for s in range(n_seq)]
+            return copies + [pltpu.make_async_copy(vhat.at[t, s], vhb.at[two, s], vh_sem.at[two, s]) for s in range(n_seq)]
 
         def flush(t):
             slot = lax.rem(t, 2)
-            return pltpu.make_async_copy(kst.at[slot], keep.at[:, :, at(t * TC, TC)], k_sem.at[slot])
+            return pltpu.make_async_copy(kst.at[slot], keep.at[t], k_sem.at[slot])
 
         def swap_y(u):
-            return remote(sendbuf.at[lax.rem(u, 2)], part.at[:, :, at(u * TC, TC)], p_send.at[u], p_recv.at[u], (dp, other))
+            return remote(sendbuf.at[lax.rem(u, 2)], part.at[u], p_send.at[u], p_recv.at[u], (dp, other))
 
         tile = ConvTile(fwd6_ref, inv6_ref, *scratch)
 
@@ -488,7 +521,7 @@
 
         for copy in fetch(0):
             copy.start()
-        forward(1)
+        forward(1, range(Q // 2))
 
         def step(t, carry):
             @pl.when(t + 1 < n_tile)
@@ -504,17 +537,21 @@
 
             @pl.when(on_b)
             def _():
-                for side in range(2):
-                    across(t, side, 1 - dp).wait_recv()
+                for q in range(Q):
+                    for side in range(2):
+                        across(t, side, 1 - dp, q).wait_recv()
 
             for copy in fetch(t):
                 copy.wait()
 
-            tile.step(land, t, vhb.at[lax.rem(t, 2)], inputs(t, 0), inputs(t, 1))
-
-            @pl.when(t + 2 < n_tile)
-            def _():
-                forward(t + 2)
+            def relay(phase):
+                ahead = 1 + 2 * phase // Q
+
+                @pl.when(t + ahead < n_tile)
+                def _():
+                    forward(t + ahead, ((phase + Q // 2) % Q,))
+
+            tile.step(land, t, vhb.at[lax.rem(t, 2)], inputs(t, 0), inputs(t, 1), relay)
 
             @pl.when(t >= 1)
             def _():
@@ -558,19 +595,21 @@
 
     @pl.when(on_a)
     def _():
-        for i in range(n_piece):
-            over(*divmod(i, 2)).wait_send()
+        for i in range(n_seq * n_cut):
+            over(*divmod(i, n_cut)).wait_send()
         for u in range(n_tile):
-            for k in range(2):
-                filt(f1, u, k).wait_send()
+            for q in range(Q):
+                for k in range(2):
+                    filt(f1, u, k, q).wait_send()
 
     @pl.when(on_b)
     def _():
-        for i in range(n_piece):
-            onward(*divmod(i, 2)).wait_send()
+        for i in range(n_seq * n_cut):
+            onward(*divmod(i, n_cut)).wait_send()
         for u in range(n_tile):
-            for side in range(2):
-                across(u, side, dp).wait_send()
+            for q in range(Q):
+                for side in range(2):
+                    across(u, side, dp, q).wait_send()
 
 
 def loop(trips):
@@ -644,7 +683,7 @@
                 else:
                     self.spectrum(4 * i + 2 * (q - 2) + k)
 
-    def step(self, land, t, vhat, data, old):
+    def step(self, land, t, vhat, data, old, relay):
         nb, nbo = self.nb, self.nbo
         far = data[3]
         self.near(land, t, 0)
@@ -656,6 +695,8 @@
         @loop(nb // 4)
         def _(i):
             self.middle(1, old, i, lambda r: self.pointwise(vhat.at[0], 0, far, self.first[0], r, 0))
+
+        relay(0)
 
         @loop(nbo // 2)
         def _(i):
@@ -667,11 +708,14 @@
                     j = 2 * i + q - 2
                     self.raw2[j] = block_spectrum(self.fwd6, self.hparts.at[1], j)
 
+        relay(1)
         self.window(1, self.raw2, far)
 
         @loop(nb // 4)
         def _(i):
             self.middle(0, data, i, lambda r: self.pointwise(vhat.at[1], 0, far, self.first[1], r, 0))
+
+        relay(2)
 
         @loop(nbo // 2)
         def _(i):
@@ -680,6 +724,8 @@
                 if q % 2 == 0:
                     self.gate_two(1, 2 * i + q // 2, old)
 
+        relay(3)
+
     def drain(self, data):
         nb, nbo = self.nb, self.nbo
 
@@ -707,7 +753,8 @@
 
 def out_body(keep, part, w_out, u_in, out, wbuf, w_sem, lhs, keep_v, stage, in_sem, u_v, o_st, o_sem):
     c = lax.rem(lax.axis_index("sp"), 2)
-    n_seq, n_pos, half_w = keep.shape
+    n_tile, n_seq, n_pos, _ = keep.shape
+    half_w = n_tile * TC
     width = 2 * half_w
     n_col, rows = width // TN, width // 4
 
@@ -719,21 +766,20 @@
         slot = lax.rem(j, 2)
         return pltpu.make_async_copy(o_st.at[slot], out.at[:, :, pl.ds(pl.multiple_of(j * TN, TN), TN)], o_sem.at[slot])
 
-    loads = [pltpu.make_async_copy(part.at[s], stage.at[s], in_sem.at[s]) for s in range(n_seq)]
-    loads += [pltpu.make_async_copy(keep.at[s], keep_v.at[s], in_sem.at[n_seq + s]) for s in range(n_seq)]
+    loads = [pltpu.make_async_copy(part.at[u], stage.at[u], in_sem.at[u]) for u in range(n_tile)]
+    loads += [pltpu.make_async_copy(keep.at[u], keep_v.at[u], in_sem.at[n_tile + u]) for u in range(n_tile)]
     for copy in loads:
         copy.start()
     for copy in weights(0, 0):
         copy.start()
-    resid = pltpu.make_async_copy(u_in, u_v, in_sem.at[2 * n_seq])
+    resid = pltpu.make_async_copy(u_in, u_v, in_sem.at[2 * n_tile])
     resid.start()
-    mine, theirs = (pl.ds(pl.multiple_of(k * half_w, half_w), half_w) for k in (c, 1 - c))
-    for s in range(n_seq):
-        loads[s].wait()
-        lhs[s, :, theirs] = stage[s].astype(BF16)
-    for s in range(n_seq):
-        loads[n_seq + s].wait()
-        lhs[s, :, mine] = keep_v[s]
+    for u in range(n_tile):
+        loads[u].wait()
+        loads[n_tile + u].wait()
+        for s in range(n_seq):
+            lhs[s, :, pl.ds(pl.multiple_of((1 - c) * half_w + u * TC, TC), TC)] = stage[u, s].astype(BF16)
+            lhs[s, :, pl.ds(pl.multiple_of(c * half_w + u * TC, TC), TC)] = keep_v[u, s]
     resid.wait()
 
     def step(j, carry):
@@ -783,16 +829,16 @@
             in_specs=[small] * 7 + [large] * 5,
             out_specs=[large] * 11,
             out_shape=[
-                shape((n_seq, n_pos, half_w), BF16), shape((n_seq, n_pos, half_w)),
-                shape((n_seq, nb + nbo, BLK, half_w), BF16), shape((n_seq, nb, BLK, half_w), BF16),
-                shape((n_seq, nb, 2 * BLK, half_w)), shape((2, nbo, 2 * BLK, half_w)),
+                shape((n_tile, n_seq, n_pos, TC), BF16), shape((n_tile, n_seq, n_pos, TC)),
+                shape((n_tile, n_seq, nb + nbo, BLK, TC), BF16), shape((n_tile, n_seq, nb, BLK, TC), BF16),
+                shape((n_tile, n_seq, nb, 2 * BLK, TC)), shape((n_tile, 2, nbo, 2 * BLK, TC)),
                 shape((n_seq, n_pos, width)), shape((n_seq, n_pos, width)), shape((n_seq, n_pos, width)),
                 shape((n_seq, 8, width)), shape((2, n_pos, half_w)),
             ],
             scratch_shapes=[
                 pltpu.VMEM((2, n_tile, 2, n_pos, TC), F32),
-                dma((2,)), dma((1,)), *[dma((n_seq, 2))] * 4, *[dma((n_seq,))] * 2, *[dma((2,))] * 2,
-                dma((2, n_tile, 2)), *[dma((n_tile, 2))] * 4, *[dma((n_tile,))] * 2,
+                dma((2,)), dma((1,)), *[dma((n_seq, 3))] * 4, *[dma((n_seq,))] * 2, *[dma((2,))] * 2,
+                dma((2, n_tile, 2)), *[dma((n_tile, Q, 2))] * 4, *[dma((n_tile,))] * 2,
             ],
             compiler_params=pltpu.CompilerParams(vmem_limit_bytes=62 << 20, collective_id=0, has_side_effects=True),
             name="hyena_main",
@@ -806,8 +852,8 @@
             out_shape=shape((n_seq, n_pos, width), BF16),
             scratch_shapes=[
                 pltpu.VMEM((2, width, TN), BF16), dma((2, 4)),
-                pltpu.VMEM((n_seq, n_pos, width), BF16), pltpu.VMEM((n_seq, n_pos, half_w), BF16), pltpu.VMEM((n_seq, n_pos, half_w), F32),
-                dma((2 * n_seq + 1,)), pltpu.VMEM((n_seq, n_pos, width), BF16), pltpu.VMEM((2, n_seq, n_pos, TN), BF16), dma((2,)),
+                pltpu.VMEM((n_seq, n_pos, width), BF16), pltpu.VMEM((n_tile, n_seq, n_pos, TC), BF16), pltpu.VMEM((n_tile, n_seq, n_pos, TC), F32),
+                dma((2 * n_tile + 1,)), pltpu.VMEM((n_seq, n_pos, width), BF16), pltpu.VMEM((2, n_seq, n_pos, TN), BF16), dma((2,)),
             ],
             compiler_params=pltpu.CompilerParams(vmem_limit_bytes=60 << 20),
             name="out_proj",

time: 347 us -> 347 us (level)
  no operation moved by 1% of the time
where the time goes in v4:
time: 347 us; the launch traced here: 345 us
  Pallas kernels  338 us (97%)
  other arithmetic  6.49 us (2%)
    pallas_call x1, Pallas kernels, local_step(): pl.pallas_call(main_body, in_specs=[small] * 7 + [large] * 5, out_specs=[...  313 us
    pallas_call x1, Pallas kernels, local_step(): pl.pallas_call(out_body, in_specs=[large] * 4, out_specs=large, out_shape...  25.2 us

profile of v4, /device:TPU:7, one launch (start us, length us, event | category | flops | bytes accessed | tf_op | source)
XLA Modules:
  0.0 344.9 jit_solution(15046187584681336732)
XLA Ops:
  0.0 6.5 %convert_element_type.3.u32 = f32[2,256,4096]{2,1,0:T(8,128)} convert(bf16[2,256,4096]{2,1,0:T(8,128)(2,1)} %u_in.1) | non-fusion elementwise | flops 2097152 | bytes 12582912 | tf_op jit(solution)/shard_map/convert_element_type | solution.py:846
  6.5 313.0 %hyena_main.1 = (bf16[8,2,256,256]{3,2,1,0:T(8,128)(2,1)}, f32[8,2,256,256]{3,2,1,0:T(8,128)}, bf16[8,2,12,128,256]{4,3,2,1,0:T(8,128)(2,1)}, bf16[8,2,8,128,256...) custom-call(bf16[256,384]{1,0:T(8,128)(2,1)} %constant.6.clone.fwd3_, ...), custom_call_target="tpu_custom_call" | custom-call | tf_op jit(solution)/shard_map/hyena_main/pallas_call | solution.py:827
  319.5 25.2 %out_proj.1 = bf16[2,256,4096]{2,1,0:T(8,128)(2,1)} custom-call(bf16[8,2,256,256]{3,2,1,0:T(8,128)(2,1)} %get-tuple-element.7.keep, f32[8,2,256,256]{3,2,1,0:T(8,128)} %get-tuple-element.8.part, bf16[4096,4096]{1,0:T(8,128)(2,1)} %w_out.1, bf16[2,256,4096]{2,1,0:T(8,128)(2,1)} %u_in.1), custom_call_target="tpu_custom_call" | custom-call | tf_op jit(solution)/shard_map/out_proj/pallas_call | solution.py:848

commit v5 on v4

--- a/solution.py
+++ b/solution.py
@@ -13,6 +13,7 @@
 TN = 512
 TC = 256
 Q = 4
+RC = 32
 MESH = pl.DeviceIdType.MESH
 
 
@@ -94,7 +95,7 @@
     n_own, hp = 2 * n_pos, n_pos // 2
     nbo = n_own // BLK
     cuts = (0, n_pos // 2, 3 * n_pos // 4, n_pos)
-    n_cut = len(cuts) - 1
+    n_cut, n_over = len(cuts) - 1, n_pos // RC
 
     def remote(src, dst, send, recv, peer):
         return pltpu.make_async_remote_copy(src, dst, send, recv, device_id=peer, device_id_type=MESH)
@@ -108,8 +109,9 @@
     def tail_copy(k):
         return remote(u32.at[:, n_pos - 8:], tail, ts.at[k], tr.at[0], (dp, 2 + k))
 
-    def over(s, h):
-        return remote(piece(u32, s, h), piece(u_x, s, h), os.at[s, h], orr.at[s, h], (dp, lax.rem(sp + 2, 4)))
+    def over(s, i):
+        rows = pl.ds(i * RC, RC)
+        return remote(u32.at[s, rows], u_x.at[s, rows], os.at[s, i], orr.at[s, i], (dp, lax.rem(sp + 2, 4)))
 
     def onward(s, h):
         return remote(piece(u_x, s, h), piece(u_fw, s, h), ws.at[s, h], wr.at[s, h], (dp, other))
@@ -164,8 +166,8 @@
 
     @pl.when(on_a)
     def _():
-        for i in range(n_seq * n_cut):
-            over(*divmod(i, n_cut)).start()
+        for i in range(n_seq * n_over):
+            over(*divmod(i, n_over)).start()
         for which, src in ((0, f1), (1, f2)):
             @pl.when(dp == which)
             def _():
@@ -378,7 +380,8 @@
 
             @pl.when(on_b)
             def _():
-                over(s, h).wait_recv()
+                for i in range(cuts[h] // RC, cuts[h + 1] // RC):
+                    over(s, i).wait_recv()
                 onward(s, h).start()
                 load_rows(stage, st_sem, [(piece(u_x, s, h), n, lhs_p, c * n)])
                 onward(s, h).wait_recv()
@@ -448,6 +451,11 @@
                             vh_st[slot, half, b] = spec[:, half * TC:(half + 1) * TC]
                 for copy in flush(j):
                     copy.start()
+
+                if spectrum:
+                    @pl.when(jnp.logical_and(s == n_seq - 1, j == 1))
+                    def _():
+                        forward(0, (Q - 1,))
                 return carry
 
             lax.fori_loop(0, nt, body, 0)
@@ -460,11 +468,16 @@
                 rows(s, h)
                 first(s, h)
             rows(s, n_cut - 1)
+
+            @pl.when(s + 1 == n_seq)
+            def _():
+                forward(0, (0,))
+
             last(s, 0, qx, False)
 
             @pl.when(s + 1 == n_seq)
             def _():
-                forward(0, range(Q))
+                forward(0, range(1, Q - 1))
 
             last(s, nt, qv, True)
             return carry
@@ -595,8 +608,8 @@
 
     @pl.when(on_a)
     def _():
-        for i in range(n_seq * n_cut):
-            over(*divmod(i, n_cut)).wait_send()
+        for i in range(n_seq * n_over):
+            over(*divmod(i, n_over)).wait_send()
         for u in range(n_tile):
             for q in range(Q):
                 for k in range(2):
@@ -837,7 +850,7 @@
             ],
             scratch_shapes=[
                 pltpu.VMEM((2, n_tile, 2, n_pos, TC), F32),
-                dma((2,)), dma((1,)), *[dma((n_seq, 3))] * 4, *[dma((n_seq,))] * 2, *[dma((2,))] * 2,
+                dma((2,)), dma((1,)), *[dma((n_seq, n_pos // RC))] * 2, *[dma((n_seq, 3))] * 2, *[dma((n_seq,))] * 2, *[dma((2,))] * 2,
                 dma((2, n_tile, 2)), *[dma((n_tile, Q, 2))] * 4, *[dma((n_tile,))] * 2,
             ],
             compiler_params=pltpu.CompilerParams(vmem_limit_bytes=62 << 20, collective_id=0, has_side_effects=True),

time: 347 us -> 344 us (level)
  no operation moved by 1% of the time
where the time goes in v5:
time: 344 us; the launch traced here: 343 us
  Pallas kernels  336 us (98%)
  other arithmetic  6.49 us (2%)
    pallas_call x1, Pallas kernels, local_step(): pl.pallas_call(main_body, in_specs=[small] * 7 + [large] * 5, out_specs=[...  311 us
    pallas_call x1, Pallas kernels, local_step(): pl.pallas_call(out_body, in_specs=[large] * 4, out_specs=large, out_shape...  25.2 us

profile of v5, /device:TPU:7, one launch (start us, length us, event | category | flops | bytes accessed | tf_op | source)
XLA Modules:
  0.0 342.8 jit_solution(11575732185211043178)
XLA Ops:
  0.0 6.5 %convert_element_type.3.u32 = f32[2,256,4096]{2,1,0:T(8,128)} convert(bf16[2,256,4096]{2,1,0:T(8,128)(2,1)} %u_in.1) | non-fusion elementwise | flops 2097152 | bytes 12582912 | tf_op jit(solution)/shard_map/convert_element_type | solution.py:859
  6.5 310.9 %hyena_main.1 = (bf16[8,2,256,256]{3,2,1,0:T(8,128)(2,1)}, f32[8,2,256,256]{3,2,1,0:T(8,128)}, bf16[8,2,12,128,256]{4,3,2,1,0:T(8,128)(2,1)}, bf16[8,2,8,128,256...) custom-call(bf16[256,384]{1,0:T(8,128)(2,1)} %constant.6.clone.fwd3_, ...), custom_call_target="tpu_custom_call" | custom-call | tf_op jit(solution)/shard_map/hyena_main/pallas_call | solution.py:840
  317.4 25.2 %out_proj.1 = bf16[2,256,4096]{2,1,0:T(8,128)(2,1)} custom-call(bf16[8,2,256,256]{3,2,1,0:T(8,128)(2,1)} %get-tuple-element.7.keep, f32[8,2,256,256]{3,2,1,0:T(8,128)} %get-tuple-element.8.part, bf16[4096,4096]{1,0:T(8,128)(2,1)} %w_out.1, bf16[2,256,4096]{2,1,0:T(8,128)(2,1)} %u_in.1), custom_call_target="tpu_custom_call" | custom-call | tf_op jit(solution)/shard_map/out_proj/pallas_call | solution.py:861

commit v6 on v4

--- a/solution.py
+++ b/solution.py
@@ -12,7 +12,8 @@
 BLK = 128
 TN = 512
 TC = 256
-Q = 4
+Q = 2
+PAIR = (0, 1)
 MESH = pl.DeviceIdType.MESH
 
 
@@ -80,8 +81,8 @@
     return dot(fwd3_ref[...], jnp.concatenate([blk, blk, blk], axis=0))
 
 
-def main_body(fwd3_ref, fwd6_ref, inv6_ref, bias_ref, taps_ref, sk1_ref, sk2_ref, u_bf, u32, w_in, f1, f2,
-              keep, part, qx, qv, vhat, far, u_sw, u_x, u_fw, tail, pf,
+def main_body(fwd3_ref, fwd6_ref, inv6_ref, bias_ref, taps_ref, sk1_ref, sk2_ref, u_bf, w_in, f1, f2,
+              keep, part, qx, qv, vhat, far, u32, tsrc, u_sw, u_x, u_fw, tail, pf,
               land, ts, tr, os, orr, ws, wr, ss, sr, fs, fr, l_sem, x_send, x_recv, y_send, y_recv, p_send, p_recv):
     sp, dp = lax.axis_index("sp"), lax.axis_index("dp")
     c = lax.rem(sp, 2)
@@ -93,7 +94,7 @@
     nt, n_tile, per = half_w // TN, half_w // TC, TN // TC
     n_own, hp = 2 * n_pos, n_pos // 2
     nbo = n_own // BLK
-    cuts = (0, n_pos // 2, 3 * n_pos // 4, n_pos)
+    cuts = (0, hp, hp + hp // 2, n_pos)
     n_cut = len(cuts) - 1
 
     def remote(src, dst, send, recv, peer):
@@ -106,7 +107,7 @@
         return ref.at[s, cuts[h]:cuts[h + 1]]
 
     def tail_copy(k):
-        return remote(u32.at[:, n_pos - 8:], tail, ts.at[k], tr.at[0], (dp, 2 + k))
+        return remote(tsrc, tail, ts.at[k], tr.at[0], (dp, 2 + k))
 
     def over(s, h):
         return remote(piece(u32, s, h), piece(u_x, s, h), os.at[s, h], orr.at[s, h], (dp, lax.rem(sp + 2, 4)))
@@ -127,11 +128,11 @@
                       x_send.at[u, q, k], x_recv.at[u, q, c], (dp, 2 + k))
 
     def landed(u, side, q):
-        ref = land.at[dp, u, side, q * qr:(q + 1) * qr]
+        ref = land.at[dp, u, side, at(q * qr, qr)]
         return remote(ref, ref, x_send.at[u, q, side], x_recv.at[u, q, side], (dp, sp))
 
     def across(u, side, f, q):
-        ref = land.at[f, u, side, q * qr:(q + 1) * qr]
+        ref = land.at[f, u, side, at(q * qr, qr)]
         return remote(ref, ref, y_send.at[u, q, side], y_recv.at[u, q, side], (1 - dp, sp))
 
     def fill(f, u, side, src, start):
@@ -157,35 +158,77 @@
         pl.semaphore_signal(barrier, inc=1, device_id=peer, device_id_type=MESH)
     pl.semaphore_wait(barrier, 4)
 
-    @pl.when(sp == 1)
-    def _():
-        for k in range(2):
-            tail_copy(k).start()
+    def widen(raw, wide, tail_raw, tail_wide, in_sem, out_sem):
+        def half(ref, s, h):
+            return ref.at[s, h * hp:h * hp + hp]
+
+        def load(s, h):
+            return pltpu.make_async_copy(half(u_bf, s, h), raw.at[h], in_sem.at[h])
+
+        last_rows = pltpu.make_async_copy(u_bf.at[:, n_pos - 8:], tail_raw, in_sem.at[2])
+        last_out = pltpu.make_async_copy(tail_wide, tsrc, out_sem.at[2])
+        order = [(s, h) for s in range(n_seq) for h in PAIR]
+        last_rows.start()
+        load(*order[0]).start()
+        last_rows.wait()
+        tail_wide[...] = tail_raw[...].astype(F32)
+        last_out.start()
+        pending = {}
+        for (s, h), following in zip(order, order[1:] + [None]):
+            if following:
+                load(*following).start()
+            load(s, h).wait()
+            if h in pending:
+                pending.pop(h).wait()
+            wide[h] = raw[h].astype(F32)
+            store = pltpu.make_async_copy(wide.at[h], half(u32, s, h), out_sem.at[h])
+            store.start()
+            if s + h:
+                pending[h] = store
+                continue
+            last_out.wait()
+
+            @pl.when(sp == 1)
+            def _():
+                for k in PAIR:
+                    tail_copy(k).start()
+
+            store.wait()
+
+            @pl.when(on_a)
+            def _():
+                over(s, h).start()
+
+        for store in pending.values():
+            store.wait()
+
+    pl.run_scoped(
+        widen, pltpu.VMEM((2, hp, width), BF16), pltpu.VMEM((2, hp, width), F32), pltpu.VMEM((n_seq, 8, width), BF16),
+        pltpu.VMEM((n_seq, 8, width), F32), pltpu.SemaphoreType.DMA((3,)), pltpu.SemaphoreType.DMA((3,)))
 
     @pl.when(on_a)
     def _():
-        for i in range(n_seq * n_cut):
+        for i in range(1, n_seq * n_cut):
             over(*divmod(i, n_cut)).start()
         for which, src in ((0, f1), (1, f2)):
             @pl.when(dp == which)
             def _():
                 for u in range(n_tile):
                     for q in range(Q):
-                        for k in range(2):
+                        for k in PAIR:
                             filt(src, u, k, q).start()
 
     for i in range(n_seq):
         swap_u(i).start()
-    for f in range(2):
+    for f in PAIR:
         swap_f(f).start()
 
-    def forward(u, quarters):
+    def forward(u, q):
         @pl.when(on_b)
         def _():
-            for q in quarters:
-                for side in range(2):
-                    landed(u, side, q).wait_recv()
-                    across(u, side, dp, q).start()
+            for side in PAIR:
+                landed(u, side, q).wait_recv()
+                across(u, side, dp, q).start()
 
     def front(wbuf, wsem, lhs, stage, st_sem, lhs_sem, tailbuf, q_st, q_sem, vh_st, vh_sem, pbuf):
         def weights(g, j, slot):
@@ -232,7 +275,7 @@
         for s in range(n_seq):
             swap_u(s).wait_recv()
         load_rows(stage, st_sem, [(u_sw.at[s, h * hp:(h + 1) * hp], hp, lhs, tail_rows + s * n_own + (1 - c) * n_pos + h * hp)
-                                  for s in range(n_seq) for h in range(2)])
+                                  for s in range(n_seq) for h in PAIR])
         for copy in own_rows:
             copy.wait()
 
@@ -324,11 +367,11 @@
                 def _():
                     flush(j - 2, slot).wait()
 
-                for f in range(2):
+                for f in PAIR:
                     split_blocks(fin.at[slot, f], parts.at[f], c * hk)
                     split_blocks(fin.at[slot, 2 + f], parts.at[f], (1 - c) * hk)
                 g_ref = fout.at[slot]
-                for f in range(2):
+                for f in PAIR:
                     for b in range(2 * hk):
                         g_ref[f, b] = block_spectrum(fwd6_ref, parts.at[f], b)
                     for b in range(2 * hk - 1, 0, -1):
@@ -342,7 +385,7 @@
             for j in (n_tile - 2, n_tile - 1):
                 flush(j, j % 2).wait()
 
-        for f in range(2):
+        for f in PAIR:
             swap_f(f).wait_recv()
         pl.run_scoped(
             far_phase, pltpu.VMEM((2, 4, n_pos, TC), F32), pltpu.SemaphoreType.DMA((2, 4)),
@@ -403,13 +446,14 @@
                             copy.wait()
 
                 p = project(h, j)
-                for core in range(2):
+                for core in PAIR:
                     pstash[core, cuts[h]:cuts[h + 1], at(j * TN, TN)] = p[core * n:(core + 1) * n]
                 return carry
 
             lax.fori_loop(0, 2 * nt, body, 0)
 
-        def last(s, base, dst, spectrum):
+        def last(s, u, dst):
+            base, spectrum = u * nt, u > 0
             h = n_cut - 1
             n = cuts[h + 1] - cuts[h]
 
@@ -431,11 +475,11 @@
 
                 taps = taps_ref[:, at(which(base + j), TN)]
                 pbuf[0:8] = jnp.zeros((8, TN), F32)
-                for core in range(2):
+                for core in PAIR:
                     old = pstash[core, :cuts[h], at((base + j) * TN, TN)].astype(F32)
                     pbuf[8 + core * n_pos:8 + core * n_pos + cuts[h]] = jnp.where(on_b, old, 0.0)
                 p = project(h, base + j).astype(F32)
-                for core in range(2):
+                for core in PAIR:
                     start = 8 + core * n_pos + cuts[h]
                     pbuf[start:start + n] = jnp.where(on_b, p[core * n:(core + 1) * n], 0.0)
                 for b in range(nbo):
@@ -448,6 +492,10 @@
                             vh_st[slot, half, b] = spec[:, half * TC:(half + 1) * TC]
                 for copy in flush(j):
                     copy.start()
+
+                @pl.when(jnp.logical_and(s == n_seq - 1, jnp.logical_and(lax.rem(j, Q) == 1, j < nt - Q * u)))
+                def _():
+                    forward(u, j // Q)
                 return carry
 
             lax.fori_loop(0, nt, body, 0)
@@ -460,13 +508,8 @@
                 rows(s, h)
                 first(s, h)
             rows(s, n_cut - 1)
-            last(s, 0, qx, False)
-
-            @pl.when(s + 1 == n_seq)
-            def _():
-                forward(0, range(Q))
-
-            last(s, nt, qv, True)
+            last(s, 0, qx)
+            last(s, 1, qv)
             return carry
 
         lax.fori_loop(0, n_seq, one_seq, 0)
@@ -521,7 +564,7 @@
 
         for copy in fetch(0):
             copy.start()
-        forward(1, range(Q // 2))
+        forward(1, Q - 1)
 
         def step(t, carry):
             @pl.when(t + 1 < n_tile)
@@ -531,25 +574,23 @@
 
             @pl.when(on_a)
             def _():
-                for f in range(2):
-                    for side in range(2):
+                for f in PAIR:
+                    for side in PAIR:
                         fill(f, t, side, f1, 0).wait()
 
             @pl.when(on_b)
             def _():
                 for q in range(Q):
-                    for side in range(2):
+                    for side in PAIR:
                         across(t, side, 1 - dp, q).wait_recv()
 
             for copy in fetch(t):
                 copy.wait()
 
-            def relay(phase):
-                ahead = 1 + 2 * phase // Q
-
-                @pl.when(t + ahead < n_tile)
+            def relay(q):
+                @pl.when(t + 2 < n_tile)
                 def _():
-                    forward(t + ahead, ((phase + Q // 2) % Q,))
+                    forward(t + 2, q)
 
             tile.step(land, t, vhb.at[lax.rem(t, 2)], inputs(t, 0), inputs(t, 1), relay)
 
@@ -585,12 +626,12 @@
 
     for s in range(n_seq):
         swap_u(s).wait_send()
-    for f in range(2):
+    for f in PAIR:
         swap_f(f).wait_send()
 
     @pl.when(sp == 1)
     def _():
-        for k in range(2):
+        for k in PAIR:
             tail_copy(k).wait_send()
 
     @pl.when(on_a)
@@ -599,7 +640,7 @@
             over(*divmod(i, n_cut)).wait_send()
         for u in range(n_tile):
             for q in range(Q):
-                for k in range(2):
+                for k in PAIR:
                     filt(f1, u, k, q).wait_send()
 
     @pl.when(on_b)
@@ -608,7 +649,7 @@
             onward(*divmod(i, n_cut)).wait_send()
         for u in range(n_tile):
             for q in range(Q):
-                for side in range(2):
+                for side in PAIR:
                     across(u, side, dp, q).wait_send()
 
 
@@ -628,7 +669,7 @@
         self.nb, self.nbo = sp0.shape[0], sq0.shape[0]
 
     def near(self, land, t, f):
-        for side in range(2):
+        for side in PAIR:
             split_blocks(land.at[f, t, side], self.hparts.at[f], side * self.nbo // 2)
 
     def window(self, f, raw, far):
@@ -677,7 +718,7 @@
         for q in range(4):
             if point is not None:
                 point(4 * i + q)
-            for k in range(2):
+            for k in PAIR:
                 if q < 2:
                     self.gate_one(s, 4 * i + 2 * q + k, data)
                 else:
@@ -696,7 +737,6 @@
         def _(i):
             self.middle(1, old, i, lambda r: self.pointwise(vhat.at[0], 0, far, self.first[0], r, 0))
 
-        relay(0)
 
         @loop(nbo // 2)
         def _(i):
@@ -708,14 +748,12 @@
                     j = 2 * i + q - 2
                     self.raw2[j] = block_spectrum(self.fwd6, self.hparts.at[1], j)
 
-        relay(1)
+        relay(0)
         self.window(1, self.raw2, far)
 
         @loop(nb // 4)
         def _(i):
             self.middle(0, data, i, lambda r: self.pointwise(vhat.at[1], 0, far, self.first[1], r, 0))
-
-        relay(2)
 
         @loop(nbo // 2)
         def _(i):
@@ -724,7 +762,7 @@
                 if q % 2 == 0:
                     self.gate_two(1, 2 * i + q // 2, old)
 
-        relay(3)
+        relay(1)
 
     def drain(self, data):
         nb, nbo = self.nb, self.nbo
@@ -759,8 +797,10 @@
     n_col, rows = width // TN, width // 4
 
     def weights(j, slot):
-        return [pltpu.make_async_copy(w_out.at[i * rows:(i + 1) * rows, pl.ds(pl.multiple_of(j * TN, TN), TN)],
-                                      wbuf.at[slot, i * rows:(i + 1) * rows], w_sem.at[slot, i]) for i in range(4)]
+        cols = pl.ds(pl.multiple_of(j * TN, TN), TN)
+        return [pltpu.make_async_copy(w_out.at[i * rows:(i + 1) * rows, cols],
+                                      wbuf.at[slot, i * rows:(i + 1) * rows], w_sem.at[slot, i]) for i in range(4)] + [
+                    pltpu.make_async_copy(u_in.at[:, :, cols], u_v.at[slot], w_sem.at[slot, 4])]
 
     def flush(j):
         slot = lax.rem(j, 2)
@@ -772,15 +812,12 @@
         copy.start()
     for copy in weights(0, 0):
         copy.start()
-    resid = pltpu.make_async_copy(u_in, u_v, in_sem.at[2 * n_tile])
-    resid.start()
     for u in range(n_tile):
         loads[u].wait()
         loads[n_tile + u].wait()
         for s in range(n_seq):
             lhs[s, :, pl.ds(pl.multiple_of((1 - c) * half_w + u * TC, TC), TC)] = stage[u, s].astype(BF16)
             lhs[s, :, pl.ds(pl.multiple_of(c * half_w + u * TC, TC), TC)] = keep_v[u, s]
-    resid.wait()
 
     def step(j, carry):
         slot = lax.rem(j, 2)
@@ -797,9 +834,8 @@
         def _():
             flush(j - 2).wait()
 
-        cols = pl.ds(pl.multiple_of(j * TN, TN), TN)
         for s in range(n_seq):
-            o_st[slot, s] = (u_v[s, :, cols].astype(F32) + dot(lhs[s], wbuf[slot])).astype(BF16)
+            o_st[slot, s] = (u_v[slot, s].astype(F32) + dot(lhs[s], wbuf[slot])).astype(BF16)
         flush(j).start()
         return carry
 
@@ -826,13 +862,13 @@
 
         keep, part, *_ = pl.pallas_call(
             main_body,
-            in_specs=[small] * 7 + [large] * 5,
-            out_specs=[large] * 11,
+            in_specs=[small] * 7 + [large] * 4,
+            out_specs=[large] * 13,
             out_shape=[
                 shape((n_tile, n_seq, n_pos, TC), BF16), shape((n_tile, n_seq, n_pos, TC)),
                 shape((n_tile, n_seq, nb + nbo, BLK, TC), BF16), shape((n_tile, n_seq, nb, BLK, TC), BF16),
                 shape((n_tile, n_seq, nb, 2 * BLK, TC)), shape((n_tile, 2, nbo, 2 * BLK, TC)),
-                shape((n_seq, n_pos, width)), shape((n_seq, n_pos, width)), shape((n_seq, n_pos, width)),
+                shape((n_seq, n_pos, width)), shape((n_seq, 8, width)), *[shape((n_seq, n_pos, width))] * 3,
                 shape((n_seq, 8, width)), shape((2, n_pos, half_w)),
             ],
             scratch_shapes=[
@@ -843,7 +879,7 @@
             compiler_params=pltpu.CompilerParams(vmem_limit_bytes=62 << 20, collective_id=0, has_side_effects=True),
             name="hyena_main",
         )(fwd3, fwd6, inv6, b_in.reshape(1, -1), conv_taps, skip_one.reshape(1, -1), skip_two.reshape(1, -1),
-          u_in, u_in.astype(F32), w_in, filt_one, filt_two)
+          u_in, w_in, filt_one, filt_two)
 
         return pl.pallas_call(
             out_body,
@@ -851,9 +887,9 @@
             out_specs=large,
             out_shape=shape((n_seq, n_pos, width), BF16),
             scratch_shapes=[
-                pltpu.VMEM((2, width, TN), BF16), dma((2, 4)),
+                pltpu.VMEM((2, width, TN), BF16), dma((2, 5)),
                 pltpu.VMEM((n_seq, n_pos, width), BF16), pltpu.VMEM((n_tile, n_seq, n_pos, TC), BF16), pltpu.VMEM((n_tile, n_seq, n_pos, TC), F32),
-                dma((2 * n_tile + 1,)), pltpu.VMEM((n_seq, n_pos, width), BF16), pltpu.VMEM((2, n_seq, n_pos, TN), BF16), dma((2,)),
+                dma((2 * n_tile,)), pltpu.VMEM((2, n_seq, n_pos, TN), BF16), pltpu.VMEM((2, n_seq, n_pos, TN), BF16), dma((2,)),
             ],
             compiler_params=pltpu.CompilerParams(vmem_limit_bytes=60 << 20),
             name="out_proj",

time: 347 us -> 335 us (0.965)
  other arithmetic: 6.49 us -> 0 us
  Pallas kernels: 338 us -> 334 us
    convert_element_type x1 -> x0, other arithmetic: 6.49 us -> none  [local_step(): u_in.astype(F32)]
where the time goes in v6:
time: 335 us; the launch traced here: 334 us
  Pallas kernels  334 us (100%)
    pallas_call x1, Pallas kernels, local_step(): pl.pallas_call(main_body, in_specs=[small] * 7 + [large] * 4, out_specs=[...  310 us
    pallas_call x1, Pallas kernels, local_step(): pl.pallas_call(out_body, in_specs=[large] * 4, out_specs=large, out_shape...  24.5 us

profile of v6, /device:TPU:7, one launch (start us, length us, event | category | flops | bytes accessed | tf_op | source)
XLA Modules:
  0.0 334.3 jit_solution(5156982268071783432)
XLA Ops:
  0.0 309.6 %hyena_main.1 = (bf16[8,2,256,256]{3,2,1,0:T(8,128)(2,1)}, f32[8,2,256,256]{3,2,1,0:T(8,128)}, bf16[8,2,12,128,256]{4,3,2,1,0:T(8,128)(2,1)}, bf16[8,2,8,128,256...) custom-call(bf16[256,384]{1,0:T(8,128)(2,1)} %constant.6.clone.fwd3_, ...), custom_call_target="tpu_custom_call" | custom-call | tf_op jit(solution)/shard_map/hyena_main/pallas_call | solution.py:863
  309.6 24.5 %out_proj.1 = bf16[2,256,4096]{2,1,0:T(8,128)(2,1)} custom-call(bf16[8,2,256,256]{3,2,1,0:T(8,128)(2,1)} %get-tuple-element.7.keep, f32[8,2,256,256]{3,2,1,0:T(8,128)} %get-tuple-element.8.part, bf16[4096,4096]{1,0:T(8,128)(2,1)} %w_out.1, bf16[2,256,4096]{2,1,0:T(8,128)(2,1)} %u_in.1), custom_call_target="tpu_custom_call" | custom-call | tf_op jit(solution)/shard_map/out_proj/pallas_call | solution.py:884

commit v7 on v6

--- a/solution.py
+++ b/solution.py
@@ -82,7 +82,7 @@
 
 
 def main_body(fwd3_ref, fwd6_ref, inv6_ref, bias_ref, taps_ref, sk1_ref, sk2_ref, u_bf, w_in, f1, f2,
-              keep, part, qx, qv, vhat, far, u32, tsrc, u_sw, u_x, u_fw, tail, pf,
+              keep, part, qx, qv, vhat, far, u32, tsrc, u_sw, u_x, tail, pf,
               land, ts, tr, os, orr, ws, wr, ss, sr, fs, fr, l_sem, x_send, x_recv, y_send, y_recv, p_send, p_recv):
     sp, dp = lax.axis_index("sp"), lax.axis_index("dp")
     c = lax.rem(sp, 2)
@@ -103,17 +103,29 @@
     def at(start, size):
         return pl.ds(pl.multiple_of(start, size), size)
 
-    def piece(ref, s, h):
-        return ref.at[s, cuts[h]:cuts[h + 1]]
-
-    def tail_copy(k):
-        return remote(tsrc, tail, ts.at[k], tr.at[0], (dp, 2 + k))
-
-    def over(s, h):
-        return remote(piece(u32, s, h), piece(u_x, s, h), os.at[s, h], orr.at[s, h], (dp, lax.rem(sp + 2, 4)))
-
-    def onward(s, h):
-        return remote(piece(u_x, s, h), piece(u_fw, s, h), ws.at[s, h], wr.at[s, h], (dp, other))
+    def share(s, h, k):
+        rows = (cuts[h + 1] - cuts[h]) // 2
+        return s, pl.ds(pl.multiple_of(cuts[h] + k * rows, rows), rows)
+
+    def tail_copy():
+        return remote(tsrc, tail, ts.at[0], tr.at[0], (dp, 3))
+
+    def tail_across():
+        return remote(tail, tail, ts.at[0], tr.at[0], (dp, other))
+
+    def over(s, h, k):
+        s, rows = share(s, h, k)
+        return remote(u32.at[s, rows], u_x.at[c, s, rows], os.at[s, h, k], orr.at[s, h, c], (dp, 2 + k))
+
+    def arrived(s, h, src):
+        at_s, rows = share(s, h, 0)
+        ref = u_x.at[src, at_s, rows]
+        return remote(ref, ref, os.at[s, h, src], orr.at[s, h, src], (dp, sp))
+
+    def onward(s, h, src):
+        at_s, rows = share(s, h, c)
+        ref = u_x.at[src, at_s, rows]
+        return remote(ref, ref, ws.at[s, h, src], wr.at[s, h, src], (dp, other))
 
     def swap_u(s):
         return remote(u32.at[s], u_sw.at[s], ss.at[s], sr.at[s], (dp, other))
@@ -190,14 +202,14 @@
 
             @pl.when(sp == 1)
             def _():
+                tail_copy().start()
+
+            store.wait()
+
+            @pl.when(on_a)
+            def _():
                 for k in PAIR:
-                    tail_copy(k).start()
-
-            store.wait()
-
-            @pl.when(on_a)
-            def _():
-                over(s, h).start()
+                    over(s, h, k).start()
 
         for store in pending.values():
             store.wait()
@@ -209,7 +221,8 @@
     @pl.when(on_a)
     def _():
         for i in range(1, n_seq * n_cut):
-            over(*divmod(i, n_cut)).start()
+            for k in PAIR:
+                over(*divmod(i, n_cut), k).start()
         for which, src in ((0, f1), (1, f2)):
             @pl.when(dp == which)
             def _():
@@ -281,7 +294,12 @@
 
         @pl.when(on_b)
         def _():
-            tail_copy(0).wait_recv()
+            tail_copy().wait_recv()
+
+            @pl.when(sp == 3)
+            def _():
+                tail_across().start()
+
             copy = pltpu.make_async_copy(tail, tailbuf, lhs_sem.at[0])
             copy.start()
             copy.wait()
@@ -421,11 +439,12 @@
 
             @pl.when(on_b)
             def _():
-                over(s, h).wait_recv()
-                onward(s, h).start()
-                load_rows(stage, st_sem, [(piece(u_x, s, h), n, lhs_p, c * n)])
-                onward(s, h).wait_recv()
-                load_rows(stage, st_sem, [(piece(u_fw, s, h), n, lhs_p, (1 - c) * n)])
+                for src in PAIR:
+                    arrived(s, h, src).wait_recv()
+                    onward(s, h, src).start()
+                for src in PAIR:
+                    onward(s, h, src).wait_recv()
+                load_rows(stage, st_sem, [(u_x.at[src, s, cuts[h]:cuts[h + 1]], n, lhs_p, src * n) for src in PAIR])
 
             @pl.when(on_a)
             def _():
@@ -631,13 +650,17 @@
 
     @pl.when(sp == 1)
     def _():
-        for k in PAIR:
-            tail_copy(k).wait_send()
+        tail_copy().wait_send()
+
+    @pl.when(sp == 3)
+    def _():
+        tail_across().wait_send()
 
     @pl.when(on_a)
     def _():
         for i in range(n_seq * n_cut):
-            over(*divmod(i, n_cut)).wait_send()
+            for k in PAIR:
+                over(*divmod(i, n_cut), k).wait_send()
         for u in range(n_tile):
             for q in range(Q):
                 for k in PAIR:
@@ -646,7 +669,8 @@
     @pl.when(on_b)
     def _():
         for i in range(n_seq * n_cut):
-            onward(*divmod(i, n_cut)).wait_send()
+            for src in PAIR:
+                onward(*divmod(i, n_cut), src).wait_send()
         for u in range(n_tile):
             for q in range(Q):
                 for side in PAIR:
@@ -863,17 +887,17 @@
         keep, part, *_ = pl.pallas_call(
             main_body,
             in_specs=[small] * 7 + [large] * 4,
-            out_specs=[large] * 13,
+            out_specs=[large] * 12,
             out_shape=[
                 shape((n_tile, n_seq, n_pos, TC), BF16), shape((n_tile, n_seq, n_pos, TC)),
                 shape((n_tile, n_seq, nb + nbo, BLK, TC), BF16), shape((n_tile, n_seq, nb, BLK, TC), BF16),
                 shape((n_tile, n_seq, nb, 2 * BLK, TC)), shape((n_tile, 2, nbo, 2 * BLK, TC)),
-                shape((n_seq, n_pos, width)), shape((n_seq, 8, width)), *[shape((n_seq, n_pos, width))] * 3,
+                shape((n_seq, n_pos, width)), shape((n_seq, 8, width)), shape((n_seq, n_pos, width)), shape((2, n_seq, n_pos, width)),
                 shape((n_seq, 8, width)), shape((2, n_pos, half_w)),
             ],
             scratch_shapes=[
                 pltpu.VMEM((2, n_tile, 2, n_pos, TC), F32),
-                dma((2,)), dma((1,)), *[dma((n_seq, 3))] * 4, *[dma((n_seq,))] * 2, *[dma((2,))] * 2,
+                dma((1,)), dma((1,)), *[dma((n_seq, 3, 2))] * 4, *[dma((n_seq,))] * 2, *[dma((2,))] * 2,
                 dma((2, n_tile, 2)), *[dma((n_tile, Q, 2))] * 4, *[dma((n_tile,))] * 2,
             ],
             compiler_params=pltpu.CompilerParams(vmem_limit_bytes=62 << 20, collective_id=0, has_side_effects=True),

time: 335 us -> 330 us (0.985)
  Pallas kernels: 334 us -> 330 us
    pallas_call x1, Pallas kernels: 310 us -> 305 us  [local_step(): pl.pallas_call(main_body, in_specs=[small] * 7 + [large] * 4, out_specs=[...]
where the time goes in v7:
time: 330 us
  Pallas kernels  330 us (100%)
    pallas_call x1, Pallas kernels, local_step(): pl.pallas_call(main_body, in_specs=[small] * 7 + [large] * 4, out_specs=[...  305 us
    pallas_call x1, Pallas kernels, local_step(): pl.pallas_call(out_body, in_specs=[large] * 4, out_specs=large, out_shape...  24.5 us

profile of v7, /device:TPU:7, one launch (start us, length us, event | category | flops | bytes accessed | tf_op | source)
XLA Modules:
  0.0 329.7 jit_solution(11764757944237660155)
XLA Ops:
  0.0 305.0 %hyena_main.1 = (bf16[8,2,256,256]{3,2,1,0:T(8,128)(2,1)}, f32[8,2,256,256]{3,2,1,0:T(8,128)}, bf16[8,2,12,128,256]{4,3,2,1,0:T(8,128)(2,1)}, bf16[8,2,8,128,256...) custom-call(bf16[256,384]{1,0:T(8,128)(2,1)} %constant.6.clone.fwd3_, ...), custom_call_target="tpu_custom_call" | custom-call | tf_op jit(solution)/shard_map/hyena_main/pallas_call | solution.py:887
  305.1 24.5 %out_proj.1 = bf16[2,256,4096]{2,1,0:T(8,128)(2,1)} custom-call(bf16[8,2,256,256]{3,2,1,0:T(8,128)(2,1)} %get-tuple-element.7.keep, f32[8,2,256,256]{3,2,1,0:T(8,128)} %get-tuple-element.8.part, bf16[4096,4096]{1,0:T(8,128)(2,1)} %w_out.1, bf16[2,256,4096]{2,1,0:T(8,128)(2,1)} %u_in.1), custom_call_target="tpu_custom_call" | custom-call | tf_op jit(solution)/shard_map/out_proj/pallas_call | solution.py:908

commit v8 on v7

--- a/solution.py
+++ b/solution.py
@@ -39,6 +39,10 @@
     return fwd3, fwd6, inv6
 
 
+def parity(x):
+    return lax.rem(x, 2)
+
+
 def dot(a, b):
     return jnp.dot(a, b, preferred_element_type=F32)
 
@@ -85,7 +89,7 @@
               keep, part, qx, qv, vhat, far, u32, tsrc, u_sw, u_x, tail, pf,
               land, ts, tr, os, orr, ws, wr, ss, sr, fs, fr, l_sem, x_send, x_recv, y_send, y_recv, p_send, p_recv):
     sp, dp = lax.axis_index("sp"), lax.axis_index("dp")
-    c = lax.rem(sp, 2)
+    c = parity(sp)
     on_b = sp >= 2
     on_a = jnp.logical_not(on_b)
     other = sp + 1 - 2 * c
@@ -171,15 +175,17 @@
     pl.semaphore_wait(barrier, 4)
 
     def widen(raw, wide, tail_raw, tail_wide, in_sem, out_sem):
-        def half(ref, s, h):
-            return ref.at[s, h * hp:h * hp + hp]
+        step = hp // 2
+
+        def part_of(ref, s, h):
+            return ref.at[s, h * step:h * step + step]
 
         def load(s, h):
-            return pltpu.make_async_copy(half(u_bf, s, h), raw.at[h], in_sem.at[h])
+            return pltpu.make_async_copy(part_of(u_bf, s, h), raw.at[h % 2], in_sem.at[h % 2])
 
         last_rows = pltpu.make_async_copy(u_bf.at[:, n_pos - 8:], tail_raw, in_sem.at[2])
         last_out = pltpu.make_async_copy(tail_wide, tsrc, out_sem.at[2])
-        order = [(s, h) for s in range(n_seq) for h in PAIR]
+        order = [(s, h) for s in range(n_seq) for h in range(n_pos // step)]
         last_rows.start()
         load(*order[0]).start()
         last_rows.wait()
@@ -190,13 +196,14 @@
             if following:
                 load(*following).start()
             load(s, h).wait()
-            if h in pending:
-                pending.pop(h).wait()
-            wide[h] = raw[h].astype(F32)
-            store = pltpu.make_async_copy(wide.at[h], half(u32, s, h), out_sem.at[h])
+            slot = h % 2
+            if slot in pending:
+                pending.pop(slot).wait()
+            wide[slot] = raw[slot].astype(F32)
+            store = pltpu.make_async_copy(wide.at[slot], part_of(u32, s, h), out_sem.at[slot])
             store.start()
             if s + h:
-                pending[h] = store
+                pending[slot] = store
                 continue
             last_out.wait()
 
@@ -208,21 +215,21 @@
 
             @pl.when(on_a)
             def _():
-                for k in PAIR:
-                    over(s, h, k).start()
+                over(s, h, 0).start()
 
         for store in pending.values():
             store.wait()
 
     pl.run_scoped(
-        widen, pltpu.VMEM((2, hp, width), BF16), pltpu.VMEM((2, hp, width), F32), pltpu.VMEM((n_seq, 8, width), BF16),
+        widen, pltpu.VMEM((2, hp // 2, width), BF16), pltpu.VMEM((2, hp // 2, width), F32), pltpu.VMEM((n_seq, 8, width), BF16),
         pltpu.VMEM((n_seq, 8, width), F32), pltpu.SemaphoreType.DMA((3,)), pltpu.SemaphoreType.DMA((3,)))
 
     @pl.when(on_a)
     def _():
-        for i in range(1, n_seq * n_cut):
+        for i in range(n_seq * n_cut):
             for k in PAIR:
-                over(*divmod(i, n_cut), k).start()
+                if i + k:
+                    over(*divmod(i, n_cut), k).start()
         for which, src in ((0, f1), (1, f2)):
             @pl.when(dp == which)
             def _():
@@ -251,7 +258,7 @@
 
         def stream(g, body, following, n=nt):
             def step(j, carry):
-                slot = lax.rem(j, 2)
+                slot = parity(j)
 
                 @pl.when(j + 1 < n)
                 def _():
@@ -371,7 +378,7 @@
                 copy.start()
 
             def step(j, carry):
-                slot = lax.rem(j, 2)
+                slot = parity(j)
 
                 @pl.when(j + 1 < n_tile)
                 def _():
@@ -432,7 +439,9 @@
                 copy.start()
             return carry
 
-        lax.fori_loop(0, 2 * nt, begin, 0)
+        @pl.when(on_b)
+        def _():
+            lax.fori_loop(0, 2 * nt, begin, 0)
 
         def rows(s, h):
             n = cuts[h + 1] - cuts[h]
@@ -459,7 +468,7 @@
 
             def body(j, carry):
                 if h == 0:
-                    @pl.when(s == 0)
+                    @pl.when(jnp.logical_and(on_b, s == 0))
                     def _():
                         for copy in weights(j):
                             copy.wait()
@@ -477,7 +486,7 @@
             n = cuts[h + 1] - cuts[h]
 
             def flush(j):
-                slot, copies = lax.rem(j, 2), []
+                slot, copies = parity(j), []
                 for half in range(per):
                     copies.append(pltpu.make_async_copy(q_st.at[slot, half], dst.at[j * per + half, s, :nbo], q_sem.at[slot, half]))
                     if spectrum:
@@ -485,7 +494,7 @@
                 return copies
 
             def body(j, carry):
-                slot = lax.rem(j, 2)
+                slot = parity(j)
 
                 @pl.when(j >= 2)
                 def _():
@@ -550,18 +559,18 @@
 
     def conv(x1b, vb, x2b, vhb, farb, in_sem, vh_sem, kst, k_sem, sendbuf, *scratch):
         def fetch(t):
-            slot, two = lax.rem(t, 3), lax.rem(t, 2)
+            slot, two = lax.rem(t, 3), parity(t)
             srcs = (qx.at[t, :, :2 * nbo], qv.at[t], qx.at[t, :, 2 * nbo:], far.at[t])
             copies = [pltpu.make_async_copy(r, b.at[slot], in_sem.at[slot, i])
                       for i, (r, b) in enumerate(zip(srcs, (x1b, vb, x2b, farb)))]
             return copies + [pltpu.make_async_copy(vhat.at[t, s], vhb.at[two, s], vh_sem.at[two, s]) for s in range(n_seq)]
 
         def flush(t):
-            slot = lax.rem(t, 2)
+            slot = parity(t)
             return pltpu.make_async_copy(kst.at[slot], keep.at[t], k_sem.at[slot])
 
         def swap_y(u):
-            return remote(sendbuf.at[lax.rem(u, 2)], part.at[u], p_send.at[u], p_recv.at[u], (dp, other))
+            return remote(sendbuf.at[parity(u)], part.at[u], p_send.at[u], p_recv.at[u], (dp, other))
 
         tile = ConvTile(fwd6_ref, inv6_ref, *scratch)
 
@@ -570,7 +579,7 @@
             return x1b.at[slot], vb.at[slot], x2b.at[slot], farb.at[slot], sk1_ref[:, cols], sk2_ref[:, cols]
 
         def emit(t):
-            slot = lax.rem(t, 2)
+            slot = parity(t)
 
             @pl.when(t >= 2)
             def _():
@@ -611,7 +620,7 @@
                 def _():
                     forward(t + 2, q)
 
-            tile.step(land, t, vhb.at[lax.rem(t, 2)], inputs(t, 0), inputs(t, 1), relay)
+            tile.step(land, t, vhb.at[parity(t)], inputs(t, 0), inputs(t, 1), relay)
 
             @pl.when(t >= 1)
             def _():
@@ -813,7 +822,7 @@
                 send[s, b * BLK:(b + 1) * BLK] = self.ybuf[s, (1 - c) * hk + b].astype(F32)
 
 
-def out_body(keep, part, w_out, u_in, out, wbuf, w_sem, lhs, keep_v, stage, in_sem, u_v, o_st, o_sem):
+def out_body(keep, part, w_out, u_in, out, wbuf, w_sem, lhs, keep_v, stage, in_sem, u_v, acc, o_st, o_sem):
     c = lax.rem(lax.axis_index("sp"), 2)
     n_tile, n_seq, n_pos, _ = keep.shape
     half_w = n_tile * TC
@@ -827,24 +836,39 @@
                     pltpu.make_async_copy(u_in.at[:, :, cols], u_v.at[slot], w_sem.at[slot, 4])]
 
     def flush(j):
-        slot = lax.rem(j, 2)
+        slot = parity(j)
         return pltpu.make_async_copy(o_st.at[slot], out.at[:, :, pl.ds(pl.multiple_of(j * TN, TN), TN)], o_sem.at[slot])
 
-    loads = [pltpu.make_async_copy(part.at[u], stage.at[u], in_sem.at[u]) for u in range(n_tile)]
-    loads += [pltpu.make_async_copy(keep.at[u], keep_v.at[u], in_sem.at[n_tile + u]) for u in range(n_tile)]
-    for copy in loads:
+    def channels(k, size):
+        return pl.ds(pl.multiple_of(k * size, size), size)
+
+    loads = [[pltpu.make_async_copy(ref.at[u], dst.at[u], in_sem.at[i, u]) for u in range(n_tile)]
+             for i, (ref, dst) in enumerate(((keep, keep_v), (part, stage)))]
+    for copy in loads[0]:
         copy.start()
     for copy in weights(0, 0):
         copy.start()
-    for u in range(n_tile):
-        loads[u].wait()
-        loads[n_tile + u].wait()
+    for copy in loads[1]:
+        copy.start()
+    for i, k in enumerate((c, 1 - c)):
+        for u, copy in enumerate(loads[i]):
+            copy.wait()
+            for s in range(n_seq):
+                lhs[s, :, channels(k * n_tile + u, TC)] = (keep_v, stage)[i][u, s].astype(BF16)
+        if i == 0:
+            for copy in weights(0, 0):
+                copy.wait()
+            for copy in weights(1, 1):
+                copy.start()
+            for s in range(n_seq):
+                acc[s] = u_v[0, s].astype(F32) + dot(lhs[s, :, channels(k, half_w)], wbuf[0, channels(k, half_w)])
+            continue
         for s in range(n_seq):
-            lhs[s, :, pl.ds(pl.multiple_of((1 - c) * half_w + u * TC, TC), TC)] = stage[u, s].astype(BF16)
-            lhs[s, :, pl.ds(pl.multiple_of(c * half_w + u * TC, TC), TC)] = keep_v[u, s]
+            o_st[0, s] = (acc[s] + dot(lhs[s, :, channels(k, half_w)], wbuf[0, channels(k, half_w)])).astype(BF16)
+    flush(0).start()
 
     def step(j, carry):
-        slot = lax.rem(j, 2)
+        slot = parity(j)
 
         @pl.when(j + 1 < n_col)
         def _():
@@ -863,7 +887,7 @@
         flush(j).start()
         return carry
 
-    lax.fori_loop(0, n_col, step, 0)
+    lax.fori_loop(1, n_col, step, 0)
     for j in (n_col - 2, n_col - 1):
         flush(j).wait()
 
@@ -913,7 +937,7 @@
             scratch_shapes=[
                 pltpu.VMEM((2, width, TN), BF16), dma((2, 5)),
                 pltpu.VMEM((n_seq, n_pos, width), BF16), pltpu.VMEM((n_tile, n_seq, n_pos, TC), BF16), pltpu.VMEM((n_tile, n_seq, n_pos, TC), F32),
-                dma((2 * n_tile,)), pltpu.VMEM((2, n_seq, n_pos, TN), BF16), pltpu.VMEM((2, n_seq, n_pos, TN), BF16), dma((2,)),
+                dma((2, n_tile)), pltpu.VMEM((2, n_seq, n_pos, TN), BF16), pltpu.VMEM((n_seq, n_pos, TN), F32), pltpu.VMEM((2, n_seq, n_pos, TN), BF16), dma((2,)),
             ],
             compiler_params=pltpu.CompilerParams(vmem_limit_bytes=60 << 20),
             name="out_proj",

time: 330 us -> 331 us (level)
  no operation moved by 1% of the time
where the time goes in v8:
time: 331 us; the launch traced here: 330 us
  Pallas kernels  330 us (100%)
    pallas_call x1, Pallas kernels, local_step(): pl.pallas_call(main_body, in_specs=[small] * 7 + [large] * 4, out_specs=[...  305 us
    pallas_call x1, Pallas kernels, local_step(): pl.pallas_call(out_body, in_specs=[large] * 4, out_specs=large, out_shape...  24.8 us

profile of v8, /device:TPU:7, one launch (start us, length us, event | category | flops | bytes accessed | tf_op | source)
XLA Modules:
  0.0 330.2 jit_solution(6245750551477325966)
XLA Ops:
  0.0 305.3 %hyena_main.1 = (bf16[8,2,256,256]{3,2,1,0:T(8,128)(2,1)}, f32[8,2,256,256]{3,2,1,0:T(8,128)}, bf16[8,2,12,128,256]{4,3,2,1,0:T(8,128)(2,1)}, bf16[8,2,8,128,256...) custom-call(bf16[256,384]{1,0:T(8,128)(2,1)} %constant.6.clone.fwd3_, ...), custom_call_target="tpu_custom_call" | custom-call | tf_op jit(solution)/shard_map/hyena_main/pallas_call | solution.py:911
  305.3 24.8 %out_proj.1 = bf16[2,256,4096]{2,1,0:T(8,128)(2,1)} custom-call(bf16[8,2,256,256]{3,2,1,0:T(8,128)(2,1)} %get-tuple-element.7.keep, f32[8,2,256,256]{3,2,1,0:T(8,128)} %get-tuple-element.8.part, bf16[4096,4096]{1,0:T(8,128)(2,1)} %w_out.1, bf16[2,256,4096]{2,1,0:T(8,128)(2,1)} %u_in.1), custom_call_target="tpu_custom_call" | custom-call | tf_op jit(solution)/shard_map/out_proj/pallas_call | solution.py:932

commit v9 on v7

--- a/solution.py
+++ b/solution.py
@@ -39,6 +39,10 @@
     return fwd3, fwd6, inv6
 
 
+def parity(x):
+    return lax.rem(x, 2)
+
+
 def dot(a, b):
     return jnp.dot(a, b, preferred_element_type=F32)
 
@@ -83,9 +87,9 @@
 
 def main_body(fwd3_ref, fwd6_ref, inv6_ref, bias_ref, taps_ref, sk1_ref, sk2_ref, u_bf, w_in, f1, f2,
               keep, part, qx, qv, vhat, far, u32, tsrc, u_sw, u_x, tail, pf,
-              land, ts, tr, os, orr, ws, wr, ss, sr, fs, fr, l_sem, x_send, x_recv, y_send, y_recv, p_send, p_recv):
+              land, held, h_sem, ts, tr, os, orr, ws, wr, ss, sr, fs, fr, l_sem, x_send, x_recv, y_send, y_recv, p_send, p_recv):
     sp, dp = lax.axis_index("sp"), lax.axis_index("dp")
-    c = lax.rem(sp, 2)
+    c = parity(sp)
     on_b = sp >= 2
     on_a = jnp.logical_not(on_b)
     other = sp + 1 - 2 * c
@@ -135,9 +139,12 @@
 
     qr = n_pos // Q
 
-    def filt(src, u, k, q):
-        return remote(src.at[q * qr:(q + 1) * qr, at(k * half_w + u * TC, TC)], land.at[dp, u, c, q * qr:(q + 1) * qr],
-                      x_send.at[u, q, k], x_recv.at[u, q, c], (dp, 2 + k))
+    def filt(u, k, q):
+        rows = pl.ds(q * qr, qr)
+        return remote(held.at[u, k, rows], land.at[dp, u, c, rows], x_send.at[u, q, k], x_recv.at[u, q, c], (dp, 2 + k))
+
+    def hold(src, u, k):
+        return pltpu.make_async_copy(src.at[:, at(k * half_w + u * TC, TC)], held.at[u, k], h_sem.at[u, k])
 
     def landed(u, side, q):
         ref = land.at[dp, u, side, at(q * qr, qr)]
@@ -154,16 +161,18 @@
         return (g + j // nt) * width + c * half_w + lax.rem(j, nt) * TN
 
     def load_rows(stage, st_sem, items):
+        size = stage.shape[1]
+        cut = [(src.at[pl.ds(i, size)], dst, row + i) for src, rows, dst, row in items for i in range(0, rows, size)]
+
         def copy(i):
-            src, rows, _, _ = items[i]
-            return pltpu.make_async_copy(src, stage.at[i % 2, :rows], st_sem.at[i % 2])
+            return pltpu.make_async_copy(cut[i][0], stage.at[i % 2], st_sem.at[i % 2])
 
         copy(0).start()
-        for i, (_, rows, dst, row) in enumerate(items):
-            if i + 1 < len(items):
+        for i, (_, dst, row) in enumerate(cut):
+            if i + 1 < len(cut):
                 copy(i + 1).start()
             copy(i).wait()
-            dst[pl.ds(pl.multiple_of(row, 16), rows), :] = stage[i % 2, :rows].astype(BF16)
+            dst[pl.ds(pl.multiple_of(row, 16), size), :] = stage[i % 2].astype(BF16)
 
     barrier = pltpu.get_barrier_semaphore()
     for peer in ((dp, other), (dp, lax.rem(sp + 2, 4)), (dp, lax.rem(other + 2, 4)), (1 - dp, sp)):
@@ -227,9 +236,16 @@
             @pl.when(dp == which)
             def _():
                 for u in range(n_tile):
-                    for q in range(Q):
-                        for k in PAIR:
-                            filt(src, u, k, q).start()
+                    for k in PAIR:
+                        hold(src, u, k).start()
+
+        for u in range(n_tile):
+            for k in PAIR:
+                hold(f1, u, k).wait()
+        for u in range(n_tile):
+            for q in range(Q):
+                for k in PAIR:
+                    filt(u, k, q).start()
 
     for i in range(n_seq):
         swap_u(i).start()
@@ -251,7 +267,7 @@
 
         def stream(g, body, following, n=nt):
             def step(j, carry):
-                slot = lax.rem(j, 2)
+                slot = parity(j)
 
                 @pl.when(j + 1 < n)
                 def _():
@@ -371,7 +387,7 @@
                 copy.start()
 
             def step(j, carry):
-                slot = lax.rem(j, 2)
+                slot = parity(j)
 
                 @pl.when(j + 1 < n_tile)
                 def _():
@@ -413,7 +429,7 @@
         front,
         pltpu.VMEM((2, width, TN), BF16), pltpu.SemaphoreType.DMA((2, 4)),
         pltpu.VMEM((n_seq * n_own + 8 * n_seq, width), BF16),
-        pltpu.VMEM((2, hp, width), F32), pltpu.SemaphoreType.DMA((2,)), pltpu.SemaphoreType.DMA((n_seq,)), pltpu.VMEM((n_seq, 8, width), F32),
+        pltpu.VMEM((2, hp // 2, width), F32), pltpu.SemaphoreType.DMA((2,)), pltpu.SemaphoreType.DMA((n_seq,)), pltpu.VMEM((n_seq, 8, width), F32),
         pltpu.VMEM((2, per, n_seq, nbo, BLK, TC), BF16), pltpu.SemaphoreType.DMA((2, per)),
         pltpu.VMEM((2, per, n_seq, nbo, 2 * BLK, TC), F32), pltpu.SemaphoreType.DMA((2, per)),
         pltpu.VMEM((n_seq, n_own + 8, TN), F32))
@@ -477,21 +493,14 @@
             n = cuts[h + 1] - cuts[h]
 
             def flush(j):
-                slot, copies = lax.rem(j, 2), []
+                copies = []
                 for half in range(per):
-                    copies.append(pltpu.make_async_copy(q_st.at[slot, half], dst.at[j * per + half, s, :nbo], q_sem.at[slot, half]))
+                    copies.append(pltpu.make_async_copy(q_st.at[half], dst.at[j * per + half, s, :nbo], q_sem.at[half]))
                     if spectrum:
-                        copies.append(pltpu.make_async_copy(vh_st.at[slot, half], vhat.at[j * per + half, s, :nbo], vh_sem.at[slot, half]))
+                        copies.append(pltpu.make_async_copy(vh_st.at[half], vhat.at[j * per + half, s, :nbo], vh_sem.at[half]))
                 return copies
 
             def body(j, carry):
-                slot = lax.rem(j, 2)
-
-                @pl.when(j >= 2)
-                def _():
-                    for copy in flush(j - 2):
-                        copy.wait()
-
                 taps = taps_ref[:, at(which(base + j), TN)]
                 pbuf[0:8] = jnp.zeros((8, TN), F32)
                 for core in PAIR:
@@ -501,14 +510,20 @@
                 for core in PAIR:
                     start = 8 + core * n_pos + cuts[h]
                     pbuf[start:start + n] = jnp.where(on_b, p[core * n:(core + 1) * n], 0.0)
+
+                @pl.when(j > 0)
+                def _():
+                    for copy in flush(j - 1):
+                        copy.wait()
+
                 for b in range(nbo):
                     blk = short_conv(pbuf, taps, b * BLK, BLK)
                     for half in range(per):
-                        q_st[slot, half, b] = blk[:, half * TC:(half + 1) * TC]
+                        q_st[half, b] = blk[:, half * TC:(half + 1) * TC]
                     if spectrum:
                         spec = block_values(fwd3_ref, blk)
                         for half in range(per):
-                            vh_st[slot, half, b] = spec[:, half * TC:(half + 1) * TC]
+                            vh_st[half, b] = spec[:, half * TC:(half + 1) * TC]
                 for copy in flush(j):
                     copy.start()
 
@@ -518,9 +533,8 @@
                 return carry
 
             lax.fori_loop(0, nt, body, 0)
-            for j in (nt - 2, nt - 1):
-                for copy in flush(j):
-                    copy.wait()
+            for copy in flush(nt - 1):
+                copy.wait()
 
         def one_seq(s, carry):
             for h in range(n_cut - 1):
@@ -536,9 +550,9 @@
     pl.run_scoped(
         prev,
         pltpu.VMEM((2 * nt, width, TN), BF16), pltpu.SemaphoreType.DMA((2 * nt, 4)),
-        pltpu.VMEM((2 * hp, width), BF16), pltpu.VMEM((2, hp, width), F32), pltpu.SemaphoreType.DMA((2,)),
-        pltpu.VMEM((2, per, nbo, BLK, TC), BF16), pltpu.SemaphoreType.DMA((2, per)),
-        pltpu.VMEM((2, per, nbo, 2 * BLK, TC), F32), pltpu.SemaphoreType.DMA((2, per)),
+        pltpu.VMEM((2 * hp, width), BF16), pltpu.VMEM((2, hp // 2, width), F32), pltpu.SemaphoreType.DMA((2,)),
+        pltpu.VMEM((per, nbo, BLK, TC), BF16), pltpu.SemaphoreType.DMA((per,)),
+        pltpu.VMEM((per, nbo, 2 * BLK, TC), F32), pltpu.SemaphoreType.DMA((per,)),
         pltpu.VMEM((n_own + 8, TN), F32), pltpu.VMEM((2, cuts[-2], 2 * half_w), BF16))
 
     @pl.when(on_a)
@@ -550,27 +564,27 @@
 
     def conv(x1b, vb, x2b, vhb, farb, in_sem, vh_sem, kst, k_sem, sendbuf, *scratch):
         def fetch(t):
-            slot, two = lax.rem(t, 3), lax.rem(t, 2)
+            slot, two = lax.rem(t, 3), parity(t)
             srcs = (qx.at[t, :, :2 * nbo], qv.at[t], qx.at[t, :, 2 * nbo:], far.at[t])
             copies = [pltpu.make_async_copy(r, b.at[slot], in_sem.at[slot, i])
                       for i, (r, b) in enumerate(zip(srcs, (x1b, vb, x2b, farb)))]
             return copies + [pltpu.make_async_copy(vhat.at[t, s], vhb.at[two, s], vh_sem.at[two, s]) for s in range(n_seq)]
 
         def flush(t):
-            slot = lax.rem(t, 2)
+            slot = parity(t)
             return pltpu.make_async_copy(kst.at[slot], keep.at[t], k_sem.at[slot])
 
         def swap_y(u):
-            return remote(sendbuf.at[lax.rem(u, 2)], part.at[u], p_send.at[u], p_recv.at[u], (dp, other))
-
-        tile = ConvTile(fwd6_ref, inv6_ref, *scratch)
+            return remote(sendbuf.at[parity(u)], part.at[u], p_send.at[u], p_recv.at[u], (dp, other))
+
+        tile = ConvTile(n_tile, fwd6_ref, inv6_ref, *scratch)
 
         def inputs(t, back):
             slot, cols = lax.rem(t + 3 - back, 3), at(c * half_w + lax.rem(t + n_tile - back, n_tile) * TC, TC)
             return x1b.at[slot], vb.at[slot], x2b.at[slot], farb.at[slot], sk1_ref[:, cols], sk2_ref[:, cols]
 
         def emit(t):
-            slot = lax.rem(t, 2)
+            slot = parity(t)
 
             @pl.when(t >= 2)
             def _():
@@ -606,12 +620,12 @@
             for copy in fetch(t):
                 copy.wait()
 
-            def relay(q):
-                @pl.when(t + 2 < n_tile)
+            def relay(q, first, last):
+                @pl.when(jnp.logical_and(t >= first, t < last))
                 def _():
-                    forward(t + 2, q)
-
-            tile.step(land, t, vhb.at[lax.rem(t, 2)], inputs(t, 0), inputs(t, 1), relay)
+                    forward(t + 2 - first // (n_tile - 2), q)
+
+            tile.step(land, t, vhb.at[parity(t)], inputs(t, 0), inputs(t, 1), relay)
 
             @pl.when(t >= 1)
             def _():
@@ -664,7 +678,7 @@
         for u in range(n_tile):
             for q in range(Q):
                 for k in PAIR:
-                    filt(f1, u, k, q).wait_send()
+                    filt(u, k, q).wait_send()
 
     @pl.when(on_b)
     def _():
@@ -687,10 +701,11 @@
 
 
 class ConvTile:
-    def __init__(self, fwd6, inv6, hparts, g1, g2, raw2, sp0, sp1, zparts, zv0, zv1, zhat, sq0, sq1, ybuf):
+    def __init__(self, steps, fwd6, inv6, hparts, g1, g2, raw2, sp0, sp1, zparts, zv0, zv1, zhat, sq0, sq1, ybuf):
         self.fwd6, self.inv6, self.hparts, self.g, self.raw2 = fwd6, inv6, hparts, (g1, g2), raw2
         self.first, self.second, self.zparts, self.zval, self.zhat, self.ybuf = (sp0, sp1), (sq0, sq1), zparts, (zv0, zv1), zhat, ybuf
         self.nb, self.nbo = sp0.shape[0], sq0.shape[0]
+        self.steps = steps
 
     def near(self, land, t, f):
         for side in PAIR:
@@ -761,6 +776,8 @@
         def _(i):
             self.middle(1, old, i, lambda r: self.pointwise(vhat.at[0], 0, far, self.first[0], r, 0))
 
+        relay(1, self.steps - 2, self.steps - 1)
+
 
         @loop(nbo // 2)
         def _(i):
@@ -772,7 +789,7 @@
                     j = 2 * i + q - 2
                     self.raw2[j] = block_spectrum(self.fwd6, self.hparts.at[1], j)
 
-        relay(0)
+        relay(0, 0, self.steps - 2)
         self.window(1, self.raw2, far)
 
         @loop(nb // 4)
@@ -786,7 +803,7 @@
                 if q % 2 == 0:
                     self.gate_two(1, 2 * i + q // 2, old)
 
-        relay(1)
+        relay(1, 0, self.steps - 3)
 
     def drain(self, data):
         nb, nbo = self.nb, self.nbo
@@ -827,7 +844,7 @@
                     pltpu.make_async_copy(u_in.at[:, :, cols], u_v.at[slot], w_sem.at[slot, 4])]
 
     def flush(j):
-        slot = lax.rem(j, 2)
+        slot = parity(j)
         return pltpu.make_async_copy(o_st.at[slot], out.at[:, :, pl.ds(pl.multiple_of(j * TN, TN), TN)], o_sem.at[slot])
 
     loads = [pltpu.make_async_copy(part.at[u], stage.at[u], in_sem.at[u]) for u in range(n_tile)]
@@ -844,7 +861,7 @@
             lhs[s, :, pl.ds(pl.multiple_of(c * half_w + u * TC, TC), TC)] = keep_v[u, s]
 
     def step(j, carry):
-        slot = lax.rem(j, 2)
+        slot = parity(j)
 
         @pl.when(j + 1 < n_col)
         def _():
@@ -896,11 +913,11 @@
                 shape((n_seq, 8, width)), shape((2, n_pos, half_w)),
             ],
             scratch_shapes=[
-                pltpu.VMEM((2, n_tile, 2, n_pos, TC), F32),
+                pltpu.VMEM((2, n_tile, 2, n_pos, TC), F32), pltpu.VMEM((n_tile, 2, n_pos, TC), F32), dma((n_tile, 2)),
                 dma((1,)), dma((1,)), *[dma((n_seq, 3, 2))] * 4, *[dma((n_seq,))] * 2, *[dma((2,))] * 2,
                 dma((2, n_tile, 2)), *[dma((n_tile, Q, 2))] * 4, *[dma((n_tile,))] * 2,
             ],
-            compiler_params=pltpu.CompilerParams(vmem_limit_bytes=62 << 20, collective_id=0, has_side_effects=True),
+            compiler_params=pltpu.CompilerParams(vmem_limit_bytes=67043328, collective_id=0, has_side_effects=True),
             name="hyena_main",
         )(fwd3, fwd6, inv6, b_in.reshape(1, -1), conv_taps, skip_one.reshape(1, -1), skip_two.reshape(1, -1),
           u_in, w_in, filt_one, filt_two)

time: 330 us -> 334 us (1.012)
  no operation moved by 1% of the time
where the time goes in v9:
time: 334 us; the launch traced here: 333 us
  Pallas kernels  333 us (100%)
    pallas_call x1, Pallas kernels, local_step(): pl.pallas_call(main_body, in_specs=[small] * 7 + [large] * 4, out_specs=[...  308 us
    pallas_call x1, Pallas kernels, local_step(): pl.pallas_call(out_body, in_specs=[large] * 4, out_specs=large, out_shape...  24.5 us

profile of v9, /device:TPU:7, one launch (start us, length us, event | category | flops | bytes accessed | tf_op | source)
XLA Modules:
  0.0 333.0 jit_solution(17340041095418155525)
XLA Ops:
  0.0 308.3 %hyena_main.1 = (bf16[8,2,256,256]{3,2,1,0:T(8,128)(2,1)}, f32[8,2,256,256]{3,2,1,0:T(8,128)}, bf16[8,2,12,128,256]{4,3,2,1,0:T(8,128)(2,1)}, bf16[8,2,8,128,256...) custom-call(bf16[256,384]{1,0:T(8,128)(2,1)} %constant.6.clone.fwd3_, ...), custom_call_target="tpu_custom_call" | custom-call | tf_op jit(solution)/shard_map/hyena_main/pallas_call | solution.py:904
  308.3 24.5 %out_proj.1 = bf16[2,256,4096]{2,1,0:T(8,128)(2,1)} custom-call(bf16[8,2,256,256]{3,2,1,0:T(8,128)(2,1)} %get-tuple-element.7.keep, f32[8,2,256,256]{3,2,1,0:T(8,128)} %get-tuple-element.8.part, bf16[4096,4096]{1,0:T(8,128)(2,1)} %w_out.1, bf16[2,256,4096]{2,1,0:T(8,128)(2,1)} %u_in.1), custom_call_target="tpu_custom_call" | custom-call | tf_op jit(solution)/shard_map/out_proj/pallas_call | solution.py:925

commit v10 on v7

--- a/solution.py
+++ b/solution.py
@@ -14,6 +14,7 @@
 TC = 256
 Q = 2
 PAIR = (0, 1)
+GR = 32
 MESH = pl.DeviceIdType.MESH
 
 
@@ -39,6 +40,10 @@
     return fwd3, fwd6, inv6
 
 
+def parity(x):
+    return lax.rem(x, 2)
+
+
 def dot(a, b):
     return jnp.dot(a, b, preferred_element_type=F32)
 
@@ -85,7 +90,7 @@
               keep, part, qx, qv, vhat, far, u32, tsrc, u_sw, u_x, tail, pf,
               land, ts, tr, os, orr, ws, wr, ss, sr, fs, fr, l_sem, x_send, x_recv, y_send, y_recv, p_send, p_recv):
     sp, dp = lax.axis_index("sp"), lax.axis_index("dp")
-    c = lax.rem(sp, 2)
+    c = parity(sp)
     on_b = sp >= 2
     on_a = jnp.logical_not(on_b)
     other = sp + 1 - 2 * c
@@ -105,7 +110,7 @@
 
     def share(s, h, k):
         rows = (cuts[h + 1] - cuts[h]) // 2
-        return s, pl.ds(pl.multiple_of(cuts[h] + k * rows, rows), rows)
+        return s, pl.ds((cuts[h] + k * rows) // GR, rows // GR)
 
     def tail_copy():
         return remote(tsrc, tail, ts.at[0], tr.at[0], (dp, 3))
@@ -156,14 +161,14 @@
     def load_rows(stage, st_sem, items):
         def copy(i):
             src, rows, _, _ = items[i]
-            return pltpu.make_async_copy(src, stage.at[i % 2, :rows], st_sem.at[i % 2])
+            return pltpu.make_async_copy(src, stage.at[i % 2, :rows // GR], st_sem.at[i % 2])
 
         copy(0).start()
         for i, (_, rows, dst, row) in enumerate(items):
             if i + 1 < len(items):
                 copy(i + 1).start()
             copy(i).wait()
-            dst[pl.ds(pl.multiple_of(row, 16), rows), :] = stage[i % 2, :rows].astype(BF16)
+            dst[pl.ds(pl.multiple_of(row, 16), rows), :] = stage[i % 2, :rows // GR].reshape(rows, width).astype(BF16)
 
     barrier = pltpu.get_barrier_semaphore()
     for peer in ((dp, other), (dp, lax.rem(sp + 2, 4)), (dp, lax.rem(other + 2, 4)), (1 - dp, sp)):
@@ -192,8 +197,8 @@
             load(s, h).wait()
             if h in pending:
                 pending.pop(h).wait()
-            wide[h] = raw[h].astype(F32)
-            store = pltpu.make_async_copy(wide.at[h], half(u32, s, h), out_sem.at[h])
+            wide[h] = raw[h].astype(F32).reshape(wide.shape[1:])
+            store = pltpu.make_async_copy(wide.at[h], u32.at[s, pl.ds(h * hp // GR, hp // GR)], out_sem.at[h])
             store.start()
             if s + h:
                 pending[h] = store
@@ -215,7 +220,7 @@
             store.wait()
 
     pl.run_scoped(
-        widen, pltpu.VMEM((2, hp, width), BF16), pltpu.VMEM((2, hp, width), F32), pltpu.VMEM((n_seq, 8, width), BF16),
+        widen, pltpu.VMEM((2, hp, width), BF16), pltpu.VMEM((2, hp // GR, GR, width), F32), pltpu.VMEM((n_seq, 8, width), BF16),
         pltpu.VMEM((n_seq, 8, width), F32), pltpu.SemaphoreType.DMA((3,)), pltpu.SemaphoreType.DMA((3,)))
 
     @pl.when(on_a)
@@ -251,7 +256,7 @@
 
         def stream(g, body, following, n=nt):
             def step(j, carry):
-                slot = lax.rem(j, 2)
+                slot = parity(j)
 
                 @pl.when(j + 1 < n)
                 def _():
@@ -287,7 +292,7 @@
             copy.start()
         for s in range(n_seq):
             swap_u(s).wait_recv()
-        load_rows(stage, st_sem, [(u_sw.at[s, h * hp:(h + 1) * hp], hp, lhs, tail_rows + s * n_own + (1 - c) * n_pos + h * hp)
+        load_rows(stage, st_sem, [(u_sw.at[s, pl.ds(h * hp // GR, hp // GR)], hp, lhs, tail_rows + s * n_own + (1 - c) * n_pos + h * hp)
                                   for s in range(n_seq) for h in PAIR])
         for copy in own_rows:
             copy.wait()
@@ -371,7 +376,7 @@
                 copy.start()
 
             def step(j, carry):
-                slot = lax.rem(j, 2)
+                slot = parity(j)
 
                 @pl.when(j + 1 < n_tile)
                 def _():
@@ -413,7 +418,7 @@
         front,
         pltpu.VMEM((2, width, TN), BF16), pltpu.SemaphoreType.DMA((2, 4)),
         pltpu.VMEM((n_seq * n_own + 8 * n_seq, width), BF16),
-        pltpu.VMEM((2, hp, width), F32), pltpu.SemaphoreType.DMA((2,)), pltpu.SemaphoreType.DMA((n_seq,)), pltpu.VMEM((n_seq, 8, width), F32),
+        pltpu.VMEM((2, hp // GR, GR, width), F32), pltpu.SemaphoreType.DMA((2,)), pltpu.SemaphoreType.DMA((n_seq,)), pltpu.VMEM((n_seq, 8, width), F32),
         pltpu.VMEM((2, per, n_seq, nbo, BLK, TC), BF16), pltpu.SemaphoreType.DMA((2, per)),
         pltpu.VMEM((2, per, n_seq, nbo, 2 * BLK, TC), F32), pltpu.SemaphoreType.DMA((2, per)),
         pltpu.VMEM((n_seq, n_own + 8, TN), F32))
@@ -444,7 +449,7 @@
                     onward(s, h, src).start()
                 for src in PAIR:
                     onward(s, h, src).wait_recv()
-                load_rows(stage, st_sem, [(u_x.at[src, s, cuts[h]:cuts[h + 1]], n, lhs_p, src * n) for src in PAIR])
+                load_rows(stage, st_sem, [(u_x.at[src, s, cuts[h] // GR:cuts[h + 1] // GR], n, lhs_p, src * n) for src in PAIR])
 
             @pl.when(on_a)
             def _():
@@ -477,7 +482,7 @@
             n = cuts[h + 1] - cuts[h]
 
             def flush(j):
-                slot, copies = lax.rem(j, 2), []
+                slot, copies = parity(j), []
                 for half in range(per):
                     copies.append(pltpu.make_async_copy(q_st.at[slot, half], dst.at[j * per + half, s, :nbo], q_sem.at[slot, half]))
                     if spectrum:
@@ -485,7 +490,7 @@
                 return copies
 
             def body(j, carry):
-                slot = lax.rem(j, 2)
+                slot = parity(j)
 
                 @pl.when(j >= 2)
                 def _():
@@ -536,7 +541,7 @@
     pl.run_scoped(
         prev,
         pltpu.VMEM((2 * nt, width, TN), BF16), pltpu.SemaphoreType.DMA((2 * nt, 4)),
-        pltpu.VMEM((2 * hp, width), BF16), pltpu.VMEM((2, hp, width), F32), pltpu.SemaphoreType.DMA((2,)),
+        pltpu.VMEM((2 * hp, width), BF16), pltpu.VMEM((2, hp // GR, GR, width), F32), pltpu.SemaphoreType.DMA((2,)),
         pltpu.VMEM((2, per, nbo, BLK, TC), BF16), pltpu.SemaphoreType.DMA((2, per)),
         pltpu.VMEM((2, per, nbo, 2 * BLK, TC), F32), pltpu.SemaphoreType.DMA((2, per)),
         pltpu.VMEM((n_own + 8, TN), F32), pltpu.VMEM((2, cuts[-2], 2 * half_w), BF16))
@@ -550,18 +555,18 @@
 
     def conv(x1b, vb, x2b, vhb, farb, in_sem, vh_sem, kst, k_sem, sendbuf, *scratch):
         def fetch(t):
-            slot, two = lax.rem(t, 3), lax.rem(t, 2)
+            slot, two = lax.rem(t, 3), parity(t)
             srcs = (qx.at[t, :, :2 * nbo], qv.at[t], qx.at[t, :, 2 * nbo:], far.at[t])
             copies = [pltpu.make_async_copy(r, b.at[slot], in_sem.at[slot, i])
                       for i, (r, b) in enumerate(zip(srcs, (x1b, vb, x2b, farb)))]
             return copies + [pltpu.make_async_copy(vhat.at[t, s], vhb.at[two, s], vh_sem.at[two, s]) for s in range(n_seq)]
 
         def flush(t):
-            slot = lax.rem(t, 2)
+            slot = parity(t)
             return pltpu.make_async_copy(kst.at[slot], keep.at[t], k_sem.at[slot])
 
         def swap_y(u):
-            return remote(sendbuf.at[lax.rem(u, 2)], part.at[u], p_send.at[u], p_recv.at[u], (dp, other))
+            return remote(sendbuf.at[parity(u)], part.at[u], p_send.at[u], p_recv.at[u], (dp, other))
 
         tile = ConvTile(fwd6_ref, inv6_ref, *scratch)
 
@@ -570,7 +575,7 @@
             return x1b.at[slot], vb.at[slot], x2b.at[slot], farb.at[slot], sk1_ref[:, cols], sk2_ref[:, cols]
 
         def emit(t):
-            slot = lax.rem(t, 2)
+            slot = parity(t)
 
             @pl.when(t >= 2)
             def _():
@@ -611,7 +616,7 @@
                 def _():
                     forward(t + 2, q)
 
-            tile.step(land, t, vhb.at[lax.rem(t, 2)], inputs(t, 0), inputs(t, 1), relay)
+            tile.step(land, t, vhb.at[parity(t)], inputs(t, 0), inputs(t, 1), relay)
 
             @pl.when(t >= 1)
             def _():
@@ -827,7 +832,7 @@
                     pltpu.make_async_copy(u_in.at[:, :, cols], u_v.at[slot], w_sem.at[slot, 4])]
 
     def flush(j):
-        slot = lax.rem(j, 2)
+        slot = parity(j)
         return pltpu.make_async_copy(o_st.at[slot], out.at[:, :, pl.ds(pl.multiple_of(j * TN, TN), TN)], o_sem.at[slot])
 
     loads = [pltpu.make_async_copy(part.at[u], stage.at[u], in_sem.at[u]) for u in range(n_tile)]
@@ -844,7 +849,7 @@
             lhs[s, :, pl.ds(pl.multiple_of(c * half_w + u * TC, TC), TC)] = keep_v[u, s]
 
     def step(j, carry):
-        slot = lax.rem(j, 2)
+        slot = parity(j)
 
         @pl.when(j + 1 < n_col)
         def _():
@@ -878,6 +883,7 @@
         nb = 2 * n_own // BLK
         nbo = nb // 2
         n_tile = half_w // TC
+        rows = n_pos // GR, GR, width
         small, large = pl.BlockSpec(memory_space=pltpu.VMEM), pl.BlockSpec(memory_space=pl.ANY)
         dma = pltpu.SemaphoreType.DMA
 
@@ -892,7 +898,7 @@
                 shape((n_tile, n_seq, n_pos, TC), BF16), shape((n_tile, n_seq, n_pos, TC)),
                 shape((n_tile, n_seq, nb + nbo, BLK, TC), BF16), shape((n_tile, n_seq, nb, BLK, TC), BF16),
                 shape((n_tile, n_seq, nb, 2 * BLK, TC)), shape((n_tile, 2, nbo, 2 * BLK, TC)),
-                shape((n_seq, n_pos, width)), shape((n_seq, 8, width)), shape((n_seq, n_pos, width)), shape((2, n_seq, n_pos, width)),
+                shape((n_seq, *rows)), shape((n_seq, 8, width)), shape((n_seq, *rows)), shape((2, n_seq, *rows)),
                 shape((n_seq, 8, width)), shape((2, n_pos, half_w)),
             ],
             scratch_shapes=[

time: 330 us -> 330 us (level)
  no operation moved by 1% of the time
where the time goes in v10:
time: 330 us
  Pallas kernels  330 us (100%)
    pallas_call x1, Pallas kernels, local_step(): pl.pallas_call(main_body, in_specs=[small] * 7 + [large] * 4, out_specs=[...  305 us
    pallas_call x1, Pallas kernels, local_step(): pl.pallas_call(out_body, in_specs=[large] * 4, out_specs=large, out_shape...  24.5 us

profile of v10, /device:TPU:7, one launch (start us, length us, event | category | flops | bytes accessed | tf_op | source)
XLA Modules:
  0.0 329.7 jit_solution(16094636599761710631)
XLA Ops:
  0.0 305.0 %hyena_main.1 = (bf16[8,2,256,256]{3,2,1,0:T(8,128)(2,1)}, f32[8,2,256,256]{3,2,1,0:T(8,128)}, bf16[8,2,12,128,256]{4,3,2,1,0:T(8,128)(2,1)}, bf16[8,2,8,128,256...) custom-call(bf16[256,384]{1,0:T(8,128)(2,1)} %constant.6.clone.fwd3_, ...), custom_call_target="tpu_custom_call" | custom-call | tf_op jit(solution)/shard_map/hyena_main/pallas_call | solution.py:893
  305.1 24.5 %out_proj.1 = bf16[2,256,4096]{2,1,0:T(8,128)(2,1)} custom-call(bf16[8,2,256,256]{3,2,1,0:T(8,128)(2,1)} %get-tuple-element.7.keep, f32[8,2,256,256]{3,2,1,0:T(8,128)} %get-tuple-element.8.part, bf16[4096,4096]{1,0:T(8,128)(2,1)} %w_out.1, bf16[2,256,4096]{2,1,0:T(8,128)(2,1)} %u_in.1), custom_call_target="tpu_custom_call" | custom-call | tf_op jit(solution)/shard_map/out_proj/pallas_call | solution.py:914

commit v11 on v10

--- a/solution.py
+++ b/solution.py
@@ -143,6 +143,11 @@
     def filt(src, u, k, q):
         return remote(src.at[q * qr:(q + 1) * qr, at(k * half_w + u * TC, TC)], land.at[dp, u, c, q * qr:(q + 1) * qr],
                       x_send.at[u, q, k], x_recv.at[u, q, c], (dp, 2 + k))
+
+    def direct(src, k):
+        u, q = n_tile - 1, Q - 1
+        return remote(src.at[q * qr:(q + 1) * qr, at(k * half_w + u * TC, TC)], land.at[1 - dp, u, c, q * qr:(q + 1) * qr],
+                      y_send.at[u, q, k], y_recv.at[u, q, c], (dp, 2 + k))
 
     def landed(u, side, q):
         ref = land.at[dp, u, side, at(q * qr, qr)]
@@ -228,13 +233,15 @@
         for i in range(1, n_seq * n_cut):
             for k in PAIR:
                 over(*divmod(i, n_cut), k).start()
-        for which, src in ((0, f1), (1, f2)):
+        for which, src, rest in ((0, f1, f2), (1, f2, f1)):
             @pl.when(dp == which)
             def _():
                 for u in range(n_tile):
                     for q in range(Q):
                         for k in PAIR:
                             filt(src, u, k, q).start()
+                for k in PAIR:
+                    direct(rest, k).start()
 
     for i in range(n_seq):
         swap_u(i).start()
@@ -608,11 +615,16 @@
                     for side in PAIR:
                         across(t, side, 1 - dp, q).wait_recv()
 
+            @pl.when(jnp.logical_and(on_b, t == n_tile - 1))
+            def _():
+                for side in PAIR:
+                    landed(t, side, Q - 1).wait_recv()
+
             for copy in fetch(t):
                 copy.wait()
 
             def relay(q):
-                @pl.when(t + 2 < n_tile)
+                @pl.when(t + 2 + q // (Q - 1) < n_tile)
                 def _():
                     forward(t + 2, q)
 
@@ -670,6 +682,8 @@
             for q in range(Q):
                 for k in PAIR:
                     filt(f1, u, k, q).wait_send()
+        for k in PAIR:
+            direct(f1, k).wait_send()
 
     @pl.when(on_b)
     def _():
@@ -677,7 +691,7 @@
             for src in PAIR:
                 onward(*divmod(i, n_cut), src).wait_send()
         for u in range(n_tile):
-            for q in range(Q):
+            for q in range(Q - u // (n_tile - 1)):
                 for side in PAIR:
                     across(u, side, dp, q).wait_send()
 

time: 330 us -> 330 us (level)
  no operation moved by 1% of the time
where the time goes in v11:
time: 330 us; the launch traced here: 329 us
  Pallas kernels  329 us (100%)
    pallas_call x1, Pallas kernels, local_step(): pl.pallas_call(main_body, in_specs=[small] * 7 + [large] * 4, out_specs=[...  305 us
    pallas_call x1, Pallas kernels, local_step(): pl.pallas_call(out_body, in_specs=[large] * 4, out_specs=large, out_shape...  24.5 us

profile of v11, /device:TPU:7, one launch (start us, length us, event | category | flops | bytes accessed | tf_op | source)
XLA Modules:
  0.0 329.3 jit_solution(10720148064558300020)
XLA Ops:
  0.0 304.7 %hyena_main.1 = (bf16[8,2,256,256]{3,2,1,0:T(8,128)(2,1)}, f32[8,2,256,256]{3,2,1,0:T(8,128)}, bf16[8,2,12,128,256]{4,3,2,1,0:T(8,128)(2,1)}, bf16[8,2,8,128,256...) custom-call(bf16[256,384]{1,0:T(8,128)(2,1)} %constant.6.clone.fwd3_, ...), custom_call_target="tpu_custom_call" | custom-call | tf_op jit(solution)/shard_map/hyena_main/pallas_call | solution.py:907
  304.7 24.5 %out_proj.1 = bf16[2,256,4096]{2,1,0:T(8,128)(2,1)} custom-call(bf16[8,2,256,256]{3,2,1,0:T(8,128)(2,1)} %get-tuple-element.7.keep, f32[8,2,256,256]{3,2,1,0:T(8,128)} %get-tuple-element.8.part, bf16[4096,4096]{1,0:T(8,128)(2,1)} %w_out.1, bf16[2,256,4096]{2,1,0:T(8,128)(2,1)} %u_in.1), custom_call_target="tpu_custom_call" | custom-call | tf_op jit(solution)/shard_map/out_proj/pallas_call | solution.py:928

commit v12 on v11

--- a/solution.py
+++ b/solution.py
@@ -624,9 +624,11 @@
                 copy.wait()
 
             def relay(q):
-                @pl.when(t + 2 + q // (Q - 1) < n_tile)
+                ahead = 2 - q
+
+                @pl.when(jnp.logical_and(t >= q, t + ahead + q < n_tile))
                 def _():
-                    forward(t + 2, q)
+                    forward(t + ahead, q)
 
             tile.step(land, t, vhb.at[parity(t)], inputs(t, 0), inputs(t, 1), relay)
 
@@ -775,6 +777,7 @@
             self.g[0][j] = block_spectrum(self.fwd6, self.hparts.at[0], j)
         self.near(land, t, 1)
         self.window(0, self.g[0], far)
+        relay(1)
 
         @loop(nb // 4)
         def _(i):
@@ -804,8 +807,6 @@
                 self.pointwise(self.zhat, 1, far, self.second[0], 4 * i + q, nbo)
                 if q % 2 == 0:
                     self.gate_two(1, 2 * i + q // 2, old)
-
-        relay(1)
 
     def drain(self, data):
         nb, nbo = self.nb, self.nbo

time: 330 us -> 330 us (level)
  no operation moved by 1% of the time
where the time goes in v12:
time: 330 us; the launch traced here: 329 us
  Pallas kernels  329 us (100%)
    pallas_call x1, Pallas kernels, local_step(): pl.pallas_call(main_body, in_specs=[small] * 7 + [large] * 4, out_specs=[...  305 us
    pallas_call x1, Pallas kernels, local_step(): pl.pallas_call(out_body, in_specs=[large] * 4, out_specs=large, out_shape...  24.5 us

profile of v12, /device:TPU:7, one launch (start us, length us, event | category | flops | bytes accessed | tf_op | source)
XLA Modules:
  0.0 329.3 jit_solution(11268071843120195781)
XLA Ops:
  0.0 304.6 %hyena_main.1 = (bf16[8,2,256,256]{3,2,1,0:T(8,128)(2,1)}, f32[8,2,256,256]{3,2,1,0:T(8,128)}, bf16[8,2,12,128,256]{4,3,2,1,0:T(8,128)(2,1)}, bf16[8,2,8,128,256...) custom-call(bf16[256,384]{1,0:T(8,128)(2,1)} %constant.6.clone.fwd3_, ...), custom_call_target="tpu_custom_call" | custom-call | tf_op jit(solution)/shard_map/hyena_main/pallas_call | solution.py:908
  304.7 24.5 %out_proj.1 = bf16[2,256,4096]{2,1,0:T(8,128)(2,1)} custom-call(bf16[8,2,256,256]{3,2,1,0:T(8,128)(2,1)} %get-tuple-element.7.keep, f32[8,2,256,256]{3,2,1,0:T(8,128)} %get-tuple-element.8.part, bf16[4096,4096]{1,0:T(8,128)(2,1)} %w_out.1, bf16[2,256,4096]{2,1,0:T(8,128)(2,1)} %u_in.1), custom_call_target="tpu_custom_call" | custom-call | tf_op jit(solution)/shard_map/out_proj/pallas_call | solution.py:929

commit v13 on v12

--- a/solution.py
+++ b/solution.py
@@ -854,8 +854,9 @@
     loads += [pltpu.make_async_copy(keep.at[u], keep_v.at[u], in_sem.at[n_tile + u]) for u in range(n_tile)]
     for copy in loads:
         copy.start()
-    for copy in weights(0, 0):
-        copy.start()
+    for j in PAIR:
+        for copy in weights(j, j):
+            copy.start()
     for u in range(n_tile):
         loads[u].wait()
         loads[n_tile + u].wait()
@@ -864,14 +865,14 @@
             lhs[s, :, pl.ds(pl.multiple_of(c * half_w + u * TC, TC), TC)] = keep_v[u, s]
 
     def step(j, carry):
-        slot = parity(j)
-
-        @pl.when(j + 1 < n_col)
+        slot, held = parity(j), lax.rem(j, 3)
+
+        @pl.when(j + 2 < n_col)
         def _():
-            for copy in weights(j + 1, 1 - slot):
+            for copy in weights(j + 2, lax.rem(j + 2, 3)):
                 copy.start()
 
-        for copy in weights(j, slot):
+        for copy in weights(j, held):
             copy.wait()
 
         @pl.when(j >= 2)
@@ -879,7 +880,7 @@
             flush(j - 2).wait()
 
         for s in range(n_seq):
-            o_st[slot, s] = (u_v[slot, s].astype(F32) + dot(lhs[s], wbuf[slot])).astype(BF16)
+            o_st[slot, s] = (u_v[held, s].astype(F32) + dot(lhs[s], wbuf[held])).astype(BF16)
         flush(j).start()
         return carry
 
@@ -932,9 +933,9 @@
             out_specs=large,
             out_shape=shape((n_seq, n_pos, width), BF16),
             scratch_shapes=[
-                pltpu.VMEM((2, width, TN), BF16), dma((2, 5)),
+                pltpu.VMEM((3, width, TN), BF16), dma((3, 5)),
                 pltpu.VMEM((n_seq, n_pos, width), BF16), pltpu.VMEM((n_tile, n_seq, n_pos, TC), BF16), pltpu.VMEM((n_tile, n_seq, n_pos, TC), F32),
-                dma((2 * n_tile,)), pltpu.VMEM((2, n_seq, n_pos, TN), BF16), pltpu.VMEM((2, n_seq, n_pos, TN), BF16), dma((2,)),
+                dma((2 * n_tile,)), pltpu.VMEM((3, n_seq, n_pos, TN), BF16), pltpu.VMEM((2, n_seq, n_pos, TN), BF16), dma((2,)),
             ],
             compiler_params=pltpu.CompilerParams(vmem_limit_bytes=60 << 20),
             name="out_proj",

time: 330 us -> 331 us (level)
  no operation moved by 1% of the time
where the time goes in v13:
time: 331 us; the launch traced here: 330 us
  Pallas kernels  330 us (100%)
    pallas_call x1, Pallas kernels, local_step(): pl.pallas_call(main_body, in_specs=[small] * 7 + [large] * 4, out_specs=[...  305 us
    pallas_call x1, Pallas kernels, local_step(): pl.pallas_call(out_body, in_specs=[large] * 4, out_specs=large, out_shape...  25.3 us

profile of v13, /device:TPU:7, one launch (start us, length us, event | category | flops | bytes accessed | tf_op | source)
XLA Modules:
  0.0 330.1 jit_solution(16593227016571732939)
XLA Ops:
  0.0 304.6 %hyena_main.1 = (bf16[8,2,256,256]{3,2,1,0:T(8,128)(2,1)}, f32[8,2,256,256]{3,2,1,0:T(8,128)}, bf16[8,2,12,128,256]{4,3,2,1,0:T(8,128)(2,1)}, bf16[8,2,8,128,256...) custom-call(bf16[256,384]{1,0:T(8,128)(2,1)} %constant.6.clone.fwd3_, ...), custom_call_target="tpu_custom_call" | custom-call | tf_op jit(solution)/shard_map/hyena_main/pallas_call | solution.py:909
  304.7 25.3 %out_proj.1 = bf16[2,256,4096]{2,1,0:T(8,128)(2,1)} custom-call(bf16[8,2,256,256]{3,2,1,0:T(8,128)(2,1)} %get-tuple-element.7.keep, f32[8,2,256,256]{3,2,1,0:T(8,128)} %get-tuple-element.8.part, bf16[4096,4096]{1,0:T(8,128)(2,1)} %w_out.1, bf16[2,256,4096]{2,1,0:T(8,128)(2,1)} %u_in.1), custom_call_target="tpu_custom_call" | custom-call | tf_op jit(solution)/shard_map/out_proj/pallas_call | solution.py:930

commit v14 on v12

--- a/solution.py
+++ b/solution.py
@@ -838,17 +838,17 @@
     n_tile, n_seq, n_pos, _ = keep.shape
     half_w = n_tile * TC
     width = 2 * half_w
-    n_col, rows = width // TN, width // 4
+    n_col, rows = width // TC, width // 4
 
     def weights(j, slot):
-        cols = pl.ds(pl.multiple_of(j * TN, TN), TN)
+        cols = pl.ds(pl.multiple_of(j * TC, TC), TC)
         return [pltpu.make_async_copy(w_out.at[i * rows:(i + 1) * rows, cols],
                                       wbuf.at[slot, i * rows:(i + 1) * rows], w_sem.at[slot, i]) for i in range(4)] + [
                     pltpu.make_async_copy(u_in.at[:, :, cols], u_v.at[slot], w_sem.at[slot, 4])]
 
     def flush(j):
         slot = parity(j)
-        return pltpu.make_async_copy(o_st.at[slot], out.at[:, :, pl.ds(pl.multiple_of(j * TN, TN), TN)], o_sem.at[slot])
+        return pltpu.make_async_copy(o_st.at[slot], out.at[:, :, pl.ds(pl.multiple_of(j * TC, TC), TC)], o_sem.at[slot])
 
     loads = [pltpu.make_async_copy(part.at[u], stage.at[u], in_sem.at[u]) for u in range(n_tile)]
     loads += [pltpu.make_async_copy(keep.at[u], keep_v.at[u], in_sem.at[n_tile + u]) for u in range(n_tile)]
@@ -932,9 +932,9 @@
             out_specs=large,
             out_shape=shape((n_seq, n_pos, width), BF16),
             scratch_shapes=[
-                pltpu.VMEM((2, width, TN), BF16), dma((2, 5)),
+                pltpu.VMEM((2, width, TC), BF16), dma((2, 5)),
                 pltpu.VMEM((n_seq, n_pos, width), BF16), pltpu.VMEM((n_tile, n_seq, n_pos, TC), BF16), pltpu.VMEM((n_tile, n_seq, n_pos, TC), F32),
-                dma((2 * n_tile,)), pltpu.VMEM((2, n_seq, n_pos, TN), BF16), pltpu.VMEM((2, n_seq, n_pos, TN), BF16), dma((2,)),
+                dma((2 * n_tile,)), pltpu.VMEM((2, n_seq, n_pos, TC), BF16), pltpu.VMEM((2, n_seq, n_pos, TC), BF16), dma((2,)),
             ],
             compiler_params=pltpu.CompilerParams(vmem_limit_bytes=60 << 20),
             name="out_proj",

time: 330 us -> 334 us (1.012)
  Pallas kernels: 329 us -> 333 us
    pallas_call x1, Pallas kernels: 24.5 us -> 28.4 us  [local_step(): pl.pallas_call(out_body, in_specs=[large] * 4, out_specs=large, out_shape...]
where the time goes in v14:
time: 334 us; the launch traced here: 333 us
  Pallas kernels  333 us (100%)
    pallas_call x1, Pallas kernels, local_step(): pl.pallas_call(main_body, in_specs=[small] * 7 + [large] * 4, out_specs=[...  305 us
    pallas_call x1, Pallas kernels, local_step(): pl.pallas_call(out_body, in_specs=[large] * 4, out_specs=large, out_shape...  28.4 us

profile of v14, /device:TPU:7, one launch (start us, length us, event | category | flops | bytes accessed | tf_op | source)
XLA Modules:
  0.0 333.2 jit_solution(3398444261181569243)
XLA Ops:
  0.0 304.6 %hyena_main.1 = (bf16[8,2,256,256]{3,2,1,0:T(8,128)(2,1)}, f32[8,2,256,256]{3,2,1,0:T(8,128)}, bf16[8,2,12,128,256]{4,3,2,1,0:T(8,128)(2,1)}, bf16[8,2,8,128,256...) custom-call(bf16[256,384]{1,0:T(8,128)(2,1)} %constant.6.clone.fwd3_, ...), custom_call_target="tpu_custom_call" | custom-call | tf_op jit(solution)/shard_map/hyena_main/pallas_call | solution.py:908
  304.7 28.4 %out_proj.1 = bf16[2,256,4096]{2,1,0:T(8,128)(2,1)} custom-call(bf16[8,2,256,256]{3,2,1,0:T(8,128)(2,1)} %get-tuple-element.7.keep, f32[8,2,256,256]{3,2,1,0:T(8,128)} %get-tuple-element.8.part, bf16[4096,4096]{1,0:T(8,128)(2,1)} %w_out.1, bf16[2,256,4096]{2,1,0:T(8,128)(2,1)} %u_in.1), custom_call_target="tpu_custom_call" | custom-call | tf_op jit(solution)/shard_map/out_proj/pallas_call | solution.py:929
